TPU v7x, 768 devices: a whole 4x8x12 slice. The times are simulated.
768 devices in a mesh: band: 192 (over y, z, core), ga: 4 (over x).
Axes of the slice: x: 4, y: 8, z: 12, core: 2. Of those that a mesh axis runs over, the one named last changes fastest.
Arguments:
- orbitals: bfloat16 [2, 192, 160, 128], P(None, 'band', 'ga'), may hold values from -8 to 8, as said below
- potential: float32 [480, 480], P('ga'), may hold values from -2 to 2
- slot_sticks: int32 [160], replicated, may hold values from -1 to 126, as said below
- stick_entries: int32 [160, 128], replicated, may hold values from -1 to 126, as said below
Outputs:
- applied_orbitals: bfloat16 [2, 192, 160, 128], P(None, 'band', 'ga')
- correlation: float32 [2, 192, 192], replicated
- reduced_hamiltonian: float32 [2, 192, 192], replicated
Inputs may be any that keep to these rules, and one draw needn't show every extreme that they name: `slot_sticks`: every gx with |gx| < 64 is held by exactly one slot; the other slots hold -1. Slots t with t // 40 = d are those of index d of ga; on some index of ga all 40 slots hold sticks. `stick_entries`: row t lists, in some order, gz + 63 for every gz with gx^2 + gz^2 < 64^2, gx being the stick of slot t, then -1 to the end of the row; rows of empty slots are all -1. `orbitals`: entries where stick_entries is -1 carry values that are not used.
All inputs are finite; a program needn't handle non-finite values.
Results may differ from a plain program's by a relative error of at most 0.001.
Values may be sent and summed in bfloat16 or wider, within the bound.
No kernel may reach another device: no remote copies, remote signals or barrier semaphores. Data moves between devices by JAX's collectives and lax.ppermute only.
A program may use at most 32 MiB of HBM per device.

v0:
```python
import jax
import jax.numpy as jnp
from jax import lax
from jax.sharding import Mesh
from jax.sharding import PartitionSpec as P

BAND = ("band_0", "band_1", "band_2")


TWO_PI = 6.283185307179586
HIGHEST_PRECISION = lax.Precision.HIGHEST


def joined_along(tiles, dim):
    tiles = jnp.moveaxis(tiles, 0, dim)
    shape = tiles.shape
    return tiles.reshape(*shape[:dim], shape[dim] * shape[dim + 1], *shape[dim + 2 :])


def sent_to_all(array, axis):
    copies = jnp.broadcast_to(array, (lax.axis_size(axis), *array.shape))
    return lax.all_to_all(copies, axis, split_axis=0, concat_axis=0, tiled=True)


def collect(array, axis, dim):
    return joined_along(sent_to_all(array, axis), dim)


def in_blocks(array, dim, length):
    before, after = (array.shape[:dim], array.shape[dim + 1 :])
    return jnp.moveaxis(array.reshape(*before, length, -1, *after), dim, 0)


def sum_at_owner(array, axis, dim):
    tiles = in_blocks(array, dim, lax.axis_size(axis))
    arrived = lax.all_to_all(tiles, axis, split_axis=0, concat_axis=0, tiled=True)
    return arrived.sum(axis=0)


def of_everyone(array, axis):
    return sent_to_all(array, axis).sum(axis=0)


def stacked_from(array, axes, turns):
    tiles = array
    for k in turns:
        tiles = lax.all_gather(tiles, axes[k])
    done = turns[::-1]
    back = [done.index(k) for k in range(len(axes))]
    tiles = tiles.transpose(*back, *range(len(axes), tiles.ndim))
    return tiles.reshape(-1, *array.shape)


def gather_axes(array, axes, turns, dim):
    return joined_along(stacked_from(array, axes, turns), dim)


def phases(frequency, position, points):
    winding = frequency[:, None] * position[None, :] % points
    angles = winding.astype(jnp.float32) * (TWO_PI / points)
    return (jnp.cos(angles), jnp.sin(angles))


def stick_phases(slot_sticks, radius, points):
    frequency = slot_sticks - radius + 1
    x_cos, x_sin = phases(frequency, jnp.arange(points, dtype=jnp.int32), points)
    filled = (slot_sticks >= 0).astype(jnp.float32)[:, None]
    return (x_cos * filled, x_sin * filled)


def selector_table(entry_lists):
    width = entry_lists.shape[1]
    return (entry_lists[:, :, None] == jnp.arange(width, dtype=jnp.int32)[None, None, :]).astype(
        jnp.bfloat16
    )


def spread_entries(coeffs, selector):
    return jnp.einsum("cbsk,skp->cbsp", coeffs, selector, preferred_element_type=jnp.float32)


def pick_entries(spectra, selector):
    return jnp.einsum(
        "cbsp,skp->cbsk", spectra, selector.astype(jnp.float32), precision=HIGHEST_PRECISION
    )


def z_forward(spread, z_cos, z_sin):
    real_part = jnp.einsum(
        "bsp,pz->bsz", spread[0], z_cos, precision=HIGHEST_PRECISION
    ) - jnp.einsum("bsp,pz->bsz", spread[1], z_sin, precision=HIGHEST_PRECISION)
    imag_part = jnp.einsum(
        "bsp,pz->bsz", spread[0], z_sin, precision=HIGHEST_PRECISION
    ) + jnp.einsum("bsp,pz->bsz", spread[1], z_cos, precision=HIGHEST_PRECISION)
    return jnp.stack([real_part, imag_part])


def plane_work(columns, x_cos, x_sin, potential):
    field_real = jnp.einsum(
        "bsz,sx->bzx", columns[0], x_cos, precision=HIGHEST_PRECISION
    ) - jnp.einsum("bsz,sx->bzx", columns[1], x_sin, precision=HIGHEST_PRECISION)
    field_imag = jnp.einsum(
        "bsz,sx->bzx", columns[0], x_sin, precision=HIGHEST_PRECISION
    ) + jnp.einsum("bsz,sx->bzx", columns[1], x_cos, precision=HIGHEST_PRECISION)
    prod_real = potential[None] * field_real
    prod_imag = potential[None] * field_imag
    back_real = jnp.einsum(
        "bzx,sx->bsz", prod_real, x_cos, precision=HIGHEST_PRECISION
    ) + jnp.einsum("bzx,sx->bsz", prod_imag, x_sin, precision=HIGHEST_PRECISION)
    back_imag = jnp.einsum(
        "bzx,sx->bsz", prod_imag, x_cos, precision=HIGHEST_PRECISION
    ) - jnp.einsum("bzx,sx->bsz", prod_real, x_sin, precision=HIGHEST_PRECISION)
    return jnp.stack([back_real, back_imag])


def z_backward(gathered, z_cos, z_sin, points):
    real_part = jnp.einsum(
        "bsz,pz->bsp", gathered[0], z_cos, precision=HIGHEST_PRECISION
    ) + jnp.einsum("bsz,pz->bsp", gathered[1], z_sin, precision=HIGHEST_PRECISION)
    imag_part = jnp.einsum(
        "bsz,pz->bsp", gathered[1], z_cos, precision=HIGHEST_PRECISION
    ) - jnp.einsum("bsz,pz->bsp", gathered[0], z_sin, precision=HIGHEST_PRECISION)
    return jnp.stack([real_part, imag_part]) / float(points * points)


def kinetic_factor(sticks, entry_lists, radius):
    gx_value = sticks - radius + 1
    gz_value = entry_lists - radius + 1
    return ((gx_value * gx_value)[:, None] + gz_value * gz_value).astype(jnp.float32) / float(
        radius * radius
    )


def cross_products(left, right, scale):
    dims = (((1,), (1,)), ((), ()))
    real_part = lax.dot_general(
        left[0], right[0], dims, preferred_element_type=jnp.float32
    ) + lax.dot_general(left[1], right[1], dims, preferred_element_type=jnp.float32)
    imag_part = lax.dot_general(
        left[0], right[1], dims, preferred_element_type=jnp.float32
    ) - lax.dot_general(left[1], right[0], dims, preferred_element_type=jnp.float32)
    return jnp.stack([real_part, imag_part]) * scale


def body(orbitals, potential, slot_sticks, stick_entries):
    points = potential.shape[1]
    plane_rows = potential.shape[0]
    width = stick_entries.shape[1]
    radius = width // 2
    band_count = orbitals.shape[1]
    slot_count = orbitals.shape[2]
    ga_index = lax.axis_index("ga")
    own_first = ga_index * slot_count
    own_lists = lax.dynamic_slice_in_dim(stick_entries, own_first, slot_count, 0)
    own_sticks = lax.dynamic_slice_in_dim(slot_sticks, own_first, slot_count, 0)
    present = own_lists >= 0
    own_selector = selector_table(own_lists)
    masked = jnp.where(present[None, None], orbitals, jnp.zeros_like(orbitals))
    frequency = jnp.arange(width, dtype=jnp.int32) - radius + 1
    local_z = ga_index * plane_rows + jnp.arange(plane_rows, dtype=jnp.int32)
    local_cos, local_sin = phases(frequency, local_z, points)
    x_cos, x_sin = stick_phases(slot_sticks, radius, points)
    columns = z_forward(
        spread_entries(collect(orbitals, "ga", 2), selector_table(stick_entries)),
        local_cos,
        local_sin,
    )
    gathered = plane_work(columns, x_cos, x_sin, potential)
    portion = gathered
    summed_slots = sum_at_owner(
        jnp.transpose(z_backward(portion, local_cos, local_sin, points), (2, 0, 1, 3)), "ga", 0
    )
    spectra = jnp.transpose(summed_slots, (1, 2, 0, 3))
    applied = pick_entries(spectra, own_selector)
    kinetic = kinetic_factor(own_sticks, own_lists, radius)
    applied_orbitals = jnp.where(
        present[None, None],
        kinetic[None, None] * orbitals.astype(jnp.float32) + applied,
        jnp.float32(0.0),
    ).astype(jnp.bfloat16)
    scale = 1.0 / (4.0 * radius * radius)
    flat_psi = masked.reshape(2, band_count, -1)
    flat_h = applied_orbitals.reshape(2, band_count, -1)
    portion = lax.all_gather(masked, BAND, axis=1, tiled=True)
    remote_psi = portion.reshape(2, portion.shape[1], -1)
    block = jnp.stack(
        [cross_products(remote_psi, flat_psi, scale), cross_products(remote_psi, flat_h, scale)]
    )
    summed = of_everyone(block, "ga")
    matrices = gather_axes(summed, BAND, (0, 1, 2), 3)
    return (applied_orbitals, matrices[0], matrices[1])


def solution(mesh):
    finer = Mesh(
        mesh.devices.reshape(8, 12, 2, mesh.shape["ga"]), ("band_0", "band_1", "band_2", "ga")
    )
    return jax.shard_map(
        body,
        mesh=finer,
        in_specs=(P(None, BAND, "ga", None), P("ga", None), P(), P()),
        out_specs=(P(None, BAND, "ga", None), P(), P()),
        check_vma=False,
    )
```

profile of v0, /device:TPU:1, one launch (start us, length us, event | category | flops | bytes accessed | tf_op | source)
XLA Modules:
  0.0 223.7 jit_solution(8836009558747451287)
XLA Ops:
  7.2 0.8 add_multiply_fusion
  8.0 0.8 convert_multiply_fusion
  8.8 0.8 broadcast_select_fusion
  10.2 0.7 copy.36
  10.9 0.7 broadcast_in_dim.21
  11.6 4.8 %all-to-all-start = ((bf16[4,2,1,40,128]{4,1,3,2,0:T(2,128)(2,1)}), bf16[4,2,1,40,128]{4,1,3,2,0:T(2,128)(2,1)S(1)}, u32[]{:S(2)}, u32[]{:S(2)}) async-start(bf16[4,2,1,40,128]{4,1,3,2,0:T(2,128)(2,1)} %broadcast_in_dim.21), calls=%async_computation | async-start | bytes 163840 | tf_op jit(solution)/shard_map/all_to_all | solution.py:22
  16.5 0.7 broadcast_add_fusion
  17.1 0.7 compare_convert_fusion
  17.8 3.2 %all-to-all-done = bf16[4,2,1,40,128]{4,1,3,2,0:T(2,128)(2,1)S(1)} async-done(((bf16[4,2,1,40,128]{4,1,3,2,0:T(2,128)(2,1)}), bf16[4,2,1,40,128]{4,1,3,2,0:T(2,128)(2,1)S(1)}, u32[]{:S(2)}, u32[]{:S(2)}) %all-to-all-start) | async-done | bytes 81952 | tf_op jit(solution)/shard_map/all_to_all | solution.py:22
  21.0 6.4 %fusion.30 = f32[2,1,160,128]{3,0,2,1:T(2,128)S(1)} fusion(bf16[2,160,128]{2,0,1:T(2,128)(2,1)S(1)} %bitcast.137, s32[160,128]{1,0:T(8,128)} %param.7), kind=kOutput, calls=%fused_computation.34 | convolution fusion | flops 13107200 | bytes 327680 | tf_op jit(solution)/shard_map/cbsk,skp->cbsp/dot_general | solution.py:79
  29.8 1.7 fusion.44
  31.5 1.7 fusion.45
  33.2 1.7 fusion.29
  34.9 1.7 fusion.43
  36.6 1.7 fusion.28
  38.3 1.7 convolution_add_fusion.3
  40.1 0.7 fusion.94
  40.8 1.7 fusion.42
  42.5 1.7 convolution_subtract_fusion.3
  46.0 7.4 %all_to_all.15 = f32[4,40,2,1,128]{4,1,2,3,0:T(8,128)S(1)} all-to-all(f32[4,40,2,1,128]{4,1,2,3,0:T(8,128)S(1)} %copy.37), channel_id=1, replica_groups=mesh['band_0'=8,'band_1'=12,'band_2'=2,'ga'=4] {'ga'}, dimensions={0} | all-to-all | bytes 327680 | tf_op jit(solution)/shard_map/all_to_all | solution.py:36
  53.4 2.8 %fusion.36 = bf16[2,1,40,128]{3,0,2,1:T(2,128)(2,1)S(1)} fusion(s32[40,128]{1,0:T(8,128)S(1)} %get-tuple-element.19, f32[2,40,128]{2,1,0:T(8,128)S(1)} %bitcast.139, pred[40,128]{1,0:T(8,128)(4,1)S(1)} %broadcast_compare_fusion, f32[40,128]{1,0:T(8,128)S(1)} %get-tuple-element.18, bf16[2,1,40,128]{3,2,1,0:T(8,128)(2,1)S(1)} %copy-done), kind=kOutput, calls=%fused_computation.46 | convolution fusion | flops 16435200 | bytes 128000 | tf_op jit(solution)/shard_map/cbsp,skp->cbsk/dot_general | solution.py:83
  56.2 87.8 %all-gather.5.cloned.1.call-done = bf16[2,192,40,128]{3,2,0,1:T(8,128)(2,1)} async-done(((bf16[2,1,40,128]{3,2,0,1:T(8,128)(2,1)}), bf16[2,192,40,128]{3,2,0,1:T(8,128)(2,1)}) %all-gather.5.cloned.1.call-update) | async-done | bytes 3932176 | tf_op jit(solution)/shard_map/all_gather | solution.py:184
  144.0 2.8 %fusion.186 = (bf16[1,192,40,128]{3,2,0,1:T(8,128)(2,1)S(1)}, bf16[1,192,40,128]{3,2,0,1:T(8,128)(2,1)S(1)}) fusion(bf16[2,192,40,128]{3,2,0,1:T(8,128)(2,1)} %all-gather.5.cloned.1.call-done), kind=kLoop, calls=%fused_computation.199 | loop fusion | bytes 7864320 | tf_op jit(solution)/shard_map/slice | solution.py:138
  148.7 0.6 fusion.11
  150.0 0.6 fusion.9
  152.6 4.0 %all-to-all-start.2 = ((f32[4,2,2,192,1]{3,2,4,1,0:T(2,128)}), f32[4,2,2,192,1]{3,2,4,1,0:T(2,128)S(1)}, u32[]{:S(2)}, u32[]{:S(2)}) async-start(f32[4,2,2,192,1]{3,2,4,1,0:T(2,128)} %broadcast_in_dim.24), calls=%async_computation.2 | async-start | bytes 32768 | tf_op jit(solution)/shard_map/all_to_all | solution.py:22
  157.1 3.6 %all-to-all-done.2 = f32[4,2,2,192,1]{3,2,4,1,0:T(2,128)S(1)} async-done(((f32[4,2,2,192,1]{3,2,4,1,0:T(2,128)}), f32[4,2,2,192,1]{3,2,4,1,0:T(2,128)S(1)}, u32[]{:S(2)}, u32[]{:S(2)}) %all-to-all-start.2) | async-done | bytes 12320 | tf_op jit(solution)/shard_map/all_to_all | solution.py:22
  160.8 19.0 %all-gather = f32[16,2,192]{2,1,0:T(2,128)S(1)} all-gather(f32[2,2,192]{2,1,0:T(2,128)S(1)} %reduce_sum.22), channel_id=2, replica_groups=mesh['band_0'=8,'band_1'=12,'band_2'=2,'ga'=4] {'band_0'}, dimensions={0}, use_global_device_ids=true | all-gather | bytes 27648 | tf_op jit(solution)/shard_map/all_gather | solution.py:47
  179.8 18.5 %all-gather.1 = f32[96,2,2,192,1]{3,2,4,1,0:T(2,128)S(1)} all-gather(f32[8,2,2,192,1]{3,2,4,1,0:T(2,128)S(1)} %bitcast.134), channel_id=3, replica_groups=mesh['band_0'=8,'band_1'=12,'band_2'=2,'ga'=4] {'band_1'}, dimensions={0}, use_global_device_ids=true | all-gather | bytes 319488 | tf_op jit(solution)/shard_map/all_gather | solution.py:47
  198.4 15.8 %all-gather.2 = f32[24,8,2,2,192,1]{4,1,0,3,2,5:T(8,128)S(1)} all-gather(f32[12,8,2,2,192,1]{4,1,0,3,2,5:T(8,128)S(1)} %bitcast.130), channel_id=4, replica_groups=mesh['band_0'=8,'band_1'=12,'band_2'=2,'ga'=4] {'band_2'}, dimensions={0}, use_global_device_ids=true | all-gather | bytes 884736 | tf_op jit(solution)/shard_map/all_gather | solution.py:47
  215.0 0.9 copy.47
  215.9 0.9 copy.48
  (41 shorter events, 10.6 us)
Async XLA Ops:
  7.2 136.9 %all-gather.5.cloned.1.call-start = ((), (), s32[]{:S(2)}) async-start(), calls=%async_computation.3 | async-start | bytes 3952640 | tf_op jit(solution)/shard_map/all_gather | solution.py:184
  11.6 9.4 %all-to-all-start = ((bf16[4,2,1,40,128]{4,1,3,2,0:T(2,128)(2,1)}), bf16[4,2,1,40,128]{4,1,3,2,0:T(2,128)(2,1)S(1)}, u32[]{:S(2)}, u32[]{:S(2)}) async-start(bf16[4,2,1,40,128]{4,1,3,2,0:T(2,128)(2,1)} %broadcast_in_dim.21), calls=%async_computation | async-start | bytes 163840 | tf_op jit(solution)/shard_map/all_to_all | solution.py:22
  27.5 5.7 %copy-start.1 = (f32[120,480]{1,0:T(8,128)S(1)}, f32[120,480]{1,0:T(8,128)}, u32[]{:S(2)}) copy-start(f32[120,480]{1,0:T(8,128)} %param.5) | copy-start | bytes 691204
  40.0 13.3 %copy-start = (bf16[2,1,40,128]{3,2,1,0:T(8,128)(2,1)S(1)}, bf16[2,1,40,128]{3,2,1,0:T(8,128)(2,1)}, u32[]{:S(2)}) copy-start(bf16[2,1,40,128]{3,2,1,0:T(8,128)(2,1)} %param.4) | copy-start | bytes 61444
  152.6 8.2 %all-to-all-start.2 = ((f32[4,2,2,192,1]{3,2,4,1,0:T(2,128)}), f32[4,2,2,192,1]{3,2,4,1,0:T(2,128)S(1)}, u32[]{:S(2)}, u32[]{:S(2)}) async-start(f32[4,2,2,192,1]{3,2,4,1,0:T(2,128)} %broadcast_in_dim.24), calls=%async_computation.2 | async-start | bytes 32768 | tf_op jit(solution)/shard_map/all_to_all | solution.py:22
Sparse Core Ops, SparseCore 0:
  12.3 131.6 all-gather.4
where the time goes:
time: 224 us
  waiting for transfers between devices  94.6 us (42%)
  blocking collectives  60.7 us (27%)
  matrix products  32.5 us (15%)
  between operations  14.3 us (6%)
  local copies, waits for them, and re-layouts  8.99 us (4%)
  starting transfers between devices  8.84 us (4%)
  other arithmetic  3.81 us (2%)
    all_gather x1, waiting for transfers between devices, body(): portion = lax.all_gather(masked, BAND, axis=1, tiled=True)  87.8 us
    all_gather x3, blocking collectives, stacked_from(): tiles = lax.all_gather(tiles, axes[k])  53.3 us
    all_to_all x2, starting transfers between devices, sent_to_all(): return lax.all_to_all(copies, axis, split_axis=0, concat_axis=0, tiled=True)  8.8 us
    all_to_all x1, blocking collectives, sum_at_owner(): lax.all_to_all(tiles, axis, split_axis=0, concat_axis=0, tiled=True)  7.36 us
    all_to_all x2, waiting for transfers between devices, sent_to_all(): return lax.all_to_all(copies, axis, split_axis=0, concat_axis=0, tiled=True)  6.8 us
    dot_general x1, matrix products, spread_entries(): jnp.einsum('cbsk,skp->cbsp', coeffs, selector, preferred_element_type=jnp...  6.44 us
  transfers between devices with their start and end apart: 3, of which 3 were waited for; matrix products, arithmetic and copies ran while one was open for 14% of the time, Pallas kernels for 0%

commit v1 on v0

v1 whole, which is shorter than its diff:
```python
import functools

import jax
import jax.numpy as jnp
import numpy as np
from jax import lax
from jax.experimental import pallas as pl
from jax.experimental.pallas import tpu as pltpu
from jax.sharding import Mesh
from jax.sharding import PartitionSpec as P

BAND = ("y", "z", "c")
M = 256
F32 = jnp.float32
BF16 = jnp.bfloat16


def hi_lo(table):
    hi = table.astype(np.float32).astype(jnp.bfloat16)
    lo = (table - hi.astype(np.float64)).astype(np.float32).astype(jnp.bfloat16)
    return np.stack([hi, lo])


def tables(points, radius):
    freq = np.arange(2 * radius) - radius + 1
    pos = np.arange(M)
    ang = 2.0 * np.pi * ((freq[:, None] * pos[None, :]) % M) / M
    cos, sin = np.cos(ang), np.sin(ang)
    wz = np.block([[cos, sin], [-sin, cos]])
    top = 2 * radius - 2
    q = np.arange(1, top + 1)
    shift = pos[:, None] / M - np.arange(points)[None, :] / points
    resample = np.ones((M, points))
    for k in q:
        resample += 2.0 * np.cos(2.0 * np.pi * k * shift)
    resample /= points
    return hi_lo(wz), hi_lo(wz.T), hi_lo(resample.T), hi_lo(resample)


def split(x):
    hi = x.astype(BF16)
    return hi, (x - hi.astype(F32)).astype(BF16)


def mm(a, b):
    return lax.dot_general(a, b, (((1,), (0,)), ((), ())), preferred_element_type=F32)


def mm_nt(a, b):
    return lax.dot_general(a, b, (((1,), (1,)), ((), ())), preferred_element_type=F32)


def first_kernel(ent_ref, orb_ref, pot_ref, bx_ref, packed_ref, own_ref):
    ent_t = ent_ref[...].T
    lane = lax.broadcasted_iota(jnp.int32, (128, 128), 1)
    sub = lax.broadcasted_iota(jnp.int32, (128, 128), 0)
    pieces = [[], []]
    for g in range(8):
        rows = []
        for r in range(5):
            s = 8 * g + r
            match = ent_t[:, s : s + 1] == lane
            rows.append(jnp.max(jnp.where(match, sub, -1), axis=0, keepdims=True))
        rows.append(jnp.full((3, 128), -1, jnp.int32))
        source = jnp.concatenate(rows, axis=0)
        index = jnp.maximum(source, 0)
        for c in range(2):
            block = orb_ref[c, 8 * g : 8 * g + 8, :]
            moved = jnp.take_along_axis(block, index, axis=1)
            pieces[c].append(jnp.where(source >= 0, moved, 0.0))
    spread = jnp.concatenate(pieces[0] + pieces[1], axis=0).astype(BF16)
    own_ref[...] = spread
    packed_ref[0:128, :] = spread
    v_hi, v_lo = split(pot_ref[...])
    vx = mm(v_hi, bx_ref[0]) + mm(v_lo, bx_ref[0]) + mm(v_hi, bx_ref[1])
    vx = jnp.concatenate([vx[:, :128], vx[:, 128:]], axis=0)
    hi, lo = split(vx)
    packed_ref[128:368, :] = hi
    packed_ref[368:608, :] = lo


def main_kernel(all_ref, own_ref, ent_ref, slot_row_ref, slot_col_ref, wz_ref, wx_ref, bz_ref, msg_ref, out_ref):
    def gathered_v(first):
        left = jnp.concatenate([all_ref[d, first : first + 120, :].astype(F32) for d in range(4)], axis=0)
        right = jnp.concatenate([all_ref[d, first + 120 : first + 240, :].astype(F32) for d in range(4)], axis=0)
        return jnp.concatenate([left, right], axis=1).astype(BF16)

    v_hi = gathered_v(128)
    v_lo = gathered_v(368)
    pot = mm(bz_ref[0], v_hi) + mm(bz_ref[1], v_hi) + mm(bz_ref[0], v_lo)
    pot = pot.T

    place = (
        lax.broadcasted_iota(jnp.int32, (128, 256), 0) == jnp.broadcast_to(slot_row_ref[...], (128, 256))
    ).astype(F32).astype(BF16)
    c_re = jnp.concatenate([all_ref[d, 0:64, :] for d in range(4)], axis=0)
    c_im = jnp.concatenate([all_ref[d, 64:128, :] for d in range(4)], axis=0)
    sticks = jnp.concatenate([mm(place, c_re), mm(place, c_im)], axis=0).astype(BF16)

    t = mm(wx_ref[0], sticks) + mm(wx_ref[1], sticks)
    t = jnp.concatenate([t[:M], t[M:]], axis=1)
    t_hi, t_lo = split(t)
    field = mm(t_hi, wz_ref[0]) + mm(t_lo, wz_ref[0]) + mm(t_hi, wz_ref[1])
    prod = jnp.concatenate([field[:, :M] * pot, field[:, M:] * pot], axis=1)
    p_hi, p_lo = split(prod)
    y = mm(p_hi, wx_ref[0]) + mm(p_lo, wx_ref[0]) + mm(p_hi, wx_ref[1])
    y = jnp.concatenate([y[:, :128], y[:, 128:]], axis=0)
    y_hi, y_lo = split(y)

    slot = slot_col_ref[...]
    pick = (lax.broadcasted_iota(jnp.int32, (64, 128), 1) == slot).astype(F32).astype(BF16)
    none = jnp.zeros((64, 128), BF16)
    pick = jnp.concatenate(
        [jnp.concatenate([pick, none], axis=1), jnp.concatenate([none, pick], axis=1)], axis=0
    )
    w_hi = mm(pick, wz_ref[0]).astype(BF16)
    w_lo = mm(pick, wz_ref[1]).astype(BF16)
    applied = (mm(w_hi, y_hi) + mm(w_hi, y_lo) + mm(w_lo, y_hi)) * (1.0 / (M * M))

    gx = slot - 63
    gz = lax.broadcasted_iota(jnp.int32, (64, 128), 1) - 63
    square = gx * gx + gz * gz
    inside = (square < 64 * 64) & (slot >= 0)
    kinetic = square.astype(F32) * (1.0 / 4096.0)
    own = own_ref[...].astype(F32)
    h = []
    for c in range(2):
        value = kinetic * own[64 * c : 64 * c + 64] + applied[64 * c : 64 * c + 64]
        h.append(jnp.where(inside, value, 0.0).astype(BF16).astype(F32))
    ent = ent_ref[...]
    index = jnp.maximum(ent, 0)
    for c in range(2):
        for g in range(8):
            rows = slice(8 * g, 8 * g + 8)
            moved = jnp.take_along_axis(h[c][rows], index[rows], axis=1)
            out_ref[c, rows, :] = jnp.where(ent[rows] >= 0, moved, 0.0)
    for g in range(8):
        rows = slice(8 * g, 8 * g + 8)
        msg = [own[rows], own[64 + 8 * g : 72 + 8 * g], h[0][rows], h[1][rows]]
        msg_ref[g] = jnp.concatenate(msg, axis=0).astype(BF16)


def product_kernel(psi_ref, own_ref, block_ref, psi_s, own_s):
    for c in range(2):
        for z in range(12):
            for y in range(8):
                band = y * 24 + z * 2 + c
                psi_s[16 * band : 16 * band + 16, :] = psi_ref[c, z, y].astype(F32)
    for y in range(8):
        own_s[32 * y : 32 * y + 32, :] = own_ref[y].astype(F32)

    def entries(ref, part, count, pitch):
        rows = [ref[pl.ds(8 * part + r, count, stride=pitch), :] for r in range(5)]
        return jnp.concatenate(rows, axis=1)

    p_re = entries(psi_s, 0, 192, 16).astype(BF16)
    p_im = entries(psi_s, 1, 192, 16).astype(BF16)
    m_re, m_im, a_re, a_im = [entries(own_s, q, 8, 32) for q in range(4)]
    left_re = jnp.concatenate([m_re, m_im, a_re, a_im], axis=0).astype(BF16)
    left_im = jnp.concatenate([m_im, -m_re, a_im, -a_re], axis=0).astype(BF16)
    block = (mm_nt(left_re, p_re) + mm_nt(left_im, p_im)) * (1.0 / 16384.0)
    block_ref[0:32, :] = block[:, :128]
    block_ref[32:48, :] = jnp.concatenate([block[:16, 128:], block[16:, 128:]], axis=1)


def last_kernel(all_ref, s_ref, h_ref, t_s):
    for c in range(2):
        for z in range(12):
            tail = all_ref[c, z, 32:48, :]
            for m in range(4):
                rows = pl.ds(z * 2 + c, 8, stride=24)
                t_s[2 * m, rows, :] = all_ref[c, z, 8 * m : 8 * m + 8, :]
                half = tail[8 * (m % 2) : 8 * (m % 2) + 8]
                if m >= 2:
                    half = jnp.concatenate([half[:, 64:], half[:, :64]], axis=1)
                t_s[2 * m + 1, rows, :] = half
    for m in range(4):
        ref = s_ref if m < 2 else h_ref
        ref[m % 2, 0:128, :] = t_s[2 * m].T
        ref[m % 2, 128:192, :] = t_s[2 * m + 1].T[:64]


def call(kernel, outs, *args, scratch=()):
    return pl.pallas_call(
        kernel,
        out_shape=outs,
        scratch_shapes=list(scratch),
        compiler_params=pltpu.CompilerParams(vmem_limit_bytes=48 * 1024 * 1024),
    )(*args)


def shape(dims, dtype):
    return jax.ShapeDtypeStruct(dims, dtype)


def body(orbitals, potential, slot_sticks, stick_entries):
    points = potential.shape[1]
    wz, wx, bx, bz = tables(points, 64)
    ga = lax.axis_index("x")
    own_lists = lax.dynamic_slice_in_dim(stick_entries, ga * 40, 40, 0)
    ent = jnp.pad(own_lists.reshape(8, 5, 128), ((0, 0), (0, 3), (0, 0)), constant_values=-1).reshape(64, 128)
    slots = jnp.pad(slot_sticks.reshape(32, 5), ((0, 0), (0, 3)), constant_values=-1)
    slot_row = slots.reshape(1, 256)
    slot_col = lax.dynamic_slice_in_dim(slots, ga * 8, 8, 0).reshape(64, 1)
    orb = jnp.pad(
        orbitals.reshape(2, 8, 5, 128).astype(F32), ((0, 0), (0, 0), (0, 3), (0, 0))
    ).reshape(2, 64, 128)
    packed, own = call(
        first_kernel, [shape((608, 128), BF16), shape((128, 128), BF16)], ent, orb, potential, bx
    )
    everyone = lax.all_gather(packed, "x")
    msg, out = call(
        main_kernel,
        [shape((8, 32, 128), BF16), shape((2, 64, 128), F32)],
        everyone, own, ent, slot_row, slot_col, wz, wx, bz,
    )
    applied_orbitals = out.reshape(2, 8, 8, 128)[:, :, :5].reshape(2, 1, 40, 128).astype(BF16)
    arrived = lax.all_to_all(msg, "y", 0, 0, tiled=True)
    psi = lax.all_gather(arrived[:, :16], "z")
    psi = lax.all_gather(psi, "c")
    block = call(
        product_kernel,
        shape((48, 128), F32),
        psi, arrived,
        scratch=[pltpu.VMEM((192 * 16, 128), F32), pltpu.VMEM((8 * 32, 128), F32)],
    )
    block = lax.all_gather(block, "x").sum(axis=0)
    block = lax.all_gather(block, "y").sum(axis=0)
    blocks = lax.all_gather(lax.all_gather(block, "z"), "c")
    correlation, reduced = call(
        last_kernel,
        [shape((2, 192, 192), F32), shape((2, 192, 192), F32)],
        blocks,
        scratch=[pltpu.VMEM((8, 192, 128), F32)],
    )
    return applied_orbitals, correlation, reduced


def solution(mesh):
    finer = Mesh(mesh.devices.reshape(8, 12, 2, mesh.shape["ga"]), ("y", "z", "c", "x"))
    return jax.shard_map(
        body,
        mesh=finer,
        in_specs=(P(None, BAND, "x", None), P("x", None), P(), P()),
        out_specs=(P(None, BAND, "x", None), P(), P()),
        check_vma=False,
    )
```

time: 224 us -> 137 us (0.61)
  waiting for transfers between devices: 94.6 us -> 6.57 us
  blocking collectives: 60.7 us -> 112 us
  matrix products: 32.5 us -> 0 us
  between operations: 14.3 us -> 0.77 us
  Pallas kernels: 0 us -> 5.66 us
  local copies, waits for them, and re-layouts: 8.99 us -> 3.39 us
  other arithmetic: 3.81 us -> 0.04 us
    all_gather x1 -> x0, waiting for transfers between devices: 87.8 us -> none  [body(): portion = lax.all_gather(masked, BAND, axis=1, tiled=True)]
    all_gather x3 -> x7, blocking collectives: 53.3 us -> 112 us  [the longest x2 31.7 us: body(): blocks = lax.all_gather(lax.all_gather(block, 'z'), 'c')]
    dot_general x26 -> x0, matrix products: 32.5 us -> none  [the longest x1 6.44 us: spread_entries(): jnp.einsum('cbsk,skp->cbsp', coeffs, selector, preferred_element_type=jnp...]
    all_to_all x1 -> x0, blocking collectives: 7.36 us -> none  [sum_at_owner(): lax.all_to_all(tiles, axis, split_axis=0, concat_axis=0, tiled=True)]
    pallas_call x0 -> x4, Pallas kernels: none -> 5.66 us  [call(): pl.pallas_call(kernel, out_shape=outs, scratch_shapes=list(scratch), comp...]
    slice x2 -> x1, local copies, waits for them, and re-layouts: 2.98 us -> 0.01 us  [body(): psi = lax.all_gather(arrived[:, :16], 'z')]
    all_to_all x2 -> x1, starting transfers between devices: 8.8 us -> 8.05 us  [body(): arrived = lax.all_to_all(msg, 'y', 0, 0, tiled=True)]
    all_to_all x2 -> x1, waiting for transfers between devices: 6.8 us -> 6.57 us  [body(): arrived = lax.all_to_all(msg, 'y', 0, 0, tiled=True)]
  transfers between devices with their start and end apart: 3 -> 1, of which waited for: 3 -> 1; matrix products, arithmetic and copies ran while one was open for 14% -> 0% of each run, Pallas kernels for 0% -> 0%
where the time goes in v1:
time: 137 us; the launch traced here: 136 us
  blocking collectives  112 us (82%)
  starting transfers between devices  8.05 us (6%)
  waiting for transfers between devices  6.57 us (5%)
  Pallas kernels  5.66 us (4%)
  local copies, waits for them, and re-layouts  3.39 us (2%)
    all_gather x2, blocking collectives, body(): blocks = lax.all_gather(lax.all_gather(block, 'z'), 'c')  31.7 us
    all_gather x1, blocking collectives, body(): psi = lax.all_gather(arrived[:, :16], 'z')  29.1 us
    all_gather x1, blocking collectives, body(): block = lax.all_gather(block, 'y').sum(axis=0)  19.1 us
    all_gather x1, blocking collectives, body(): everyone = lax.all_gather(packed, 'x')  11.4 us
    all_gather x1, blocking collectives, body(): psi = lax.all_gather(psi, 'c')  11.1 us
    all_gather x1, blocking collectives, body(): block = lax.all_gather(block, 'x').sum(axis=0)  9.47 us
    all_to_all x1, starting transfers between devices, body(): arrived = lax.all_to_all(msg, 'y', 0, 0, tiled=True)  8.05 us
    all_to_all x1, waiting for transfers between devices, body(): arrived = lax.all_to_all(msg, 'y', 0, 0, tiled=True)  6.57 us
  transfers between devices with their start and end apart: 1, of which 1 were waited for; matrix products, arithmetic and copies ran while one was open for 0% of the time, Pallas kernels for 0%

profile of v1, /device:TPU:1, one launch (start us, length us, event | category | flops | bytes accessed | tf_op | source)
XLA Modules:
  0.0 136.3 jit_solution(11788149959731340876)
XLA Ops:
  0.6 0.0 copy-start
  0.6 0.0 copy-start.4
  0.7 0.8 reshape.51
  1.5 0.1 reshape.52.slot_row_ref
  1.6 0.0 copy-done
  1.7 0.7 copy.27
  2.4 0.1 reshape.64.slot_col_ref
  2.5 0.0 copy-done.4
  2.5 0.0 copy-start.5
  2.6 0.9 copy-done.5
  3.5 0.0 copy-start.2
  3.5 0.0 copy-start.3
  3.5 1.6 %shard_map.103 = (bf16[608,128]{1,0:T(8,128)(2,1)S(1)}, bf16[128,128]{1,0:T(8,128)(2,1)S(1)}) custom-call(s32[64,128]{1,0:T(8,128)S(1)} %pad_bitcast_fusion.ent_ref, f32[2,64,128]{2,1,0:T(8,128)S(1)} %bitcast_convert_fusion.orb_ref, f32[120,480]{1,0:T(8,128)S(1)} %copy-done.5, bf16[2,480,256]{2,1,0:T(8,128)(2,1)S(1)} %copy-done.4), custom_call_target="tpu_custom_call" | custom-call | tf_op jit(solution)/shard_map/pallas_call | solution.py:184
  5.1 0.0 copy-start.1
  5.1 11.4 %all-gather = bf16[2432,128]{1,0:T(8,128)(2,1)S(1)} all-gather(bf16[608,128]{1,0:T(8,128)(2,1)S(1)} %get-tuple-element.9), channel_id=2, replica_groups=mesh['y'=8,'z'=12,'c'=2,'x'=4] {'x'}, dimensions={0}, use_global_device_ids=true | all-gather | bytes 778240 | tf_op jit(solution)/shard_map/all_gather | solution.py:211
  16.4 0.0 copy-done.2
  16.4 0.0 copy-done.3
  16.4 0.0 copy-done.1
  16.5 2.3 %shard_map.104 = (bf16[8,32,128]{2,1,0:T(8,128)(2,1)}, f32[2,64,128]{2,1,0:T(8,128)S(1)}) custom-call(bf16[4,608,128]{2,1,0:T(8,128)(2,1)S(1)} %bitcast.18, bf16[128,128]{1,0:T(8,128)(2,1)S(1)} %get-tuple-element.10.own_ref, s32[64,128]{1,0:T(8,128)S(1)} %pad_bitcast_fusion.ent_ref, s32[1,256]{1,0:T(1,128)S(1)} %reshape.52.slot_row_ref, ...), custom_call_target="tpu_custom_call" | custom-call | tf_op jit(solution)/shard_map/pallas_call | solution.py:184
  18.8 8.0 %all-to-all-start = ((bf16[8,32,128]{2,1,0:T(8,128)(2,1)}), bf16[8,32,128]{2,1,0:T(8,128)(2,1)S(1)}, u32[]{:S(2)}, u32[]{:S(2)}) async-start(bf16[8,32,128]{2,1,0:T(8,128)(2,1)} %get-tuple-element.12), calls=%async_computation | async-start | bytes 131072 | tf_op jit(solution)/shard_map/all_to_all | solution.py:218
  26.9 0.6 copy.31
  27.5 6.6 %all-to-all-done.own_ref = bf16[8,32,128]{2,1,0:T(8,128)(2,1)S(1)} async-done(((bf16[8,32,128]{2,1,0:T(8,128)(2,1)}), bf16[8,32,128]{2,1,0:T(8,128)(2,1)S(1)}, u32[]{:S(2)}, u32[]{:S(2)}) %all-to-all-start) | async-done | bytes 65568 | tf_op jit(solution)/shard_map/all_to_all | solution.py:218
  34.1 29.1 %all-gather.1 = bf16[96,16,128]{2,1,0:T(8,128)(2,1)S(1)} all-gather(bf16[8,16,128]{2,1,0:T(8,128)(2,1)S(1)} %slice.10), channel_id=3, replica_groups=mesh['y'=8,'z'=12,'c'=2,'x'=4] {'z'}, dimensions={0}, use_global_device_ids=true | all-gather | bytes 425984 | tf_op jit(solution)/shard_map/all_gather | solution.py:219
  63.2 11.1 %all-gather.2 = bf16[24,8,16,128]{3,2,1,0:T(8,128)(2,1)S(1)} all-gather(bf16[12,8,16,128]{3,2,1,0:T(8,128)(2,1)S(1)} %bitcast.20), channel_id=4, replica_groups=mesh['y'=8,'z'=12,'c'=2,'x'=4] {'c'}, dimensions={0}, use_global_device_ids=true | all-gather | bytes 1179648 | tf_op jit(solution)/shard_map/all_gather | solution.py:220
  74.3 0.6 shard_map.105
  74.9 9.5 %all-gather.3 = f32[192,128]{1,0:T(8,128)S(1)} all-gather(f32[48,128]{1,0:T(8,128)S(1)} %shard_map.105), channel_id=5, replica_groups=mesh['y'=8,'z'=12,'c'=2,'x'=4] {'x'}, dimensions={0}, use_global_device_ids=true | all-gather | bytes 122880 | tf_op jit(solution)/shard_map/all_gather | solution.py:227
  84.4 19.1 %all-gather.4 = f32[384,128]{1,0:T(8,128)S(1)} all-gather(f32[48,128]{1,0:T(8,128)S(1)} %reduce_sum.18), channel_id=6, replica_groups=mesh['y'=8,'z'=12,'c'=2,'x'=4] {'y'}, dimensions={0}, use_global_device_ids=true | all-gather | bytes 221184 | tf_op jit(solution)/shard_map/all_gather | solution.py:228
  103.5 16.0 %all-gather.5 = f32[576,128]{1,0:T(8,128)S(1)} all-gather(f32[48,128]{1,0:T(8,128)S(1)} %reduce_sum.19), channel_id=7, replica_groups=mesh['y'=8,'z'=12,'c'=2,'x'=4] {'z'}, dimensions={0}, use_global_device_ids=true | all-gather | bytes 319488 | tf_op jit(solution)/shard_map/all_gather | solution.py:229
  119.4 15.7 %all-gather.6 = f32[24,48,128]{2,1,0:T(8,128)S(1)} all-gather(f32[12,48,128]{2,1,0:T(8,128)S(1)} %bitcast.21), channel_id=8, replica_groups=mesh['y'=8,'z'=12,'c'=2,'x'=4] {'c'}, dimensions={0}, use_global_device_ids=true | all-gather | bytes 884736 | tf_op jit(solution)/shard_map/all_gather | solution.py:229
  135.2 1.2 shard_map.106
  (12 shorter events, 0.1 us)
Async XLA Ops:
  0.6 1.0 copy-start
  0.6 1.9 %copy-start.4 = (bf16[2,480,256]{2,1,0:T(8,128)(2,1)S(1)}, bf16[2,480,256]{2,1,0:T(8,128)(2,1)}, u32[]{:S(2)}) copy-start(bf16[2,480,256]{2,1,0:T(8,128)(2,1)} %constant.29.clone.bx_ref) | copy-start | bytes 1474564
  2.5 0.9 copy-start.5
  3.5 13.0 %copy-start.2 = (bf16[2,512,256]{2,1,0:T(8,128)(2,1)S(1)}, bf16[2,512,256]{2,1,0:T(8,128)(2,1)}, u32[]{:S(2)}) copy-start(bf16[2,512,256]{2,1,0:T(8,128)(2,1)} %constant.31.clone.wx_ref) | copy-start | bytes 1572868
  3.5 13.0 %copy-start.3 = (bf16[2,256,512]{2,1,0:T(8,128)(2,1)S(1)}, bf16[2,256,512]{2,1,0:T(8,128)(2,1)}, u32[]{:S(2)}) copy-start(bf16[2,256,512]{2,1,0:T(8,128)(2,1)} %constant.30.clone.wz_ref) | copy-start | bytes 1572868
  5.1 11.4 %copy-start.1 = (bf16[2,256,480]{2,1,0:T(8,128)(2,1)S(1)}, bf16[2,256,480]{2,1,0:T(8,128)(2,1)}, u32[]{:S(2)}) copy-start(bf16[2,256,480]{2,1,0:T(8,128)(2,1)} %constant.32.clone.bz_ref) | copy-start | bytes 1474564
  18.8 15.3 %all-to-all-start = ((bf16[8,32,128]{2,1,0:T(8,128)(2,1)}), bf16[8,32,128]{2,1,0:T(8,128)(2,1)S(1)}, u32[]{:S(2)}, u32[]{:S(2)}) async-start(bf16[8,32,128]{2,1,0:T(8,128)(2,1)} %get-tuple-element.12), calls=%async_computation | async-start | bytes 131072 | tf_op jit(solution)/shard_map/all_to_all | solution.py:218

commit v2 on v1

--- a/solution.py
+++ b/solution.py
@@ -50,27 +50,30 @@
     return lax.dot_general(a, b, (((1,), (1,)), ((), ())), preferred_element_type=F32)
 
 
-def first_kernel(ent_ref, orb_ref, pot_ref, bx_ref, packed_ref, own_ref):
-    ent_t = ent_ref[...].T
+def first_kernel(ent_ref, orb_ref, pot_ref, bx_ref, zmsg_ref, packed_ref, orb_s):
+    first = pl.multiple_of(lax.axis_index("x") * 40, 8)
+    ent_t = ent_ref[pl.ds(first, 40), :].T
+    orb_s[:, 0:40, :] = orb_ref[...].astype(F32)
+    orb_s[:, 40:48, :] = jnp.zeros((2, 8, 128), F32)
     lane = lax.broadcasted_iota(jnp.int32, (128, 128), 1)
     sub = lax.broadcasted_iota(jnp.int32, (128, 128), 0)
     pieces = [[], []]
     for g in range(8):
         rows = []
         for r in range(5):
-            s = 8 * g + r
+            s = 5 * g + r
             match = ent_t[:, s : s + 1] == lane
             rows.append(jnp.max(jnp.where(match, sub, -1), axis=0, keepdims=True))
         rows.append(jnp.full((3, 128), -1, jnp.int32))
         source = jnp.concatenate(rows, axis=0)
         index = jnp.maximum(source, 0)
         for c in range(2):
-            block = orb_ref[c, 8 * g : 8 * g + 8, :]
-            moved = jnp.take_along_axis(block, index, axis=1)
+            moved = jnp.take_along_axis(orb_s[c, 5 * g : 5 * g + 8, :], index, axis=1)
             pieces[c].append(jnp.where(source >= 0, moved, 0.0))
-    spread = jnp.concatenate(pieces[0] + pieces[1], axis=0).astype(BF16)
-    own_ref[...] = spread
-    packed_ref[0:128, :] = spread
+        group = jnp.concatenate([pieces[0][g], pieces[1][g]], axis=0).astype(BF16)
+        for z in range(12):
+            zmsg_ref[z, g] = group
+    packed_ref[0:128, :] = jnp.concatenate(pieces[0] + pieces[1], axis=0).astype(BF16)
     v_hi, v_lo = split(pot_ref[...])
     vx = mm(v_hi, bx_ref[0]) + mm(v_lo, bx_ref[0]) + mm(v_hi, bx_ref[1])
     vx = jnp.concatenate([vx[:, :128], vx[:, 128:]], axis=0)
@@ -79,7 +82,11 @@
     packed_ref[368:608, :] = lo
 
 
-def main_kernel(all_ref, own_ref, ent_ref, slot_row_ref, slot_col_ref, wz_ref, wx_ref, bz_ref, msg_ref, out_ref):
+def main_kernel(
+    all_ref, psi_ref, ent_ref, slot_row_ref, slot_col_ref, wz_ref, wx_ref, bz_ref, msg_ref, out_ref, psi_s, ent_s, out_s
+):
+    d = lax.axis_index("x")
+
     def gathered_v(first):
         left = jnp.concatenate([all_ref[d, first : first + 120, :].astype(F32) for d in range(4)], axis=0)
         right = jnp.concatenate([all_ref[d, first + 120 : first + 240, :].astype(F32) for d in range(4)], axis=0)
@@ -122,45 +129,60 @@
     square = gx * gx + gz * gz
     inside = (square < 64 * 64) & (slot >= 0)
     kinetic = square.astype(F32) * (1.0 / 4096.0)
-    own = own_ref[...].astype(F32)
+    own = all_ref[d, 0:128, :].astype(F32)
     h = []
     for c in range(2):
         value = kinetic * own[64 * c : 64 * c + 64] + applied[64 * c : 64 * c + 64]
         h.append(jnp.where(inside, value, 0.0).astype(BF16).astype(F32))
-    ent = ent_ref[...]
-    index = jnp.maximum(ent, 0)
+    ent_s[0:40, :] = ent_ref[pl.ds(pl.multiple_of(d * 40, 8), 40), :]
+    ent_s[40:48, :] = jnp.full((8, 128), -1, jnp.int32)
+    for g in range(8):
+        ent = ent_s[5 * g : 5 * g + 8, :]
+        index = jnp.maximum(ent, 0)
+        for c in range(2):
+            moved = jnp.take_along_axis(h[c][8 * g : 8 * g + 8], index, axis=1)
+            out_s[c, 5 * g : 5 * g + 8, :] = jnp.where(ent >= 0, moved, 0.0)
+    out_ref[...] = out_s[:, 0:40, :].astype(BF16)
+
+    for z in range(12):
+        for g in range(8):
+            psi_s[128 * z + 16 * g : 128 * z + 16 * g + 16, :] = psi_ref[z, g].astype(F32)
+    for g in range(8):
+        rows = []
+        for r in range(5):
+            for c in range(2):
+                rows.append(psi_s[pl.ds(16 * g + 8 * c + r, 12, stride=128), :])
+        rows += [h[0][8 * g : 8 * g + 8], h[1][8 * g : 8 * g + 8], jnp.zeros((8, 128), F32)]
+        msg_ref[g] = jnp.concatenate(rows, axis=0).astype(BF16)
+
+
+def product_kernel(both_ref, own_ref, block_ref, all_s, own_s, psi_s):
     for c in range(2):
-        for g in range(8):
-            rows = slice(8 * g, 8 * g + 8)
-            moved = jnp.take_along_axis(h[c][rows], index[rows], axis=1)
-            out_ref[c, rows, :] = jnp.where(ent[rows] >= 0, moved, 0.0)
-    for g in range(8):
-        rows = slice(8 * g, 8 * g + 8)
-        msg = [own[rows], own[64 + 8 * g : 72 + 8 * g], h[0][rows], h[1][rows]]
-        msg_ref[g] = jnp.concatenate(msg, axis=0).astype(BF16)
-
-
-def product_kernel(psi_ref, own_ref, block_ref, psi_s, own_s):
-    for c in range(2):
-        for z in range(12):
-            for y in range(8):
-                band = y * 24 + z * 2 + c
-                psi_s[16 * band : 16 * band + 16, :] = psi_ref[c, z, y].astype(F32)
+        for y in range(8):
+            at = (8 * c + y) * 144
+            all_s[at : at + 144, :] = both_ref[c, y].astype(F32)
+            for r in range(5):
+                for part in range(2):
+                    row = at + 24 * r + 12 * part
+                    psi_s[5 * part + r, pl.ds(24 * y + c, 12, stride=2), :] = all_s[row : row + 12, :]
     for y in range(8):
-        own_s[32 * y : 32 * y + 32, :] = own_ref[y].astype(F32)
-
-    def entries(ref, part, count, pitch):
-        rows = [ref[pl.ds(8 * part + r, count, stride=pitch), :] for r in range(5)]
+        own_s[144 * y : 144 * y + 144, :] = own_ref[y].astype(F32)
+    z = lax.axis_index("z")
+
+    def entries(first, pitch):
+        rows = [own_s[pl.ds(first + pitch * r, 8, stride=144), :] for r in range(5)]
         return jnp.concatenate(rows, axis=1)
 
-    p_re = entries(psi_s, 0, 192, 16).astype(BF16)
-    p_im = entries(psi_s, 1, 192, 16).astype(BF16)
-    m_re, m_im, a_re, a_im = [entries(own_s, q, 8, 32) for q in range(4)]
+    m_re, m_im = entries(z, 24), entries(z + 12, 24)
+    a_re, a_im = entries(120, 1), entries(128, 1)
     left_re = jnp.concatenate([m_re, m_im, a_re, a_im], axis=0).astype(BF16)
     left_im = jnp.concatenate([m_im, -m_re, a_im, -a_re], axis=0).astype(BF16)
+    p_re = jnp.concatenate([psi_s[r] for r in range(5)], axis=1).astype(BF16)
+    p_im = jnp.concatenate([psi_s[5 + r] for r in range(5)], axis=1).astype(BF16)
     block = (mm_nt(left_re, p_re) + mm_nt(left_im, p_im)) * (1.0 / 16384.0)
-    block_ref[0:32, :] = block[:, :128]
-    block_ref[32:48, :] = jnp.concatenate([block[:16, 128:], block[16:, 128:]], axis=1)
+    for x in range(4):
+        block_ref[x, 0:32, :] = block[:, :128]
+        block_ref[x, 32:48, :] = jnp.concatenate([block[:16, 128:], block[16:, 128:]], axis=1)
 
 
 def last_kernel(all_ref, s_ref, h_ref, t_s):
@@ -194,46 +216,42 @@
 
 
 def body(orbitals, potential, slot_sticks, stick_entries):
-    points = potential.shape[1]
-    wz, wx, bx, bz = tables(points, 64)
-    ga = lax.axis_index("x")
-    own_lists = lax.dynamic_slice_in_dim(stick_entries, ga * 40, 40, 0)
-    ent = jnp.pad(own_lists.reshape(8, 5, 128), ((0, 0), (0, 3), (0, 0)), constant_values=-1).reshape(64, 128)
+    wz, wx, bx, bz = tables(potential.shape[1], 64)
     slots = jnp.pad(slot_sticks.reshape(32, 5), ((0, 0), (0, 3)), constant_values=-1)
     slot_row = slots.reshape(1, 256)
-    slot_col = lax.dynamic_slice_in_dim(slots, ga * 8, 8, 0).reshape(64, 1)
-    orb = jnp.pad(
-        orbitals.reshape(2, 8, 5, 128).astype(F32), ((0, 0), (0, 0), (0, 3), (0, 0))
-    ).reshape(2, 64, 128)
-    packed, own = call(
-        first_kernel, [shape((608, 128), BF16), shape((128, 128), BF16)], ent, orb, potential, bx
-    )
+    slot_col = lax.dynamic_slice_in_dim(slots, lax.axis_index("x") * 8, 8, 0).reshape(64, 1)
+    zmsg, packed = call(
+        first_kernel,
+        [shape((12, 8, 16, 128), BF16), shape((608, 128), BF16)],
+        stick_entries, orbitals.reshape(2, 40, 128), potential, bx,
+        scratch=[pltpu.VMEM((2, 48, 128), F32)],
+    )
+    psi = lax.all_to_all(zmsg, "z", 0, 0, tiled=True)
     everyone = lax.all_gather(packed, "x")
     msg, out = call(
         main_kernel,
-        [shape((8, 32, 128), BF16), shape((2, 64, 128), F32)],
-        everyone, own, ent, slot_row, slot_col, wz, wx, bz,
-    )
-    applied_orbitals = out.reshape(2, 8, 8, 128)[:, :, :5].reshape(2, 1, 40, 128).astype(BF16)
+        [shape((8, 144, 128), BF16), shape((2, 40, 128), BF16)],
+        everyone, psi, stick_entries, slot_row, slot_col, wz, wx, bz,
+        scratch=[pltpu.VMEM((1536, 128), F32), pltpu.VMEM((48, 128), jnp.int32), pltpu.VMEM((2, 48, 128), F32)],
+    )
     arrived = lax.all_to_all(msg, "y", 0, 0, tiled=True)
-    psi = lax.all_gather(arrived[:, :16], "z")
-    psi = lax.all_gather(psi, "c")
+    both = lax.all_gather(arrived, "c")
     block = call(
         product_kernel,
-        shape((48, 128), F32),
-        psi, arrived,
-        scratch=[pltpu.VMEM((192 * 16, 128), F32), pltpu.VMEM((8 * 32, 128), F32)],
-    )
-    block = lax.all_gather(block, "x").sum(axis=0)
-    block = lax.all_gather(block, "y").sum(axis=0)
-    blocks = lax.all_gather(lax.all_gather(block, "z"), "c")
+        shape((4, 48, 128), F32),
+        both, arrived,
+        scratch=[pltpu.VMEM((2304, 128), F32), pltpu.VMEM((1152, 128), F32), pltpu.VMEM((10, 192, 128), F32)],
+    )
+    block = lax.all_to_all(block, "x", 0, 0, tiled=True).sum(axis=0)
+    block = lax.all_to_all(jnp.broadcast_to(block, (8, 48, 128)), "y", 0, 0, tiled=True).sum(axis=0)
+    block = lax.all_to_all(jnp.broadcast_to(block, (12, 48, 128)), "z", 0, 0, tiled=True)
     correlation, reduced = call(
         last_kernel,
         [shape((2, 192, 192), F32), shape((2, 192, 192), F32)],
-        blocks,
+        lax.all_gather(block, "c"),
         scratch=[pltpu.VMEM((8, 192, 128), F32)],
     )
-    return applied_orbitals, correlation, reduced
+    return out.reshape(orbitals.shape), correlation, reduced
 
 
 def solution(mesh):

time: 137 us -> 111 us (0.81)
  blocking collectives: 112 us -> 77.7 us
  starting transfers between devices: 8.05 us -> 15.8 us
    all_gather x6 -> x2, blocking collectives: 100 us -> 12.5 us  [the longest x1 6.95 us: body(): lax.all_gather(block, 'c')]
    all_to_all x0 -> x4, blocking collectives: none -> 53 us  [the longest x1 17 us: body(): lax.all_to_all(jnp.broadcast_to(block, (12, 48, 128)), 'z', 0, 0, tiled=T...]
    all_to_all x1, starting transfers between devices: 8.05 us -> 15.8 us  [body(): psi = lax.all_to_all(zmsg, 'z', 0, 0, tiled=True)]
    unnamed x15 -> x18, local copies, waits for them, and re-layouts: 2.35 us -> 3.6 us
where the time goes in v2:
time: 111 us
  blocking collectives  77.7 us (70%)
  starting transfers between devices  15.8 us (14%)
  Pallas kernels  6.52 us (6%)
  waiting for transfers between devices  6.16 us (6%)
  local copies, waits for them, and re-layouts  3.91 us (4%)
    all_to_all x1, blocking collectives, body(): lax.all_to_all(jnp.broadcast_to(block, (12, 48, 128)), 'z', 0, 0, tiled=T...  17 us
    all_to_all x1, blocking collectives, body(): arrived = lax.all_to_all(msg, 'y', 0, 0, tiled=True)  16.4 us
    all_to_all x1, starting transfers between devices, body(): psi = lax.all_to_all(zmsg, 'z', 0, 0, tiled=True)  15.8 us
    all_gather x1, blocking collectives, body(): everyone = lax.all_gather(packed, 'x')  12.2 us
    all_to_all x1, blocking collectives, body(): lax.all_to_all(jnp.broadcast_to(block, (8, 48, 128)), 'y', 0, 0, tiled=True)  11.1 us
    all_to_all x1, blocking collectives, body(): block = lax.all_to_all(block, 'x', 0, 0, tiled=True).sum(axis=0)  8.46 us
    all_gather x1, blocking collectives, body(): lax.all_gather(block, 'c')  6.95 us
    pallas_call x4, Pallas kernels, call(): pl.pallas_call(kernel, out_shape=outs, scratch_shapes=list(scratch), comp...  6.52 us
  transfers between devices with their start and end apart: 1, of which 1 were waited for; matrix products, arithmetic and copies ran while one was open for 0% of the time, Pallas kernels for 0%

profile of v2, /device:TPU:1, one launch (start us, length us, event | category | flops | bytes accessed | tf_op | source)
XLA Modules:
  0.0 110.9 jit_solution(12097937784115928195)
XLA Ops:
  0.6 0.0 copy-start.3
  0.6 1.0 copy-done.3
  1.7 0.0 copy-start.4
  1.7 0.9 copy-done.4
  2.6 0.0 copy-start.6
  2.6 0.9 copy-done.6
  3.5 0.0 copy-start.7
  3.5 0.7 copy-done.7
  4.2 0.0 copy-start.8
  4.2 2.3 %shard_map.103 = (bf16[12,8,16,128]{3,2,1,0:T(8,128)(2,1)}, bf16[608,128]{1,0:T(8,128)(2,1)S(1)}) custom-call(s32[160,128]{1,0:T(8,128)S(1)} %copy-done.4, bf16[2,40,128]{2,1,0:T(8,128)(2,1)S(1)} %bitcast.10, f32[120,480]{1,0:T(8,128)S(1)} %copy-done.6, bf16[2,480,256]{2,1,0:T(8,128)(2,1)S(1)} %copy-done.3), custom_call_target="tpu_custom_call" | custom-call | tf_op jit(solution)/shard_map/pallas_call | solution.py:206
  6.6 0.0 copy-start.1
  6.6 15.8 %all-to-all-start = ((bf16[12,8,16,128]{3,2,1,0:T(8,128)(2,1)}), bf16[12,8,16,128]{3,2,1,0:T(8,128)(2,1)S(1)}, u32[]{:S(2)}, u32[]{:S(2)}) async-start(bf16[12,8,16,128]{3,2,1,0:T(8,128)(2,1)} %get-tuple-element.10), calls=%async_computation | async-start | bytes 786432 | tf_op jit(solution)/shard_map/all_to_all | solution.py:229
  22.4 0.0 copy-start
  22.4 0.0 copy-done.8
  22.4 0.1 reshape.22
  22.5 0.1 reshape.23.slot_row_ref
  22.6 0.1 reshape.29.slot_col_ref
  22.7 12.2 %all-gather = bf16[2432,128]{1,0:T(8,128)(2,1)S(1)} all-gather(bf16[608,128]{1,0:T(8,128)(2,1)S(1)} %get-tuple-element.9), channel_id=2, replica_groups=mesh['y'=8,'z'=12,'c'=2,'x'=4] {'x'}, dimensions={0}, use_global_device_ids=true | all-gather | bytes 778240 | tf_op jit(solution)/shard_map/all_gather | solution.py:230
  34.9 6.2 %all-to-all-done.psi_ref = bf16[12,8,16,128]{3,2,1,0:T(8,128)(2,1)S(1)} async-done(((bf16[12,8,16,128]{3,2,1,0:T(8,128)(2,1)}), bf16[12,8,16,128]{3,2,1,0:T(8,128)(2,1)S(1)}, u32[]{:S(2)}, u32[]{:S(2)}) %all-to-all-start) | async-done | bytes 393248 | tf_op jit(solution)/shard_map/all_to_all | solution.py:229
  41.1 0.0 copy-done.1
  41.1 0.0 copy-done.2
  41.1 0.0 copy-done
  41.1 0.0 copy-done.5
  41.1 2.6 %shard_map.104 = (bf16[8,144,128]{2,1,0:T(8,128)(2,1)S(1)}, bf16[2,40,128]{2,1,0:T(8,128)(2,1)}) custom-call(bf16[4,608,128]{2,1,0:T(8,128)(2,1)S(1)} %bitcast.7, bf16[12,8,16,128]{3,2,1,0:T(8,128)(2,1)S(1)} %all-to-all-done.psi_ref, s32[160,128]{1,0:T(8,128)S(1)} %copy-done.5, s32[1,256]{1,0:T(1,128)S(1)} %reshape.23.slot_row_ref, ...), custom_call_target="tpu_custom_call" | custom-call | tf_op jit(solution)/shard_map/pallas_call | solution.py:206
  43.7 16.4 %all_to_all.25.own_ref = bf16[8,144,128]{2,1,0:T(8,128)(2,1)S(1)} all-to-all(bf16[8,144,128]{2,1,0:T(8,128)(2,1)S(1)} %get-tuple-element.12), channel_id=1, replica_groups=mesh['y'=8,'z'=12,'c'=2,'x'=4] {'y'}, dimensions={0} | all-to-all | bytes 589824 | tf_op jit(solution)/shard_map/all_to_all | solution.py:237
  60.1 5.5 %all-gather.1 = bf16[16,144,128]{2,1,0:T(8,128)(2,1)S(1)} all-gather(bf16[8,144,128]{2,1,0:T(8,128)(2,1)S(1)} %all_to_all.25.own_ref), channel_id=3, replica_groups=mesh['y'=8,'z'=12,'c'=2,'x'=4] {'c'}, dimensions={0}, use_global_device_ids=true | all-gather | bytes 884736 | tf_op jit(solution)/shard_map/all_gather | solution.py:238
  65.6 0.5 shard_map.105
  66.1 8.5 %all_to_all.26 = f32[4,48,128]{2,1,0:T(8,128)S(1)} all-to-all(f32[4,48,128]{2,1,0:T(8,128)S(1)} %shard_map.105), channel_id=1, replica_groups=mesh['y'=8,'z'=12,'c'=2,'x'=4] {'x'}, dimensions={0} | all-to-all | bytes 196608 | tf_op jit(solution)/shard_map/all_to_all | solution.py:245
  74.6 11.1 %all_to_all.27 = f32[8,48,128]{2,1,0:T(8,128)S(1)} all-to-all(f32[8,48,128]{2,1,0:T(8,128)S(1)} %broadcast_in_dim.6), channel_id=1, replica_groups=mesh['y'=8,'z'=12,'c'=2,'x'=4] {'y'}, dimensions={0} | all-to-all | bytes 393216 | tf_op jit(solution)/shard_map/all_to_all | solution.py:246
  85.8 17.0 %all_to_all.28 = f32[12,48,128]{2,1,0:T(8,128)S(1)} all-to-all(f32[12,48,128]{2,1,0:T(8,128)S(1)} %broadcast_in_dim.7), channel_id=1, replica_groups=mesh['y'=8,'z'=12,'c'=2,'x'=4] {'z'}, dimensions={0} | all-to-all | bytes 589824 | tf_op jit(solution)/shard_map/all_to_all | solution.py:247
  102.8 6.9 %all-gather.2 = f32[24,48,128]{2,1,0:T(8,128)S(1)} all-gather(f32[12,48,128]{2,1,0:T(8,128)S(1)} %all_to_all.28), channel_id=4, replica_groups=mesh['y'=8,'z'=12,'c'=2,'x'=4] {'c'}, dimensions={0}, use_global_device_ids=true | all-gather | bytes 884736 | tf_op jit(solution)/shard_map/all_gather | solution.py:251
  109.7 1.2 %shard_map.106 = (f32[2,192,192]{2,1,0:T(8,128)}, f32[2,192,192]{2,1,0:T(8,128)}) custom-call(f32[2,12,48,128]{3,2,1,0:T(8,128)S(1)} %bitcast.8), custom_call_target="tpu_custom_call" | custom-call | tf_op jit(solution)/shard_map/pallas_call | solution.py:206
  (8 shorter events, 0.1 us)
Async XLA Ops:
  0.6 1.0 copy-start.3
  1.7 0.9 copy-start.4
  2.6 0.9 copy-start.6
  3.5 0.7 copy-start.7
  4.2 18.2 %copy-start.8 = (s32[160]{0:T(256)S(1)}, s32[160]{0:T(256)}, u32[]{:S(2)}) copy-start(s32[160]{0:T(256)} %param.10) | copy-start | bytes 1924
  6.6 34.5 %copy-start.1 = (bf16[2,512,256]{2,1,0:T(8,128)(2,1)S(1)}, bf16[2,512,256]{2,1,0:T(8,128)(2,1)}, u32[]{:S(2)}) copy-start(bf16[2,512,256]{2,1,0:T(8,128)(2,1)} %constant.24.clone.wx_ref) | copy-start | bytes 1572868
  6.6 34.5 %copy-start.2 = (bf16[2,256,512]{2,1,0:T(8,128)(2,1)S(1)}, bf16[2,256,512]{2,1,0:T(8,128)(2,1)}, u32[]{:S(2)}) copy-start(bf16[2,256,512]{2,1,0:T(8,128)(2,1)} %constant.23.clone.wz_ref) | copy-start | bytes 1572868
  6.6 34.5 %all-to-all-start = ((bf16[12,8,16,128]{3,2,1,0:T(8,128)(2,1)}), bf16[12,8,16,128]{3,2,1,0:T(8,128)(2,1)S(1)}, u32[]{:S(2)}, u32[]{:S(2)}) async-start(bf16[12,8,16,128]{3,2,1,0:T(8,128)(2,1)} %get-tuple-element.10), calls=%async_computation | async-start | bytes 786432 | tf_op jit(solution)/shard_map/all_to_all | solution.py:229
  22.4 18.7 %copy-start = (bf16[2,256,480]{2,1,0:T(8,128)(2,1)S(1)}, bf16[2,256,480]{2,1,0:T(8,128)(2,1)}, u32[]{:S(2)}) copy-start(bf16[2,256,480]{2,1,0:T(8,128)(2,1)} %constant.25.clone.bz_ref) | copy-start | bytes 1474564
  22.7 18.4 %copy-start.5 = (s32[160,128]{1,0:T(8,128)S(1)}, s32[160,128]{1,0:T(8,128)}, u32[]{:S(2)}) copy-start(s32[160,128]{1,0:T(8,128)} %ent_ref.3) | copy-start | bytes 245764

commit v3 on v2

v3 whole, which is shorter than its diff:
```python
import functools

import jax
import jax.numpy as jnp
import numpy as np
from jax import lax
from jax.experimental import pallas as pl
from jax.experimental.pallas import tpu as pltpu
from jax.sharding import Mesh
from jax.sharding import PartitionSpec as P

BAND = ("y", "z", "c")
M = 256
F32 = jnp.float32
BF16 = jnp.bfloat16


def hi_lo(table):
    hi = table.astype(np.float32).astype(jnp.bfloat16)
    lo = (table - hi.astype(np.float64)).astype(np.float32).astype(jnp.bfloat16)
    return np.stack([hi, lo])


def tables(points, radius):
    freq = np.arange(2 * radius) - radius + 1
    pos = np.arange(M)
    ang = 2.0 * np.pi * ((freq[:, None] * pos[None, :]) % M) / M
    cos, sin = np.cos(ang), np.sin(ang)
    wz = np.block([[cos, sin], [-sin, cos]])
    top = 2 * radius - 2
    q = np.arange(1, top + 1)
    shift = pos[:, None] / M - np.arange(points)[None, :] / points
    resample = np.ones((M, points))
    for k in q:
        resample += 2.0 * np.cos(2.0 * np.pi * k * shift)
    resample /= points
    return hi_lo(wz), hi_lo(wz.T), hi_lo(resample.T), hi_lo(resample)


def split(x):
    hi = x.astype(BF16)
    return hi, (x - hi.astype(F32)).astype(BF16)


def mm(a, b):
    return lax.dot_general(a, b, (((1,), (0,)), ((), ())), preferred_element_type=F32)


def mm_nt(a, b):
    return lax.dot_general(a, b, (((1,), (1,)), ((), ())), preferred_element_type=F32)


def first_kernel(ent_hbm, orb_hbm, pot_hbm, bx_hbm, zmsg_ref, packed_ref, ent_s, orb_s, pot_s, bx_s, sems):
    first = pl.multiple_of(lax.axis_index("x") * 40, 8)
    copies = [
        pltpu.make_async_copy(src, dst, sems.at[i])
        for i, (src, dst) in enumerate(
            [(ent_hbm.at[pl.ds(first, 40), :], ent_s), (orb_hbm, orb_s), (bx_hbm, bx_s), (pot_hbm, pot_s)]
        )
    ]
    for copy in copies:
        copy.start()
    copies[0].wait()
    copies[1].wait()
    ent_t = ent_s[...].T
    orb = orb_s[...].astype(F32)
    lane = lax.broadcasted_iota(jnp.int32, (128, 128), 1)
    sub = lax.broadcasted_iota(jnp.int32, (128, 128), 0)
    pieces = [[], []]
    for g in range(5):
        rows = []
        for r in range(8):
            s = 8 * g + r
            match = ent_t[:, s : s + 1] == lane
            rows.append(jnp.max(jnp.where(match, sub, -1), axis=0, keepdims=True))
        source = jnp.concatenate(rows, axis=0)
        index = jnp.maximum(source, 0)
        for c in range(2):
            moved = jnp.take_along_axis(orb[c, 8 * g : 8 * g + 8, :], index, axis=1)
            pieces[c].append(jnp.where(source >= 0, moved, 0.0))
    spread = jnp.concatenate(pieces[0] + pieces[1], axis=0).astype(BF16)
    for z in range(12):
        zmsg_ref[z] = spread
    packed_ref[0:80, :] = spread
    copies[2].wait()
    copies[3].wait()
    v_hi, v_lo = split(pot_s[...])
    vx = mm(v_hi, bx_s[0]) + mm(v_lo, bx_s[0]) + mm(v_hi, bx_s[1])
    vx = jnp.concatenate([vx[:, :128], vx[:, 128:]], axis=0)
    hi, lo = split(vx)
    packed_ref[80:320, :] = hi
    packed_ref[320:560, :] = lo


def main_kernel(all_ref, ent_ref, slot_row_ref, slot_col_ref, wz_ref, wx_ref, bz_ref, h_ref, out_ref):
    d = lax.axis_index("x")
    first = pl.multiple_of(d * 40, 8)

    def rows_of_all(start, count):
        return jnp.concatenate([all_ref[d, start : start + count, :].astype(F32) for d in range(4)], axis=0)

    def gathered_v(start):
        halves = [rows_of_all(start, 120), rows_of_all(start + 120, 120)]
        return jnp.concatenate(halves, axis=1).astype(BF16)

    v_hi = gathered_v(80)
    v_lo = gathered_v(320)
    pot = mm(bz_ref[0], v_hi) + mm(bz_ref[1], v_hi) + mm(bz_ref[0], v_lo)
    pot = pot.T

    place = (
        lax.broadcasted_iota(jnp.int32, (128, 160), 0) == jnp.broadcast_to(slot_row_ref[...], (128, 160))
    ).astype(F32).astype(BF16)
    c_re = rows_of_all(0, 40).astype(BF16)
    c_im = rows_of_all(40, 40).astype(BF16)
    sticks = jnp.concatenate([mm(place, c_re), mm(place, c_im)], axis=0).astype(BF16)

    t = mm(wx_ref[0], sticks) + mm(wx_ref[1], sticks)
    t = jnp.concatenate([t[:M], t[M:]], axis=1)
    t_hi, t_lo = split(t)
    field = mm(t_hi, wz_ref[0]) + mm(t_lo, wz_ref[0]) + mm(t_hi, wz_ref[1])
    prod = jnp.concatenate([field[:, :M] * pot, field[:, M:] * pot], axis=1)
    p_hi, p_lo = split(prod)
    y = mm(p_hi, wx_ref[0]) + mm(p_lo, wx_ref[0]) + mm(p_hi, wx_ref[1])
    y = jnp.concatenate([y[:, :128], y[:, 128:]], axis=0)
    y_hi, y_lo = split(y)

    slot = slot_col_ref[pl.ds(first, 40), :]
    pick = (lax.broadcasted_iota(jnp.int32, (40, 128), 1) == slot).astype(F32)
    none = jnp.zeros((40, 128), F32)
    pick = jnp.concatenate(
        [jnp.concatenate([pick, none], axis=1), jnp.concatenate([none, pick], axis=1)], axis=0
    ).astype(BF16)
    w_hi = mm(pick, wz_ref[0]).astype(BF16)
    w_lo = mm(pick, wz_ref[1]).astype(BF16)
    applied = (mm(w_hi, y_hi) + mm(w_hi, y_lo) + mm(w_lo, y_hi)) * (1.0 / (M * M))

    gx = slot - 63
    gz = lax.broadcasted_iota(jnp.int32, (40, 128), 1) - 63
    square = gx * gx + gz * gz
    inside = (square < 64 * 64) & (slot >= 0)
    kinetic = square.astype(F32) * (1.0 / 4096.0)
    own = all_ref[d, 0:80, :].astype(F32)
    ent = ent_ref[pl.ds(first, 40), :]
    index = jnp.maximum(ent, 0)
    for c in range(2):
        value = kinetic * own[40 * c : 40 * c + 40] + applied[40 * c : 40 * c + 40]
        h = jnp.where(inside, value, 0.0).astype(BF16).astype(F32)
        h_ref[40 * c : 40 * c + 40, :] = h
        moved = [jnp.take_along_axis(h[8 * g : 8 * g + 8], index[8 * g : 8 * g + 8], axis=1) for g in range(5)]
        out_ref[c] = jnp.where(ent >= 0, jnp.concatenate(moved, axis=0), 0.0).astype(BF16)


def message_kernel(psi_ref, h_ref, msg_ref, psi_s):
    for z in range(12):
        psi_s[80 * z : 80 * z + 80, :] = psi_ref[z].astype(F32)
    for y in range(8):
        rows = [psi_s[pl.ds(y, 120, stride=8), :], h_ref[pl.ds(y, 10, stride=8), :], jnp.zeros((14, 128), F32)]
        msg_ref[y] = jnp.concatenate(rows, axis=0).astype(BF16)


def product_kernel(both_ref, own_ref, block_ref, all_s, own_s, psi_s):
    for c in range(2):
        for y in range(8):
            at = (8 * c + y) * 144
            all_s[at : at + 144, :] = both_ref[c, y].astype(F32)
            for q in range(10):
                psi_s[q, pl.ds(24 * y + c, 12, stride=2), :] = all_s[pl.ds(at + q, 12, stride=10), :]
    for y in range(8):
        own_s[144 * y : 144 * y + 144, :] = own_ref[y].astype(F32)

    def entries(first):
        rows = [own_s[pl.ds(first + r, 8, stride=144), :] for r in range(5)]
        return jnp.concatenate(rows, axis=1)

    z = lax.axis_index("z") * 10
    m_re, m_im = entries(z), entries(z + 5)
    a_re, a_im = entries(120), entries(125)
    left_re = jnp.concatenate([m_re, m_im, a_re, a_im], axis=0).astype(BF16)
    left_im = jnp.concatenate([m_im, -m_re, a_im, -a_re], axis=0).astype(BF16)
    p_re = jnp.concatenate([psi_s[r] for r in range(5)], axis=1).astype(BF16)
    p_im = jnp.concatenate([psi_s[5 + r] for r in range(5)], axis=1).astype(BF16)
    block = (mm_nt(left_re, p_re) + mm_nt(left_im, p_im)) * (1.0 / 16384.0)
    for x in range(4):
        block_ref[x, 0:32, :] = block[:, :128]
        block_ref[x, 32:48, :] = jnp.concatenate([block[:16, 128:], block[16:, 128:]], axis=1)


def last_kernel(all_ref, s_ref, h_ref, t_s):
    for c in range(2):
        for z in range(12):
            tail = all_ref[c, z, 32:48, :]
            for m in range(4):
                rows = pl.ds(z * 2 + c, 8, stride=24)
                t_s[2 * m, rows, :] = all_ref[c, z, 8 * m : 8 * m + 8, :]
                half = tail[8 * (m % 2) : 8 * (m % 2) + 8]
                if m >= 2:
                    half = jnp.concatenate([half[:, 64:], half[:, :64]], axis=1)
                t_s[2 * m + 1, rows, :] = half
    for m in range(4):
        ref = s_ref if m < 2 else h_ref
        ref[m % 2, 0:128, :] = t_s[2 * m].T
        ref[m % 2, 128:192, :] = t_s[2 * m + 1].T[:64]


def call(kernel, outs, *args, scratch=(), hbm=False):
    space = {"in_specs": [pl.BlockSpec(memory_space=pltpu.HBM)] * len(args)} if hbm else {}
    if hbm:
        args = [pltpu.with_memory_space_constraint(a, pltpu.HBM) for a in args]
    return pl.pallas_call(
        kernel,
        out_shape=outs,
        scratch_shapes=list(scratch),
        compiler_params=pltpu.CompilerParams(vmem_limit_bytes=48 * 1024 * 1024),
        **space,
    )(*args)


def shape(dims, dtype):
    return jax.ShapeDtypeStruct(dims, dtype)


def body(orbitals, potential, slot_sticks, stick_entries):
    wz, wx, bx, bz = tables(potential.shape[1], 64)
    zmsg, packed = call(
        first_kernel,
        [shape((12, 80, 128), BF16), shape((560, 128), BF16)],
        stick_entries, orbitals.reshape(2, 40, 128), potential, bx,
        scratch=[
            pltpu.VMEM((40, 128), jnp.int32),
            pltpu.VMEM((2, 40, 128), BF16),
            pltpu.VMEM((120, 480), F32),
            pltpu.VMEM((2, 480, 256), BF16),
            pltpu.SemaphoreType.DMA((4,)),
        ],
        hbm=True,
    )
    psi = lax.all_to_all(zmsg, "z", 0, 0, tiled=True)
    everyone = lax.all_gather(packed, "x")
    h, out = call(
        main_kernel,
        [shape((80, 128), F32), shape((2, 40, 128), BF16)],
        everyone, stick_entries, slot_sticks.reshape(1, 160), slot_sticks.reshape(160, 1), wz, wx, bz,
    )
    msg = call(message_kernel, shape((8, 144, 128), BF16), psi, h, scratch=[pltpu.VMEM((960, 128), F32)])
    arrived = lax.all_to_all(msg, "y", 0, 0, tiled=True)
    both = lax.all_gather(arrived, "c")
    block = call(
        product_kernel,
        shape((4, 48, 128), F32),
        both, arrived,
        scratch=[pltpu.VMEM((2304, 128), F32), pltpu.VMEM((1152, 128), F32), pltpu.VMEM((10, 192, 128), F32)],
    )
    block = lax.all_to_all(block, "x", 0, 0, tiled=True).sum(axis=0)
    block = lax.all_to_all(jnp.broadcast_to(block, (8, 48, 128)), "y", 0, 0, tiled=True).sum(axis=0)
    block = lax.all_to_all(jnp.broadcast_to(block, (12, 48, 128)), "z", 0, 0, tiled=True)
    correlation, reduced = call(
        last_kernel,
        [shape((2, 192, 192), F32), shape((2, 192, 192), F32)],
        lax.all_gather(block, "c"),
        scratch=[pltpu.VMEM((8, 192, 128), F32)],
    )
    return out.reshape(orbitals.shape), correlation, reduced


def solution(mesh):
    finer = Mesh(mesh.devices.reshape(8, 12, 2, mesh.shape["ga"]), ("y", "z", "c", "x"))
    return jax.shard_map(
        body,
        mesh=finer,
        in_specs=(P(None, BAND, "x", None), P("x", None), P(), P()),
        out_specs=(P(None, BAND, "x", None), P(), P()),
        check_vma=False,
    )
```

time: 111 us -> 106 us (0.955)
  waiting for transfers between devices: 6.16 us -> 0.01 us
  blocking collectives: 77.7 us -> 82.2 us
  local copies, waits for them, and re-layouts: 3.91 us -> 0.17 us
    all_to_all x1, waiting for transfers between devices: 6.16 us -> 0.01 us  [body(): psi = lax.all_to_all(zmsg, 'z', 0, 0, tiled=True)]
    all_to_all x1, blocking collectives: 17 us -> 21.8 us  [body(): lax.all_to_all(jnp.broadcast_to(block, (12, 48, 128)), 'z', 0, 0, tiled=T...]
    unnamed x18 -> x10, local copies, waits for them, and re-layouts: 3.6 us -> 0.03 us
    pallas_call x4 -> x5, Pallas kernels: 6.52 us -> 7.03 us  [call(): pl.pallas_call(kernel, out_shape=outs, scratch_shapes=list(scratch), comp...]
  transfers between devices with their start and end apart: 1 -> 1, of which waited for: 1 -> 0; matrix products, arithmetic and copies ran while one was open for 0% -> 0% of each run, Pallas kernels for 0% -> 2%
where the time goes in v3:
time: 106 us
  blocking collectives  82.2 us (78%)
  starting transfers between devices  15.8 us (15%)
  Pallas kernels  7.03 us (7%)
    all_to_all x1, blocking collectives, body(): lax.all_to_all(jnp.broadcast_to(block, (12, 48, 128)), 'z', 0, 0, tiled=T...  21.8 us
    all_to_all x1, blocking collectives, body(): arrived = lax.all_to_all(msg, 'y', 0, 0, tiled=True)  16.4 us
    all_to_all x1, starting transfers between devices, body(): psi = lax.all_to_all(zmsg, 'z', 0, 0, tiled=True)  15.8 us
    all_gather x1, blocking collectives, body(): everyone = lax.all_gather(packed, 'x')  12 us
    all_to_all x1, blocking collectives, body(): lax.all_to_all(jnp.broadcast_to(block, (8, 48, 128)), 'y', 0, 0, tiled=True)  11.1 us
    all_to_all x1, blocking collectives, body(): block = lax.all_to_all(block, 'x', 0, 0, tiled=True).sum(axis=0)  8.37 us
    pallas_call x5, Pallas kernels, call(): pl.pallas_call(kernel, out_shape=outs, scratch_shapes=list(scratch), comp...  7.03 us
    all_gather x1, blocking collectives, body(): lax.all_gather(block, 'c')  6.95 us
  transfers between devices with their start and end apart: 1, of which 0 were waited for; matrix products, arithmetic and copies ran while one was open for 0% of the time, Pallas kernels for 2%

profile of v3, /device:TPU:1, one launch (start us, length us, event | category | flops | bytes accessed | tf_op | source)
XLA Modules:
  0.0 106.0 jit_solution(278783055358391889)
XLA Ops:
  0.6 0.0 copy-start.4
  0.6 0.0 copy-start.2
  0.7 2.9 %shard_map.103 = (bf16[12,80,128]{2,1,0:T(8,128)(2,1)}, bf16[560,128]{1,0:T(8,128)(2,1)S(1)}) custom-call(s32[160,128]{1,0:T(8,128)} %ent_ref.1, bf16[2,40,128]{2,1,0:T(8,128)(2,1)} %bitcast.14, f32[120,480]{1,0:T(8,128)} %pot_hbm.1, bf16[2,480,256]{2,1,0:T(8,128)(2,1)} %constant.10.clone.bx_hbm), custom_call_target="tpu_custom_call" | custom-call | tf_op jit(solution)/shard_map/pallas_call | solution.py:210
  3.5 0.0 copy-start.1
  3.5 15.8 %all-to-all-start = ((bf16[12,80,128]{2,1,0:T(8,128)(2,1)}), bf16[12,80,128]{2,1,0:T(8,128)(2,1)S(1)}, u32[]{:S(2)}, u32[]{:S(2)}) async-start(bf16[12,80,128]{2,1,0:T(8,128)(2,1)} %get-tuple-element.11), calls=%async_computation | async-start | bytes 491520 | tf_op jit(solution)/shard_map/all_to_all | solution.py:238
  19.4 0.0 copy-start
  19.4 0.0 copy-done.4
  19.4 0.1 copy.16.slot_col_ref
  19.5 0.0 copy-start.3
  19.5 12.0 %all-gather = bf16[2240,128]{1,0:T(8,128)(2,1)S(1)} all-gather(bf16[560,128]{1,0:T(8,128)(2,1)S(1)} %get-tuple-element.9), channel_id=2, replica_groups=mesh['y'=8,'z'=12,'c'=2,'x'=4] {'x'}, dimensions={0}, use_global_device_ids=true | all-gather | bytes 716800 | tf_op jit(solution)/shard_map/all_gather | solution.py:239
  31.5 0.0 copy-done.2
  31.5 0.0 copy-done.1
  31.5 0.0 copy-done
  31.5 0.0 copy-done.3
  31.5 2.4 %shard_map.104 = (f32[80,128]{1,0:T(8,128)S(1)}, bf16[2,40,128]{2,1,0:T(8,128)(2,1)}) custom-call(bf16[4,560,128]{2,1,0:T(8,128)(2,1)S(1)} %bitcast.11, s32[160,128]{1,0:T(8,128)S(1)} %copy-done.3, s32[1,160]{1,0:T(1,128)S(1)} %bitcast.13, s32[160,1]{1,0:T(8,128)S(1)} %copy.16.slot_col_ref, bf16[2,256,512]{2,1,0:T(8,128)(2,1)S(1)} %copy-done.2, ...), custom_call_target="tpu_custom_call" | custom-call | tf_op jit(solution)/shard_map/pallas_call | solution.py:210
  33.9 0.0 all-to-all-done.psi_ref
  33.9 0.1 shard_map.105
  34.0 16.4 %all_to_all.25.own_ref = bf16[8,144,128]{2,1,0:T(8,128)(2,1)S(1)} all-to-all(bf16[8,144,128]{2,1,0:T(8,128)(2,1)S(1)} %shard_map.105), channel_id=1, replica_groups=mesh['y'=8,'z'=12,'c'=2,'x'=4] {'y'}, dimensions={0} | all-to-all | bytes 589824 | tf_op jit(solution)/shard_map/all_to_all | solution.py:246
  50.4 5.6 %all-gather.1 = bf16[16,144,128]{2,1,0:T(8,128)(2,1)S(1)} all-gather(bf16[8,144,128]{2,1,0:T(8,128)(2,1)S(1)} %all_to_all.25.own_ref), channel_id=3, replica_groups=mesh['y'=8,'z'=12,'c'=2,'x'=4] {'c'}, dimensions={0}, use_global_device_ids=true | all-gather | bytes 884736 | tf_op jit(solution)/shard_map/all_gather | solution.py:247
  56.0 0.5 shard_map.106
  56.5 8.4 %all_to_all.26 = f32[4,48,128]{2,1,0:T(8,128)S(1)} all-to-all(f32[4,48,128]{2,1,0:T(8,128)S(1)} %shard_map.106), channel_id=1, replica_groups=mesh['y'=8,'z'=12,'c'=2,'x'=4] {'x'}, dimensions={0} | all-to-all | bytes 196608 | tf_op jit(solution)/shard_map/all_to_all | solution.py:254
  64.9 11.1 %all_to_all.27 = f32[8,48,128]{2,1,0:T(8,128)S(1)} all-to-all(f32[8,48,128]{2,1,0:T(8,128)S(1)} %broadcast_in_dim.6), channel_id=1, replica_groups=mesh['y'=8,'z'=12,'c'=2,'x'=4] {'y'}, dimensions={0} | all-to-all | bytes 393216 | tf_op jit(solution)/shard_map/all_to_all | solution.py:255
  76.1 21.8 %all_to_all.28 = f32[12,48,128]{2,1,0:T(8,128)S(1)} all-to-all(f32[12,48,128]{2,1,0:T(8,128)S(1)} %broadcast_in_dim.7), channel_id=1, replica_groups=mesh['y'=8,'z'=12,'c'=2,'x'=4] {'z'}, dimensions={0} | all-to-all | bytes 589824 | tf_op jit(solution)/shard_map/all_to_all | solution.py:256
  97.9 6.9 %all-gather.2 = f32[24,48,128]{2,1,0:T(8,128)S(1)} all-gather(f32[12,48,128]{2,1,0:T(8,128)S(1)} %all_to_all.28), channel_id=4, replica_groups=mesh['y'=8,'z'=12,'c'=2,'x'=4] {'c'}, dimensions={0}, use_global_device_ids=true | all-gather | bytes 884736 | tf_op jit(solution)/shard_map/all_gather | solution.py:260
  104.9 1.2 %shard_map.107 = (f32[2,192,192]{2,1,0:T(8,128)}, f32[2,192,192]{2,1,0:T(8,128)}) custom-call(f32[2,12,48,128]{3,2,1,0:T(8,128)S(1)} %bitcast.9), custom_call_target="tpu_custom_call" | custom-call | tf_op jit(solution)/shard_map/pallas_call | solution.py:210
  (4 shorter events, 0.1 us)
Async XLA Ops:
  0.6 18.8 %copy-start.4 = (s32[160]{0:T(256)S(1)}, s32[160]{0:T(256)}, u32[]{:S(2)}) copy-start(s32[160]{0:T(256)} %param.10) | copy-start | bytes 1924
  0.6 30.9 %copy-start.2 = (bf16[2,256,512]{2,1,0:T(8,128)(2,1)S(1)}, bf16[2,256,512]{2,1,0:T(8,128)(2,1)}, u32[]{:S(2)}) copy-start(bf16[2,256,512]{2,1,0:T(8,128)(2,1)} %constant.11.clone.wz_ref) | copy-start | bytes 1572868
  3.5 28.0 %copy-start.1 = (bf16[2,512,256]{2,1,0:T(8,128)(2,1)S(1)}, bf16[2,512,256]{2,1,0:T(8,128)(2,1)}, u32[]{:S(2)}) copy-start(bf16[2,512,256]{2,1,0:T(8,128)(2,1)} %constant.12.clone.wx_ref) | copy-start | bytes 1572868
  3.5 30.4 %all-to-all-start = ((bf16[12,80,128]{2,1,0:T(8,128)(2,1)}), bf16[12,80,128]{2,1,0:T(8,128)(2,1)S(1)}, u32[]{:S(2)}, u32[]{:S(2)}) async-start(bf16[12,80,128]{2,1,0:T(8,128)(2,1)} %get-tuple-element.11), calls=%async_computation | async-start | bytes 491520 | tf_op jit(solution)/shard_map/all_to_all | solution.py:238
  19.4 12.1 %copy-start = (bf16[2,256,480]{2,1,0:T(8,128)(2,1)S(1)}, bf16[2,256,480]{2,1,0:T(8,128)(2,1)}, u32[]{:S(2)}) copy-start(bf16[2,256,480]{2,1,0:T(8,128)(2,1)} %constant.13.clone.bz_ref) | copy-start | bytes 1474564
  19.5 12.0 %copy-start.3 = (s32[160,128]{1,0:T(8,128)S(1)}, s32[160,128]{1,0:T(8,128)}, u32[]{:S(2)}) copy-start(s32[160,128]{1,0:T(8,128)} %ent_ref.1) | copy-start | bytes 245764

commit v4 on v3

--- a/solution.py
+++ b/solution.py
@@ -92,7 +92,7 @@
     packed_ref[320:560, :] = lo
 
 
-def main_kernel(all_ref, ent_ref, slot_row_ref, slot_col_ref, wz_ref, wx_ref, bz_ref, h_ref, out_ref):
+def main_kernel(all_ref, ent_ref, slot_row_ref, slot_col_ref, wz_ref, wx_ref, bz_ref, msg_ref, out_ref):
     d = lax.axis_index("x")
     first = pl.multiple_of(d * 40, 8)
 
@@ -143,60 +143,63 @@
     own = all_ref[d, 0:80, :].astype(F32)
     ent = ent_ref[pl.ds(first, 40), :]
     index = jnp.maximum(ent, 0)
+    message = [own]
     for c in range(2):
         value = kinetic * own[40 * c : 40 * c + 40] + applied[40 * c : 40 * c + 40]
         h = jnp.where(inside, value, 0.0).astype(BF16).astype(F32)
-        h_ref[40 * c : 40 * c + 40, :] = h
+        message.append(h)
         moved = [jnp.take_along_axis(h[8 * g : 8 * g + 8], index[8 * g : 8 * g + 8], axis=1) for g in range(5)]
         out_ref[c] = jnp.where(ent >= 0, jnp.concatenate(moved, axis=0), 0.0).astype(BF16)
-
-
-def message_kernel(psi_ref, h_ref, msg_ref, psi_s):
-    for z in range(12):
-        psi_s[80 * z : 80 * z + 80, :] = psi_ref[z].astype(F32)
+    message = jnp.concatenate(message, axis=0).astype(BF16)
     for y in range(8):
-        rows = [psi_s[pl.ds(y, 120, stride=8), :], h_ref[pl.ds(y, 10, stride=8), :], jnp.zeros((14, 128), F32)]
-        msg_ref[y] = jnp.concatenate(rows, axis=0).astype(BF16)
-
-
-def product_kernel(both_ref, own_ref, block_ref, all_s, own_s, psi_s):
+        msg_ref[y] = message
+
+
+def rows_kernel(psi_ref, p_ref, psi_s):
     for c in range(2):
-        for y in range(8):
-            at = (8 * c + y) * 144
-            all_s[at : at + 144, :] = both_ref[c, y].astype(F32)
-            for q in range(10):
-                psi_s[q, pl.ds(24 * y + c, 12, stride=2), :] = all_s[pl.ds(at + q, 12, stride=10), :]
+        for z in range(12):
+            at = (2 * z + c) * 80
+            psi_s[at : at + 80, :] = psi_ref[c, z].astype(F32)
+    pad = jnp.zeros((8, 128), F32)
+    for part in range(2):
+        for s in range(40):
+            block = jnp.concatenate([psi_s[pl.ds(40 * part + s, 24, stride=80), :], pad], axis=0)
+            p_ref[part, :, 128 * s : 128 * s + 128] = block.astype(BF16)
+
+
+def product_kernel(p_ref, own_ref, block_ref, own_s):
     for y in range(8):
-        own_s[144 * y : 144 * y + 144, :] = own_ref[y].astype(F32)
+        own_s[160 * y : 160 * y + 160, :] = own_ref[y].astype(F32)
 
     def entries(first):
-        rows = [own_s[pl.ds(first + r, 8, stride=144), :] for r in range(5)]
+        rows = [own_s[pl.ds(first + s, 8, stride=160), :] for s in range(40)]
         return jnp.concatenate(rows, axis=1)
 
-    z = lax.axis_index("z") * 10
-    m_re, m_im = entries(z), entries(z + 5)
-    a_re, a_im = entries(120), entries(125)
+    m_re, m_im, a_re, a_im = [entries(40 * q) for q in range(4)]
     left_re = jnp.concatenate([m_re, m_im, a_re, a_im], axis=0).astype(BF16)
     left_im = jnp.concatenate([m_im, -m_re, a_im, -a_re], axis=0).astype(BF16)
-    p_re = jnp.concatenate([psi_s[r] for r in range(5)], axis=1).astype(BF16)
-    p_im = jnp.concatenate([psi_s[5 + r] for r in range(5)], axis=1).astype(BF16)
-    block = (mm_nt(left_re, p_re) + mm_nt(left_im, p_im)) * (1.0 / 16384.0)
+    block = (mm_nt(left_re, p_ref[0]) + mm_nt(left_im, p_ref[1])) * (1.0 / 16384.0)
+    row = [block[8 * m : 8 * m + 8, :24] for m in range(4)] + [jnp.zeros((8, 32), F32)]
+    row = jnp.concatenate(row, axis=1)
     for x in range(4):
-        block_ref[x, 0:32, :] = block[:, :128]
-        block_ref[x, 32:48, :] = jnp.concatenate([block[:16, 128:], block[16:, 128:]], axis=1)
+        block_ref[x] = row
+
+
+def pack_kernel(blocks_ref, packed_ref):
+    row = jnp.concatenate([blocks_ref[z][:, :96] for z in range(12)], axis=1)
+    for y in range(8):
+        packed_ref[y] = row
 
 
 def last_kernel(all_ref, s_ref, h_ref, t_s):
     for c in range(2):
         for z in range(12):
-            tail = all_ref[c, z, 32:48, :]
             for m in range(4):
+                at = 96 * z + 24 * m
+                row = jnp.concatenate([all_ref[c, y, :, at : at + 24] for y in range(8)], axis=1)
                 rows = pl.ds(z * 2 + c, 8, stride=24)
-                t_s[2 * m, rows, :] = all_ref[c, z, 8 * m : 8 * m + 8, :]
-                half = tail[8 * (m % 2) : 8 * (m % 2) + 8]
-                if m >= 2:
-                    half = jnp.concatenate([half[:, 64:], half[:, :64]], axis=1)
-                t_s[2 * m + 1, rows, :] = half
+                t_s[2 * m, rows, :] = row[:, :128]
+                t_s[2 * m + 1, rows, 0:64] = row[:, 128:]
     for m in range(4):
         ref = s_ref if m < 2 else h_ref
         ref[m % 2, 0:128, :] = t_s[2 * m].T
@@ -237,27 +240,24 @@
     )
     psi = lax.all_to_all(zmsg, "z", 0, 0, tiled=True)
     everyone = lax.all_gather(packed, "x")
-    h, out = call(
+    msg, out = call(
         main_kernel,
-        [shape((80, 128), F32), shape((2, 40, 128), BF16)],
+        [shape((8, 160, 128), BF16), shape((2, 40, 128), BF16)],
         everyone, stick_entries, slot_sticks.reshape(1, 160), slot_sticks.reshape(160, 1), wz, wx, bz,
     )
-    msg = call(message_kernel, shape((8, 144, 128), BF16), psi, h, scratch=[pltpu.VMEM((960, 128), F32)])
-    arrived = lax.all_to_all(msg, "y", 0, 0, tiled=True)
-    both = lax.all_gather(arrived, "c")
-    block = call(
-        product_kernel,
-        shape((4, 48, 128), F32),
-        both, arrived,
-        scratch=[pltpu.VMEM((2304, 128), F32), pltpu.VMEM((1152, 128), F32), pltpu.VMEM((10, 192, 128), F32)],
-    )
+    own = lax.all_to_all(msg, "y", 0, 0, tiled=True)
+    rows = call(
+        rows_kernel, shape((2, 32, 5120), BF16), lax.all_gather(psi, "c"), scratch=[pltpu.VMEM((1920, 128), F32)]
+    )
+    block = call(product_kernel, shape((4, 8, 128), F32), rows, own, scratch=[pltpu.VMEM((1280, 128), F32)])
     block = lax.all_to_all(block, "x", 0, 0, tiled=True).sum(axis=0)
-    block = lax.all_to_all(jnp.broadcast_to(block, (8, 48, 128)), "y", 0, 0, tiled=True).sum(axis=0)
-    block = lax.all_to_all(jnp.broadcast_to(block, (12, 48, 128)), "z", 0, 0, tiled=True)
+    blocks = lax.all_to_all(jnp.broadcast_to(block, (12, 8, 128)), "z", 0, 0, tiled=True)
+    packed = call(pack_kernel, shape((8, 8, 1152), F32), blocks)
+    packed = lax.all_to_all(packed, "y", 0, 0, tiled=True)
     correlation, reduced = call(
         last_kernel,
         [shape((2, 192, 192), F32), shape((2, 192, 192), F32)],
-        lax.all_gather(block, "c"),
+        lax.all_gather(packed, "c"),
         scratch=[pltpu.VMEM((8, 192, 128), F32)],
     )
     return out.reshape(orbitals.shape), correlation, reduced

time: 106 us -> 102 us (0.962)
  blocking collectives: 82.2 us -> 64.8 us
  starting transfers between devices: 15.8 us -> 22.7 us
  waiting for transfers between devices: 0.01 us -> 5.33 us
  Pallas kernels: 7.03 us -> 8.32 us
    all_to_all x3 -> x2, blocking collectives: 49.3 us -> 31.3 us  [the longest x1 18.7 us: body(): lax.all_to_all(jnp.broadcast_to(block, (12, 8, 128)), 'z', 0, 0, tiled=True)]
    all_to_all x0 -> x1, starting transfers between devices: none -> 6.82 us  [body(): own = lax.all_to_all(msg, 'y', 0, 0, tiled=True)]
    all_to_all x0 -> x1, waiting for transfers between devices: none -> 5.33 us  [body(): own = lax.all_to_all(msg, 'y', 0, 0, tiled=True)]
    all_gather x2, blocking collectives: 12.5 us -> 14.7 us  [the longest x1 10.3 us: body(): lax.all_gather(packed, 'c')]
    all_to_all x1, blocking collectives: 8.37 us -> 6.77 us  [body(): block = lax.all_to_all(block, 'x', 0, 0, tiled=True).sum(axis=0)]
    pallas_call x5 -> x6, Pallas kernels: 7.03 us -> 8.32 us  [call(): pl.pallas_call(kernel, out_shape=outs, scratch_shapes=list(scratch), comp...]
  transfers between devices with their start and end apart: 1 -> 2, of which waited for: 0 -> 1; matrix products, arithmetic and copies ran while one was open for 0% -> 0% of each run, Pallas kernels for 2% -> 3%
where the time goes in v4:
time: 102 us
  blocking collectives  64.8 us (64%)
  starting transfers between devices  22.7 us (22%)
  Pallas kernels  8.32 us (8%)
  waiting for transfers between devices  5.33 us (5%)
    all_to_all x1, blocking collectives, body(): lax.all_to_all(jnp.broadcast_to(block, (12, 8, 128)), 'z', 0, 0, tiled=True)  18.7 us
    all_to_all x1, starting transfers between devices, body(): psi = lax.all_to_all(zmsg, 'z', 0, 0, tiled=True)  15.8 us
    all_to_all x1, blocking collectives, body(): packed = lax.all_to_all(packed, 'y', 0, 0, tiled=True)  12.7 us
    all_gather x1, blocking collectives, body(): everyone = lax.all_gather(packed, 'x')  12 us
    all_gather x1, blocking collectives, body(): lax.all_gather(packed, 'c')  10.3 us
    pallas_call x6, Pallas kernels, call(): pl.pallas_call(kernel, out_shape=outs, scratch_shapes=list(scratch), comp...  8.32 us
    all_to_all x1, starting transfers between devices, body(): own = lax.all_to_all(msg, 'y', 0, 0, tiled=True)  6.82 us
    all_to_all x1, blocking collectives, body(): block = lax.all_to_all(block, 'x', 0, 0, tiled=True).sum(axis=0)  6.77 us
  transfers between devices with their start and end apart: 2, of which 1 were waited for; matrix products, arithmetic and copies ran while one was open for 0% of the time, Pallas kernels for 3%

profile of v4, /device:TPU:1, one launch (start us, length us, event | category | flops | bytes accessed | tf_op | source)
XLA Modules:
  0.0 102.0 jit_solution(3112666898827174183)
XLA Ops:
  0.6 0.0 copy-start.4
  0.6 0.0 copy-start.2
  0.7 2.9 %shard_map.103 = (bf16[12,80,128]{2,1,0:T(8,128)(2,1)}, bf16[560,128]{1,0:T(8,128)(2,1)S(1)}) custom-call(s32[160,128]{1,0:T(8,128)} %ent_ref.1, bf16[2,40,128]{2,1,0:T(8,128)(2,1)} %bitcast.14, f32[120,480]{1,0:T(8,128)} %pot_hbm.1, bf16[2,480,256]{2,1,0:T(8,128)(2,1)} %constant.10.clone.bx_hbm), custom_call_target="tpu_custom_call" | custom-call | tf_op jit(solution)/shard_map/pallas_call | solution.py:213
  3.5 0.0 copy-start.1
  3.5 15.8 %all-to-all-start = ((bf16[12,80,128]{2,1,0:T(8,128)(2,1)}), bf16[12,80,128]{2,1,0:T(8,128)(2,1)S(1)}, u32[]{:S(2)}, u32[]{:S(2)}) async-start(bf16[12,80,128]{2,1,0:T(8,128)(2,1)} %get-tuple-element.11), calls=%async_computation | async-start | bytes 491520 | tf_op jit(solution)/shard_map/all_to_all | solution.py:241
  19.4 0.0 copy-start
  19.4 0.0 copy-done.4
  19.4 0.1 copy.14.slot_col_ref
  19.5 0.0 copy-start.3
  19.5 12.0 %all-gather = bf16[2240,128]{1,0:T(8,128)(2,1)S(1)} all-gather(bf16[560,128]{1,0:T(8,128)(2,1)S(1)} %get-tuple-element.9), channel_id=2, replica_groups=mesh['y'=8,'z'=12,'c'=2,'x'=4] {'x'}, dimensions={0}, use_global_device_ids=true | all-gather | bytes 716800 | tf_op jit(solution)/shard_map/all_gather | solution.py:242
  31.5 0.0 copy-done.2
  31.5 0.0 copy-done.1
  31.5 0.0 copy-done
  31.5 0.0 copy-done.3
  31.5 2.4 %shard_map.104 = (bf16[8,160,128]{2,1,0:T(8,128)(2,1)}, bf16[2,40,128]{2,1,0:T(8,128)(2,1)}) custom-call(bf16[4,560,128]{2,1,0:T(8,128)(2,1)S(1)} %bitcast.10, s32[160,128]{1,0:T(8,128)S(1)} %copy-done.3, s32[1,160]{1,0:T(1,128)S(1)} %bitcast.13, s32[160,1]{1,0:T(8,128)S(1)} %copy.14.slot_col_ref, bf16[2,256,512]{2,1,0:T(8,128)(2,1)S(1)} %copy-done, ...), custom_call_target="tpu_custom_call" | custom-call | tf_op jit(solution)/shard_map/pallas_call | solution.py:213
  33.9 0.0 all-to-all-done
  33.9 6.8 %all-to-all-start.1 = ((bf16[8,160,128]{2,1,0:T(8,128)(2,1)}), bf16[8,160,128]{2,1,0:T(8,128)(2,1)S(1)}, u32[]{:S(2)}, u32[]{:S(2)}) async-start(bf16[8,160,128]{2,1,0:T(8,128)(2,1)} %get-tuple-element.12), calls=%async_computation.1 | async-start | bytes 655360 | tf_op jit(solution)/shard_map/all_to_all | solution.py:248
  40.8 4.4 %all-gather.1 = bf16[24,80,128]{2,1,0:T(8,128)(2,1)S(1)} all-gather(bf16[12,80,128]{2,1,0:T(8,128)(2,1)S(1)} %all-to-all-done), channel_id=3, replica_groups=mesh['y'=8,'z'=12,'c'=2,'x'=4] {'c'}, dimensions={0}, use_global_device_ids=true | all-gather | bytes 737280 | tf_op jit(solution)/shard_map/all_gather | solution.py:250
  45.2 0.4 shard_map.105.p_ref
  45.6 5.3 %all-to-all-done.1.own_ref = bf16[8,160,128]{2,1,0:T(8,128)(2,1)S(1)} async-done(((bf16[8,160,128]{2,1,0:T(8,128)(2,1)}), bf16[8,160,128]{2,1,0:T(8,128)(2,1)S(1)}, u32[]{:S(2)}, u32[]{:S(2)}) %all-to-all-start.1) | async-done | bytes 327712 | tf_op jit(solution)/shard_map/all_to_all | solution.py:248
  50.9 0.6 shard_map.106
  51.5 6.8 %all_to_all.25 = f32[4,8,128]{2,1,0:T(8,128)S(1)} all-to-all(f32[4,8,128]{2,1,0:T(8,128)S(1)} %shard_map.106), channel_id=1, replica_groups=mesh['y'=8,'z'=12,'c'=2,'x'=4] {'x'}, dimensions={0} | all-to-all | bytes 32768 | tf_op jit(solution)/shard_map/all_to_all | solution.py:253
  58.3 18.7 %all_to_all.26.blocks_ref = f32[12,8,128]{2,1,0:T(8,128)S(1)} all-to-all(f32[12,8,128]{2,1,0:T(8,128)S(1)} %broadcast_in_dim.3), channel_id=1, replica_groups=mesh['y'=8,'z'=12,'c'=2,'x'=4] {'z'}, dimensions={0} | all-to-all | bytes 98304 | tf_op jit(solution)/shard_map/all_to_all | solution.py:254
  76.9 0.1 shard_map.107
  77.0 12.7 %all_to_all.27 = f32[8,8,1152]{2,1,0:T(8,128)S(1)} all-to-all(f32[8,8,1152]{2,1,0:T(8,128)S(1)} %shard_map.107), channel_id=1, replica_groups=mesh['y'=8,'z'=12,'c'=2,'x'=4] {'y'}, dimensions={0} | all-to-all | bytes 589824 | tf_op jit(solution)/shard_map/all_to_all | solution.py:256
  89.7 10.3 %all-gather.2 = f32[16,8,1152]{2,1,0:T(8,128)S(1)} all-gather(f32[8,8,1152]{2,1,0:T(8,128)S(1)} %all_to_all.27), channel_id=4, replica_groups=mesh['y'=8,'z'=12,'c'=2,'x'=4] {'c'}, dimensions={0}, use_global_device_ids=true | all-gather | bytes 884736 | tf_op jit(solution)/shard_map/all_gather | solution.py:260
  100.1 2.0 %shard_map.108 = (f32[2,192,192]{2,1,0:T(8,128)}, f32[2,192,192]{2,1,0:T(8,128)}) custom-call(f32[2,8,8,1152]{3,2,1,0:T(8,128)S(1)} %bitcast.9), custom_call_target="tpu_custom_call" | custom-call | tf_op jit(solution)/shard_map/pallas_call | solution.py:213
  (2 shorter events, 0.0 us)
Async XLA Ops:
  0.6 18.8 %copy-start.4 = (s32[160]{0:T(256)S(1)}, s32[160]{0:T(256)}, u32[]{:S(2)}) copy-start(s32[160]{0:T(256)} %param.10) | copy-start | bytes 1924
  0.6 30.9 %copy-start.2 = (bf16[2,256,480]{2,1,0:T(8,128)(2,1)S(1)}, bf16[2,256,480]{2,1,0:T(8,128)(2,1)}, u32[]{:S(2)}) copy-start(bf16[2,256,480]{2,1,0:T(8,128)(2,1)} %constant.13.clone.bz_ref) | copy-start | bytes 1474564
  3.5 28.0 %copy-start.1 = (bf16[2,512,256]{2,1,0:T(8,128)(2,1)S(1)}, bf16[2,512,256]{2,1,0:T(8,128)(2,1)}, u32[]{:S(2)}) copy-start(bf16[2,512,256]{2,1,0:T(8,128)(2,1)} %constant.12.clone.wx_ref) | copy-start | bytes 1572868
  3.5 30.4 %all-to-all-start = ((bf16[12,80,128]{2,1,0:T(8,128)(2,1)}), bf16[12,80,128]{2,1,0:T(8,128)(2,1)S(1)}, u32[]{:S(2)}, u32[]{:S(2)}) async-start(bf16[12,80,128]{2,1,0:T(8,128)(2,1)} %get-tuple-element.11), calls=%async_computation | async-start | bytes 491520 | tf_op jit(solution)/shard_map/all_to_all | solution.py:241
  19.4 12.1 %copy-start = (bf16[2,256,512]{2,1,0:T(8,128)(2,1)S(1)}, bf16[2,256,512]{2,1,0:T(8,128)(2,1)}, u32[]{:S(2)}) copy-start(bf16[2,256,512]{2,1,0:T(8,128)(2,1)} %constant.11.clone.wz_ref) | copy-start | bytes 1572868
  19.5 12.0 %copy-start.3 = (s32[160,128]{1,0:T(8,128)S(1)}, s32[160,128]{1,0:T(8,128)}, u32[]{:S(2)}) copy-start(s32[160,128]{1,0:T(8,128)} %ent_ref.1) | copy-start | bytes 245764
  33.9 16.9 %all-to-all-start.1 = ((bf16[8,160,128]{2,1,0:T(8,128)(2,1)}), bf16[8,160,128]{2,1,0:T(8,128)(2,1)S(1)}, u32[]{:S(2)}, u32[]{:S(2)}) async-start(bf16[8,160,128]{2,1,0:T(8,128)(2,1)} %get-tuple-element.12), calls=%async_computation.1 | async-start | bytes 655360 | tf_op jit(solution)/shard_map/all_to_all | solution.py:248

commit v5 on v4

--- a/solution.py
+++ b/solution.py
@@ -50,7 +50,7 @@
     return lax.dot_general(a, b, (((1,), (1,)), ((), ())), preferred_element_type=F32)
 
 
-def first_kernel(ent_hbm, orb_hbm, pot_hbm, bx_hbm, zmsg_ref, packed_ref, ent_s, orb_s, pot_s, bx_s, sems):
+def first_kernel(ent_hbm, orb_hbm, pot_hbm, bx_hbm, zmsg_hbm, packed_ref, ent_s, orb_s, pot_s, bx_s, sems):
     first = pl.multiple_of(lax.axis_index("x") * 40, 8)
     copies = [
         pltpu.make_async_copy(src, dst, sems.at[i])
@@ -79,9 +79,10 @@
             moved = jnp.take_along_axis(orb[c, 8 * g : 8 * g + 8, :], index, axis=1)
             pieces[c].append(jnp.where(source >= 0, moved, 0.0))
     spread = jnp.concatenate(pieces[0] + pieces[1], axis=0).astype(BF16)
-    for z in range(12):
-        zmsg_ref[z] = spread
     packed_ref[0:80, :] = spread
+    sends = [pltpu.make_async_copy(packed_ref.at[0:80, :], zmsg_hbm.at[z], sems.at[4 + z]) for z in range(12)]
+    for send in sends:
+        send.start()
     copies[2].wait()
     copies[3].wait()
     v_hi, v_lo = split(pot_s[...])
@@ -90,6 +91,8 @@
     hi, lo = split(vx)
     packed_ref[80:320, :] = hi
     packed_ref[320:560, :] = lo
+    for send in sends:
+        send.wait()
 
 
 def main_kernel(all_ref, ent_ref, slot_row_ref, slot_col_ref, wz_ref, wx_ref, bz_ref, msg_ref, out_ref):
@@ -181,34 +184,41 @@
     block = (mm_nt(left_re, p_ref[0]) + mm_nt(left_im, p_ref[1])) * (1.0 / 16384.0)
     row = [block[8 * m : 8 * m + 8, :24] for m in range(4)] + [jnp.zeros((8, 32), F32)]
     row = jnp.concatenate(row, axis=1)
-    for x in range(4):
-        block_ref[x] = row
-
-
-def pack_kernel(blocks_ref, packed_ref):
-    row = jnp.concatenate([blocks_ref[z][:, :96] for z in range(12)], axis=1)
-    for y in range(8):
-        packed_ref[y] = row
+    for peer in range(32):
+        block_ref[peer] = row
+
+
+def join_kernel(blocks_ref, joined_ref):
+    sums = [(blocks_ref[y, 0] + blocks_ref[y, 1]) + (blocks_ref[y, 2] + blocks_ref[y, 3]) for y in range(8)]
+    block = [jnp.concatenate([sums[y][:, 24 * m : 24 * m + 24] for y in range(8)], axis=1) for m in range(4)]
+    tail = [
+        jnp.concatenate([block[0][:, 128:], block[2][:, 128:]], axis=1),
+        jnp.concatenate([block[1][:, 128:], block[3][:, 128:]], axis=1),
+    ]
+    joined = jnp.concatenate([b[:, :128] for b in block] + tail, axis=0)
+    for z in range(12):
+        joined_ref[z] = joined
 
 
 def last_kernel(all_ref, s_ref, h_ref, t_s):
     for c in range(2):
         for z in range(12):
+            rows = pl.ds(z * 2 + c, 8, stride=24)
+            tail = all_ref[c, z, 32:48, :]
+            swapped = jnp.concatenate([tail[:, 64:], tail[:, :64]], axis=1)
             for m in range(4):
-                at = 96 * z + 24 * m
-                row = jnp.concatenate([all_ref[c, y, :, at : at + 24] for y in range(8)], axis=1)
-                rows = pl.ds(z * 2 + c, 8, stride=24)
-                t_s[2 * m, rows, :] = row[:, :128]
-                t_s[2 * m + 1, rows, 0:64] = row[:, 128:]
+                t_s[2 * m, rows, :] = all_ref[c, z, 8 * m : 8 * m + 8, :]
+                half = swapped if m >= 2 else tail
+                t_s[2 * m + 1, rows, :] = half[8 * (m % 2) : 8 * (m % 2) + 8]
     for m in range(4):
         ref = s_ref if m < 2 else h_ref
         ref[m % 2, 0:128, :] = t_s[2 * m].T
         ref[m % 2, 128:192, :] = t_s[2 * m + 1].T[:64]
 
 
-def call(kernel, outs, *args, scratch=(), hbm=False):
-    space = {"in_specs": [pl.BlockSpec(memory_space=pltpu.HBM)] * len(args)} if hbm else {}
+def call(kernel, outs, *args, scratch=(), hbm=False, **space):
     if hbm:
+        space["in_specs"] = [pl.BlockSpec(memory_space=pltpu.HBM)] * len(args)
         args = [pltpu.with_memory_space_constraint(a, pltpu.HBM) for a in args]
     return pl.pallas_call(
         kernel,
@@ -234,9 +244,10 @@
             pltpu.VMEM((2, 40, 128), BF16),
             pltpu.VMEM((120, 480), F32),
             pltpu.VMEM((2, 480, 256), BF16),
-            pltpu.SemaphoreType.DMA((4,)),
+            pltpu.SemaphoreType.DMA((16,)),
         ],
         hbm=True,
+        out_specs=[pl.BlockSpec(memory_space=pltpu.HBM), pl.BlockSpec(memory_space=pltpu.VMEM)],
     )
     psi = lax.all_to_all(zmsg, "z", 0, 0, tiled=True)
     everyone = lax.all_gather(packed, "x")
@@ -249,15 +260,14 @@
     rows = call(
         rows_kernel, shape((2, 32, 5120), BF16), lax.all_gather(psi, "c"), scratch=[pltpu.VMEM((1920, 128), F32)]
     )
-    block = call(product_kernel, shape((4, 8, 128), F32), rows, own, scratch=[pltpu.VMEM((1280, 128), F32)])
-    block = lax.all_to_all(block, "x", 0, 0, tiled=True).sum(axis=0)
-    blocks = lax.all_to_all(jnp.broadcast_to(block, (12, 8, 128)), "z", 0, 0, tiled=True)
-    packed = call(pack_kernel, shape((8, 8, 1152), F32), blocks)
-    packed = lax.all_to_all(packed, "y", 0, 0, tiled=True)
+    block = call(product_kernel, shape((32, 8, 128), F32), rows, own, scratch=[pltpu.VMEM((1280, 128), F32)])
+    blocks = lax.all_to_all(block, ("y", "x"), 0, 0, tiled=True)
+    joined = call(join_kernel, shape((12, 48, 128), F32), blocks.reshape(8, 4, 8, 128))
+    joined = lax.all_to_all(joined, "z", 0, 0, tiled=True)
     correlation, reduced = call(
         last_kernel,
         [shape((2, 192, 192), F32), shape((2, 192, 192), F32)],
-        lax.all_gather(packed, "c"),
+        lax.all_gather(joined, "c"),
         scratch=[pltpu.VMEM((8, 192, 128), F32)],
     )
     return out.reshape(orbitals.shape), correlation, reduced

time: 102 us -> 97 us (0.951)
  blocking collectives: 64.8 us -> 60.1 us
    all_to_all x3 -> x2, blocking collectives: 38.1 us -> 35.4 us  [the longest x1 21.8 us: body(): joined = lax.all_to_all(joined, 'z', 0, 0, tiled=True)]
    all_gather x1, blocking collectives: 10.3 us -> 8.35 us  [body(): lax.all_gather(joined, 'c')]
where the time goes in v5:
time: 97 us; the launch traced here: 96.6 us
  blocking collectives  60.1 us (62%)
  starting transfers between devices  22.7 us (23%)
  Pallas kernels  7.67 us (8%)
  waiting for transfers between devices  5.33 us (5%)
    all_to_all x1, blocking collectives, body(): joined = lax.all_to_all(joined, 'z', 0, 0, tiled=True)  21.8 us
    all_to_all x1, starting transfers between devices, body(): psi = lax.all_to_all(zmsg, 'z', 0, 0, tiled=True)  15.8 us
    all_to_all x1, blocking collectives, body(): blocks = lax.all_to_all(block, ('y', 'x'), 0, 0, tiled=True)  13.6 us
    all_gather x1, blocking collectives, body(): everyone = lax.all_gather(packed, 'x')  12 us
    all_gather x1, blocking collectives, body(): lax.all_gather(joined, 'c')  8.35 us
    pallas_call x6, Pallas kernels, call(): pl.pallas_call(kernel, out_shape=outs, scratch_shapes=list(scratch), comp...  7.67 us
    all_to_all x1, starting transfers between devices, body(): own = lax.all_to_all(msg, 'y', 0, 0, tiled=True)  6.82 us
    all_to_all x1, waiting for transfers between devices, body(): own = lax.all_to_all(msg, 'y', 0, 0, tiled=True)  5.33 us
  transfers between devices with their start and end apart: 2, of which 1 were waited for; matrix products, arithmetic and copies ran while one was open for 0% of the time, Pallas kernels for 3%

profile of v5, /device:TPU:1, one launch (start us, length us, event | category | flops | bytes accessed | tf_op | source)
XLA Modules:
  0.0 96.6 jit_solution(3487999209753372435)
XLA Ops:
  0.6 0.0 copy-start.4
  0.6 0.0 copy-start.2
  0.7 2.9 %shard_map.103 = (bf16[12,80,128]{2,1,0:T(8,128)(2,1)}, bf16[560,128]{1,0:T(8,128)(2,1)S(1)}) custom-call(s32[160,128]{1,0:T(8,128)} %ent_ref.1, bf16[2,40,128]{2,1,0:T(8,128)(2,1)} %bitcast.16, f32[120,480]{1,0:T(8,128)} %pot_hbm.1, bf16[2,480,256]{2,1,0:T(8,128)(2,1)} %constant.8.clone.bx_hbm), custom_call_target="tpu_custom_call" | custom-call | tf_op jit(solution)/shard_map/pallas_call | solution.py:223
  3.6 0.0 copy-start.1
  3.6 15.8 %all-to-all-start = ((bf16[12,80,128]{2,1,0:T(8,128)(2,1)}), bf16[12,80,128]{2,1,0:T(8,128)(2,1)S(1)}, u32[]{:S(2)}, u32[]{:S(2)}) async-start(bf16[12,80,128]{2,1,0:T(8,128)(2,1)} %get-tuple-element.11), calls=%async_computation | async-start | bytes 491520 | tf_op jit(solution)/shard_map/all_to_all | solution.py:252
  19.5 0.0 copy-start
  19.5 0.0 copy-done.4
  19.5 0.1 copy.14.slot_col_ref
  19.6 0.0 copy-start.3
  19.6 12.0 %all-gather = bf16[2240,128]{1,0:T(8,128)(2,1)S(1)} all-gather(bf16[560,128]{1,0:T(8,128)(2,1)S(1)} %get-tuple-element.9), channel_id=2, replica_groups=mesh['y'=8,'z'=12,'c'=2,'x'=4] {'x'}, dimensions={0}, use_global_device_ids=true | all-gather | bytes 716800 | tf_op jit(solution)/shard_map/all_gather | solution.py:253
  31.6 0.0 copy-done.2
  31.6 0.0 copy-done.1
  31.6 0.0 copy-done
  31.6 0.0 copy-done.3
  31.6 2.4 %shard_map.104 = (bf16[8,160,128]{2,1,0:T(8,128)(2,1)}, bf16[2,40,128]{2,1,0:T(8,128)(2,1)}) custom-call(bf16[4,560,128]{2,1,0:T(8,128)(2,1)S(1)} %bitcast.11, s32[160,128]{1,0:T(8,128)S(1)} %copy-done.3, s32[1,160]{1,0:T(1,128)S(1)} %bitcast.15, s32[160,1]{1,0:T(8,128)S(1)} %copy.14.slot_col_ref, bf16[2,256,512]{2,1,0:T(8,128)(2,1)S(1)} %copy-done.2, ...), custom_call_target="tpu_custom_call" | custom-call | tf_op jit(solution)/shard_map/pallas_call | solution.py:223
  34.0 0.0 all-to-all-done
  34.0 6.8 %all-to-all-start.1 = ((bf16[8,160,128]{2,1,0:T(8,128)(2,1)}), bf16[8,160,128]{2,1,0:T(8,128)(2,1)S(1)}, u32[]{:S(2)}, u32[]{:S(2)}) async-start(bf16[8,160,128]{2,1,0:T(8,128)(2,1)} %get-tuple-element.12), calls=%async_computation.1 | async-start | bytes 655360 | tf_op jit(solution)/shard_map/all_to_all | solution.py:259
  40.8 4.4 %all-gather.1 = bf16[24,80,128]{2,1,0:T(8,128)(2,1)S(1)} all-gather(bf16[12,80,128]{2,1,0:T(8,128)(2,1)S(1)} %all-to-all-done), channel_id=3, replica_groups=mesh['y'=8,'z'=12,'c'=2,'x'=4] {'c'}, dimensions={0}, use_global_device_ids=true | all-gather | bytes 737280 | tf_op jit(solution)/shard_map/all_gather | solution.py:261
  45.2 0.4 shard_map.105.p_ref
  45.6 5.3 %all-to-all-done.1.own_ref = bf16[8,160,128]{2,1,0:T(8,128)(2,1)S(1)} async-done(((bf16[8,160,128]{2,1,0:T(8,128)(2,1)}), bf16[8,160,128]{2,1,0:T(8,128)(2,1)S(1)}, u32[]{:S(2)}, u32[]{:S(2)}) %all-to-all-start.1) | async-done | bytes 327712 | tf_op jit(solution)/shard_map/all_to_all | solution.py:259
  51.0 0.6 shard_map.106
  51.6 13.6 %all_to_all.20 = f32[32,8,128]{2,1,0:T(8,128)S(1)} all-to-all(f32[32,8,128]{2,1,0:T(8,128)S(1)} %shard_map.106), channel_id=1, replica_groups=mesh['y'=8,'z'=12,'c'=2,'x'=4] {'y','x'}, dimensions={0} | all-to-all | bytes 262144 | tf_op jit(solution)/shard_map/all_to_all | solution.py:264
  65.2 0.1 shard_map.107
  65.3 21.8 %all_to_all.21 = f32[12,48,128]{2,1,0:T(8,128)S(1)} all-to-all(f32[12,48,128]{2,1,0:T(8,128)S(1)} %shard_map.107), channel_id=1, replica_groups=mesh['y'=8,'z'=12,'c'=2,'x'=4] {'z'}, dimensions={0} | all-to-all | bytes 589824 | tf_op jit(solution)/shard_map/all_to_all | solution.py:266
  87.1 8.3 %all-gather.2 = f32[24,48,128]{2,1,0:T(8,128)S(1)} all-gather(f32[12,48,128]{2,1,0:T(8,128)S(1)} %all_to_all.21), channel_id=4, replica_groups=mesh['y'=8,'z'=12,'c'=2,'x'=4] {'c'}, dimensions={0}, use_global_device_ids=true | all-gather | bytes 884736 | tf_op jit(solution)/shard_map/all_gather | solution.py:270
  95.4 1.2 %shard_map.108 = (f32[2,192,192]{2,1,0:T(8,128)}, f32[2,192,192]{2,1,0:T(8,128)}) custom-call(f32[2,12,48,128]{3,2,1,0:T(8,128)S(1)} %bitcast.10), custom_call_target="tpu_custom_call" | custom-call | tf_op jit(solution)/shard_map/pallas_call | solution.py:223
Async XLA Ops:
  0.6 18.8 %copy-start.4 = (s32[160]{0:T(256)S(1)}, s32[160]{0:T(256)}, u32[]{:S(2)}) copy-start(s32[160]{0:T(256)} %param.10) | copy-start | bytes 1924
  0.6 31.0 %copy-start.2 = (bf16[2,256,512]{2,1,0:T(8,128)(2,1)S(1)}, bf16[2,256,512]{2,1,0:T(8,128)(2,1)}, u32[]{:S(2)}) copy-start(bf16[2,256,512]{2,1,0:T(8,128)(2,1)} %constant.9.clone.wz_ref) | copy-start | bytes 1572868
  3.6 28.0 %copy-start.1 = (bf16[2,256,480]{2,1,0:T(8,128)(2,1)S(1)}, bf16[2,256,480]{2,1,0:T(8,128)(2,1)}, u32[]{:S(2)}) copy-start(bf16[2,256,480]{2,1,0:T(8,128)(2,1)} %constant.11.clone.bz_ref) | copy-start | bytes 1474564
  3.6 30.4 %all-to-all-start = ((bf16[12,80,128]{2,1,0:T(8,128)(2,1)}), bf16[12,80,128]{2,1,0:T(8,128)(2,1)S(1)}, u32[]{:S(2)}, u32[]{:S(2)}) async-start(bf16[12,80,128]{2,1,0:T(8,128)(2,1)} %get-tuple-element.11), calls=%async_computation | async-start | bytes 491520 | tf_op jit(solution)/shard_map/all_to_all | solution.py:252
  19.5 12.1 %copy-start = (bf16[2,512,256]{2,1,0:T(8,128)(2,1)S(1)}, bf16[2,512,256]{2,1,0:T(8,128)(2,1)}, u32[]{:S(2)}) copy-start(bf16[2,512,256]{2,1,0:T(8,128)(2,1)} %constant.10.clone.wx_ref) | copy-start | bytes 1572868
  19.6 12.0 %copy-start.3 = (s32[160,128]{1,0:T(8,128)S(1)}, s32[160,128]{1,0:T(8,128)}, u32[]{:S(2)}) copy-start(s32[160,128]{1,0:T(8,128)} %ent_ref.1) | copy-start | bytes 245764
  34.0 16.9 %all-to-all-start.1 = ((bf16[8,160,128]{2,1,0:T(8,128)(2,1)}), bf16[8,160,128]{2,1,0:T(8,128)(2,1)S(1)}, u32[]{:S(2)}, u32[]{:S(2)}) async-start(bf16[8,160,128]{2,1,0:T(8,128)(2,1)} %get-tuple-element.12), calls=%async_computation.1 | async-start | bytes 655360 | tf_op jit(solution)/shard_map/all_to_all | solution.py:259

commit v6 on v5

--- a/solution.py
+++ b/solution.py
@@ -50,20 +50,10 @@
     return lax.dot_general(a, b, (((1,), (1,)), ((), ())), preferred_element_type=F32)
 
 
-def first_kernel(ent_hbm, orb_hbm, pot_hbm, bx_hbm, zmsg_hbm, packed_ref, ent_s, orb_s, pot_s, bx_s, sems):
+def first_kernel(ent_ref, orb_ref, pot_ref, bx_ref, packed_ref):
     first = pl.multiple_of(lax.axis_index("x") * 40, 8)
-    copies = [
-        pltpu.make_async_copy(src, dst, sems.at[i])
-        for i, (src, dst) in enumerate(
-            [(ent_hbm.at[pl.ds(first, 40), :], ent_s), (orb_hbm, orb_s), (bx_hbm, bx_s), (pot_hbm, pot_s)]
-        )
-    ]
-    for copy in copies:
-        copy.start()
-    copies[0].wait()
-    copies[1].wait()
-    ent_t = ent_s[...].T
-    orb = orb_s[...].astype(F32)
+    ent_t = ent_ref[pl.ds(first, 40), :].T
+    orb = orb_ref[...].astype(F32)
     lane = lax.broadcasted_iota(jnp.int32, (128, 128), 1)
     sub = lax.broadcasted_iota(jnp.int32, (128, 128), 0)
     pieces = [[], []]
@@ -80,22 +70,15 @@
             pieces[c].append(jnp.where(source >= 0, moved, 0.0))
     spread = jnp.concatenate(pieces[0] + pieces[1], axis=0).astype(BF16)
     packed_ref[0:80, :] = spread
-    sends = [pltpu.make_async_copy(packed_ref.at[0:80, :], zmsg_hbm.at[z], sems.at[4 + z]) for z in range(12)]
-    for send in sends:
-        send.start()
-    copies[2].wait()
-    copies[3].wait()
-    v_hi, v_lo = split(pot_s[...])
-    vx = mm(v_hi, bx_s[0]) + mm(v_lo, bx_s[0]) + mm(v_hi, bx_s[1])
+    v_hi, v_lo = split(pot_ref[...])
+    vx = mm(v_hi, bx_ref[0]) + mm(v_lo, bx_ref[0]) + mm(v_hi, bx_ref[1])
     vx = jnp.concatenate([vx[:, :128], vx[:, 128:]], axis=0)
     hi, lo = split(vx)
     packed_ref[80:320, :] = hi
     packed_ref[320:560, :] = lo
-    for send in sends:
-        send.wait()
-
-
-def main_kernel(all_ref, ent_ref, slot_row_ref, slot_col_ref, wz_ref, wx_ref, bz_ref, msg_ref, out_ref):
+
+
+def main_kernel(all_ref, orb_ref, ent_ref, slot_row_ref, slot_col_ref, wz_ref, wx_ref, bz_ref, msg_ref, out_ref):
     d = lax.axis_index("x")
     first = pl.multiple_of(d * 40, 8)
 
@@ -146,14 +129,15 @@
     own = all_ref[d, 0:80, :].astype(F32)
     ent = ent_ref[pl.ds(first, 40), :]
     index = jnp.maximum(ent, 0)
-    message = [own]
+    masked, applied_rows = [], []
     for c in range(2):
         value = kinetic * own[40 * c : 40 * c + 40] + applied[40 * c : 40 * c + 40]
         h = jnp.where(inside, value, 0.0).astype(BF16).astype(F32)
-        message.append(h)
         moved = [jnp.take_along_axis(h[8 * g : 8 * g + 8], index[8 * g : 8 * g + 8], axis=1) for g in range(5)]
-        out_ref[c] = jnp.where(ent >= 0, jnp.concatenate(moved, axis=0), 0.0).astype(BF16)
-    message = jnp.concatenate(message, axis=0).astype(BF16)
+        applied_rows.append(jnp.where(ent >= 0, jnp.concatenate(moved, axis=0), 0.0))
+        masked.append(jnp.where(ent >= 0, orb_ref[c].astype(F32), 0.0))
+        out_ref[c] = applied_rows[c].astype(BF16)
+    message = jnp.concatenate(masked + applied_rows, axis=0).astype(BF16)
     for y in range(8):
         msg_ref[y] = message
 
@@ -182,7 +166,10 @@
     left_re = jnp.concatenate([m_re, m_im, a_re, a_im], axis=0).astype(BF16)
     left_im = jnp.concatenate([m_im, -m_re, a_im, -a_re], axis=0).astype(BF16)
     block = (mm_nt(left_re, p_ref[0]) + mm_nt(left_im, p_ref[1])) * (1.0 / 16384.0)
-    row = [block[8 * m : 8 * m + 8, :24] for m in range(4)] + [jnp.zeros((8, 32), F32)]
+    shift = (128 - 2 * lax.axis_index("z")) % 128
+    corr = block[:16, :24]
+    corr = pltpu.roll(jnp.concatenate([corr, corr, jnp.zeros((16, 80), F32)], axis=1), shift, 1)
+    row = [block[16:24, :24], block[24:, :24], corr[:8, :14], corr[8:, :14], jnp.zeros((8, 52), F32)]
     row = jnp.concatenate(row, axis=1)
     for peer in range(32):
         block_ref[peer] = row
@@ -190,36 +177,68 @@
 
 def join_kernel(blocks_ref, joined_ref):
     sums = [(blocks_ref[y, 0] + blocks_ref[y, 1]) + (blocks_ref[y, 2] + blocks_ref[y, 3]) for y in range(8)]
-    block = [jnp.concatenate([sums[y][:, 24 * m : 24 * m + 24] for y in range(8)], axis=1) for m in range(4)]
-    tail = [
-        jnp.concatenate([block[0][:, 128:], block[2][:, 128:]], axis=1),
-        jnp.concatenate([block[1][:, 128:], block[3][:, 128:]], axis=1),
+    ham = [jnp.concatenate([sums[y][:, 24 * m : 24 * m + 24] for y in range(8)], axis=1) for m in range(2)]
+    pad = [jnp.zeros((8, 16), F32)]
+    corr = [
+        jnp.concatenate([sums[y][:, 48 + 14 * m : 62 + 14 * m] for y in range(8)] + pad, axis=1) for m in range(2)
     ]
-    joined = jnp.concatenate([b[:, :128] for b in block] + tail, axis=0)
+    tail = jnp.concatenate([ham[0][:, 128:], ham[1][:, 128:]], axis=1)
+    joined = jnp.concatenate([ham[0][:, :128], ham[1][:, :128], tail] + corr, axis=0)
     for z in range(12):
         joined_ref[z] = joined
 
 
-def last_kernel(all_ref, s_ref, h_ref, t_s):
+def corr_lanes():
+    lane = np.arange(256)
+    ahead = (lane % 24 - 2 * np.arange(12)[:, None]) % 24
+    source = np.where((ahead < 14) & (lane < 192), lane // 24 * 14 + ahead, 0)
+    return source.reshape(24, 128).astype(np.int32)
+
+
+def last_kernel(all_ref, lane_ref, s_hbm, h_hbm, t_s, out_s, sems):
     for c in range(2):
         for z in range(12):
             rows = pl.ds(z * 2 + c, 8, stride=24)
-            tail = all_ref[c, z, 32:48, :]
-            swapped = jnp.concatenate([tail[:, 64:], tail[:, :64]], axis=1)
-            for m in range(4):
-                t_s[2 * m, rows, :] = all_ref[c, z, 8 * m : 8 * m + 8, :]
-                half = swapped if m >= 2 else tail
-                t_s[2 * m + 1, rows, :] = half[8 * (m % 2) : 8 * (m % 2) + 8]
-    for m in range(4):
-        ref = s_ref if m < 2 else h_ref
-        ref[m % 2, 0:128, :] = t_s[2 * m].T
-        ref[m % 2, 128:192, :] = t_s[2 * m + 1].T[:64]
-
-
-def call(kernel, outs, *args, scratch=(), hbm=False, **space):
-    if hbm:
-        space["in_specs"] = [pl.BlockSpec(memory_space=pltpu.HBM)] * len(args)
-        args = [pltpu.with_memory_space_constraint(a, pltpu.HBM) for a in args]
+            tail = all_ref[c, z, 16:24, :]
+            t_s[0, rows, :] = all_ref[c, z, 0:8, :]
+            t_s[1, rows, :] = tail
+            t_s[2, rows, :] = all_ref[c, z, 8:16, :]
+            t_s[3, rows, :] = jnp.concatenate([tail[:, 64:], tail[:, :64]], axis=1)
+    sends = []
+    for m in range(2):
+        out_s[m, 0:128, :] = t_s[2 * m].T
+        out_s[m, 128:192, :] = t_s[2 * m + 1].T[:64]
+        sends.append(pltpu.make_async_copy(out_s.at[m], h_hbm.at[m], sems.at[m]))
+        sends[-1].start()
+    for z in range(12):
+        low = jnp.broadcast_to(lane_ref[2 * z : 2 * z + 1, :], (8, 128))
+        high = jnp.broadcast_to(lane_ref[2 * z + 1 : 2 * z + 2, :], (8, 128))
+        for c in range(2):
+            rows = pl.ds(z * 2 + c, 8, stride=24)
+            for m in range(2):
+                corr = all_ref[c, z, 24 + 8 * m : 32 + 8 * m, :]
+                t_s[4 + 2 * m, rows, :] = jnp.take_along_axis(corr, low, axis=1)
+                t_s[5 + 2 * m, rows, :] = jnp.take_along_axis(corr, high, axis=1)
+
+    def z_of(band):
+        return (band >> 1) - 12 * ((band * 2731) >> 16)
+
+    for m in range(2):
+        low, high = t_s[4 + 2 * m], t_s[5 + 2 * m]
+        for start, count, turned in ((0, 128, low.T), (128, 64, high.T[:64])):
+            band_i = lax.broadcasted_iota(jnp.int32, (count, 192), 0) + start
+            band_j = lax.broadcasted_iota(jnp.int32, (count, 192), 1)
+            ahead = z_of(band_i) - z_of(band_j)
+            direct = ((ahead >= 0) & (ahead <= 6)) | (ahead <= -6)
+            mirror = jnp.concatenate([low[start : start + count], high[start : start + count, :64]], axis=1)
+            out_s[2 + m, start : start + count, :] = jnp.where(direct, turned, mirror if m == 0 else -mirror)
+        sends.append(pltpu.make_async_copy(out_s.at[2 + m], s_hbm.at[m], sems.at[2 + m]))
+        sends[-1].start()
+    for send in sends:
+        send.wait()
+
+
+def call(kernel, outs, *args, scratch=(), **space):
     return pl.pallas_call(
         kernel,
         out_shape=outs,
@@ -235,40 +254,29 @@
 
 def body(orbitals, potential, slot_sticks, stick_entries):
     wz, wx, bx, bz = tables(potential.shape[1], 64)
-    zmsg, packed = call(
-        first_kernel,
-        [shape((12, 80, 128), BF16), shape((560, 128), BF16)],
-        stick_entries, orbitals.reshape(2, 40, 128), potential, bx,
-        scratch=[
-            pltpu.VMEM((40, 128), jnp.int32),
-            pltpu.VMEM((2, 40, 128), BF16),
-            pltpu.VMEM((120, 480), F32),
-            pltpu.VMEM((2, 480, 256), BF16),
-            pltpu.SemaphoreType.DMA((16,)),
-        ],
-        hbm=True,
-        out_specs=[pl.BlockSpec(memory_space=pltpu.HBM), pl.BlockSpec(memory_space=pltpu.VMEM)],
-    )
-    psi = lax.all_to_all(zmsg, "z", 0, 0, tiled=True)
+    own = orbitals.reshape(2, 40, 128)
+    psi = lax.all_to_all(jnp.broadcast_to(own.reshape(80, 128), (12, 80, 128)), "z", 0, 0, tiled=True)
+    packed = call(first_kernel, shape((560, 128), BF16), stick_entries, own, potential, bx)
     everyone = lax.all_gather(packed, "x")
     msg, out = call(
         main_kernel,
         [shape((8, 160, 128), BF16), shape((2, 40, 128), BF16)],
-        everyone, stick_entries, slot_sticks.reshape(1, 160), slot_sticks.reshape(160, 1), wz, wx, bz,
-    )
-    own = lax.all_to_all(msg, "y", 0, 0, tiled=True)
+        everyone, own, stick_entries, slot_sticks.reshape(1, 160), slot_sticks.reshape(160, 1), wz, wx, bz,
+    )
+    arrived = lax.all_to_all(msg, "y", 0, 0, tiled=True)
     rows = call(
         rows_kernel, shape((2, 32, 5120), BF16), lax.all_gather(psi, "c"), scratch=[pltpu.VMEM((1920, 128), F32)]
     )
-    block = call(product_kernel, shape((32, 8, 128), F32), rows, own, scratch=[pltpu.VMEM((1280, 128), F32)])
+    block = call(product_kernel, shape((32, 8, 128), F32), rows, arrived, scratch=[pltpu.VMEM((1280, 128), F32)])
     blocks = lax.all_to_all(block, ("y", "x"), 0, 0, tiled=True)
-    joined = call(join_kernel, shape((12, 48, 128), F32), blocks.reshape(8, 4, 8, 128))
+    joined = call(join_kernel, shape((12, 40, 128), F32), blocks.reshape(8, 4, 8, 128))
     joined = lax.all_to_all(joined, "z", 0, 0, tiled=True)
     correlation, reduced = call(
         last_kernel,
         [shape((2, 192, 192), F32), shape((2, 192, 192), F32)],
-        lax.all_gather(joined, "c"),
-        scratch=[pltpu.VMEM((8, 192, 128), F32)],
+        lax.all_gather(joined, "c"), corr_lanes(),
+        scratch=[pltpu.VMEM((8, 192, 128), F32), pltpu.VMEM((4, 192, 192), F32), pltpu.SemaphoreType.DMA((4,))],
+        out_specs=[pl.BlockSpec(memory_space=pltpu.HBM)] * 2,
     )
     return out.reshape(orbitals.shape), correlation, reduced
 

time: 97 us -> 97.4 us (level)
  local copies, waits for them, and re-layouts: 0.14 us -> 2.38 us
  Pallas kernels: 7.67 us -> 6.41 us
    broadcast_in_dim x0 -> x1, local copies, waits for them, and re-layouts: none -> 1.51 us  [body(): jnp.broadcast_to(own.reshape(80, 128), (12, 80, 128))]
    pallas_call x6, Pallas kernels: 7.67 us -> 6.41 us  [call(): pl.pallas_call(kernel, out_shape=outs, scratch_shapes=list(scratch), comp...]
  transfers between devices with their start and end apart: 2 -> 2, of which waited for: 1 -> 1; matrix products, arithmetic and copies ran while one was open for 0% -> 0% of each run, Pallas kernels for 3% -> 4%
where the time goes in v6:
time: 97.4 us; the launch traced here: 96.9 us
  blocking collectives  59.4 us (61%)
  starting transfers between devices  22.6 us (23%)
  Pallas kernels  6.41 us (7%)
  waiting for transfers between devices  5.37 us (6%)
  local copies, waits for them, and re-layouts  2.38 us (2%)
    all_to_all x1, blocking collectives, body(): joined = lax.all_to_all(joined, 'z', 0, 0, tiled=True)  20.9 us
    all_to_all x1, starting transfers between devices, body(): lax.all_to_all(jnp.broadcast_to(own.reshape(80, 128), (12, 80, 128)), 'z'...  15.8 us
    all_to_all x1, blocking collectives, body(): blocks = lax.all_to_all(block, ('y', 'x'), 0, 0, tiled=True)  13.6 us
    all_gather x1, blocking collectives, body(): everyone = lax.all_gather(packed, 'x')  12 us
    all_gather x1, blocking collectives, body(): lax.all_gather(joined, 'c')  8.51 us
    all_to_all x1, starting transfers between devices, body(): arrived = lax.all_to_all(msg, 'y', 0, 0, tiled=True)  6.81 us
    pallas_call x6, Pallas kernels, call(): pl.pallas_call(kernel, out_shape=outs, scratch_shapes=list(scratch), comp...  6.41 us
    all_to_all x1, waiting for transfers between devices, body(): arrived = lax.all_to_all(msg, 'y', 0, 0, tiled=True)  5.36 us
  transfers between devices with their start and end apart: 2, of which 1 were waited for; matrix products, arithmetic and copies ran while one was open for 0% of the time, Pallas kernels for 4%

profile of v6, /device:TPU:1, one launch (start us, length us, event | category | flops | bytes accessed | tf_op | source)
XLA Modules:
  0.0 96.9 jit_solution(11307108395769532937)
XLA Ops:
  0.6 0.0 copy-start.3
  0.6 1.5 %broadcast_in_dim.3 = bf16[12,80,128]{2,1,0:T(8,128)(2,1)} broadcast(bf16[80,128]{1,0:T(8,128)(2,1)} %bitcast.15), dimensions={1,2} | broadcast | bytes 266240 | tf_op jit(solution)/shard_map/broadcast_in_dim | solution.py:258
  2.2 0.0 copy-start.8
  2.2 0.0 copy-start.5
  2.2 0.0 copy-start.6
  2.2 15.8 %all-to-all-start = ((bf16[12,80,128]{2,1,0:T(8,128)(2,1)}), bf16[12,80,128]{2,1,0:T(8,128)(2,1)S(1)}, u32[]{:S(2)}, u32[]{:S(2)}) async-start(bf16[12,80,128]{2,1,0:T(8,128)(2,1)} %broadcast_in_dim.3), calls=%async_computation | async-start | bytes 491520 | tf_op jit(solution)/shard_map/all_to_all | solution.py:258
  18.0 0.0 copy-start.4
  18.0 0.0 copy-done.8
  18.0 0.1 copy.15.slot_col_ref
  18.1 0.0 copy-done.3
  18.1 0.0 copy-done.5
  18.1 0.0 copy-done.6
  18.2 0.7 copy-done.4
  18.9 0.0 copy-start.1
  18.9 1.3 %shard_map.112 = bf16[560,128]{1,0:T(8,128)(2,1)S(1)} custom-call(s32[160,128]{1,0:T(8,128)S(1)} %copy-done.4, bf16[2,40,128]{2,1,0:T(8,128)(2,1)S(1)} %bitcast.16, f32[120,480]{1,0:T(8,128)S(1)} %copy-done.5, bf16[2,480,256]{2,1,0:T(8,128)(2,1)S(1)} %copy-done.3), custom_call_target="tpu_custom_call" | custom-call | tf_op jit(solution)/shard_map/pallas_call | solution.py:242
  20.2 12.0 %all-gather = bf16[2240,128]{1,0:T(8,128)(2,1)S(1)} all-gather(bf16[560,128]{1,0:T(8,128)(2,1)S(1)} %shard_map.112), channel_id=2, replica_groups=mesh['y'=8,'z'=12,'c'=2,'x'=4] {'x'}, dimensions={0}, use_global_device_ids=true | all-gather | bytes 716800 | tf_op jit(solution)/shard_map/all_gather | solution.py:260
  32.2 0.0 copy-done.1
  32.2 0.0 copy-done.2
  32.2 0.0 copy-done
  32.2 2.5 %shard_map.113 = (bf16[8,160,128]{2,1,0:T(8,128)(2,1)}, bf16[2,40,128]{2,1,0:T(8,128)(2,1)}) custom-call(bf16[4,560,128]{2,1,0:T(8,128)(2,1)S(1)} %bitcast.11, bf16[2,40,128]{2,1,0:T(8,128)(2,1)S(1)} %bitcast.17, s32[160,128]{1,0:T(8,128)S(1)} %copy-done.4, s32[1,160]{1,0:T(1,128)S(1)} %bitcast.19, s32[160,1]{1,0:T(8,128)S(1)} %copy.15.slot_col_ref, ...), custom_call_target="tpu_custom_call" | custom-call | tf_op jit(solution)/shard_map/pallas_call | solution.py:242
  34.7 0.0 all-to-all-done
  34.7 6.8 %all-to-all-start.1 = ((bf16[8,160,128]{2,1,0:T(8,128)(2,1)}), bf16[8,160,128]{2,1,0:T(8,128)(2,1)S(1)}, u32[]{:S(2)}, u32[]{:S(2)}) async-start(bf16[8,160,128]{2,1,0:T(8,128)(2,1)} %get-tuple-element.8), calls=%async_computation.1 | async-start | bytes 655360 | tf_op jit(solution)/shard_map/all_to_all | solution.py:266
  41.5 4.4 %all-gather.1 = bf16[24,80,128]{2,1,0:T(8,128)(2,1)S(1)} all-gather(bf16[12,80,128]{2,1,0:T(8,128)(2,1)S(1)} %all-to-all-done), channel_id=3, replica_groups=mesh['y'=8,'z'=12,'c'=2,'x'=4] {'c'}, dimensions={0}, use_global_device_ids=true | all-gather | bytes 737280 | tf_op jit(solution)/shard_map/all_gather | solution.py:268
  45.9 0.4 shard_map.114.p_ref
  46.3 5.4 %all-to-all-done.1.own_ref = bf16[8,160,128]{2,1,0:T(8,128)(2,1)S(1)} async-done(((bf16[8,160,128]{2,1,0:T(8,128)(2,1)}), bf16[8,160,128]{2,1,0:T(8,128)(2,1)S(1)}, u32[]{:S(2)}, u32[]{:S(2)}) %all-to-all-start.1) | async-done | bytes 327712 | tf_op jit(solution)/shard_map/all_to_all | solution.py:266
  51.7 0.7 shard_map.115
  52.4 13.6 %all_to_all.20 = f32[32,8,128]{2,1,0:T(8,128)S(1)} all-to-all(f32[32,8,128]{2,1,0:T(8,128)S(1)} %shard_map.115), channel_id=1, replica_groups=mesh['y'=8,'z'=12,'c'=2,'x'=4] {'y','x'}, dimensions={0} | all-to-all | bytes 262144 | tf_op jit(solution)/shard_map/all_to_all | solution.py:271
  66.0 0.1 shard_map.116
  66.2 20.9 %all_to_all.21 = f32[12,40,128]{2,1,0:T(8,128)S(1)} all-to-all(f32[12,40,128]{2,1,0:T(8,128)S(1)} %shard_map.116), channel_id=1, replica_groups=mesh['y'=8,'z'=12,'c'=2,'x'=4] {'z'}, dimensions={0} | all-to-all | bytes 491520 | tf_op jit(solution)/shard_map/all_to_all | solution.py:273
  87.1 8.5 %all-gather.2 = f32[24,40,128]{2,1,0:T(8,128)S(1)} all-gather(f32[12,40,128]{2,1,0:T(8,128)S(1)} %all_to_all.21), channel_id=4, replica_groups=mesh['y'=8,'z'=12,'c'=2,'x'=4] {'c'}, dimensions={0}, use_global_device_ids=true | all-gather | bytes 737280 | tf_op jit(solution)/shard_map/all_gather | solution.py:277
  95.6 0.0 copy-done.7
  95.6 1.3 %shard_map.117 = (f32[2,192,192]{2,1,0:T(8,128)}, f32[2,192,192]{2,1,0:T(8,128)}) custom-call(f32[2,12,40,128]{3,2,1,0:T(8,128)S(1)} %bitcast.12, s32[24,128]{1,0:T(8,128)S(1)} %copy-done.7), custom_call_target="tpu_custom_call" | custom-call | tf_op jit(solution)/shard_map/pallas_call | solution.py:242
  (3 shorter events, 0.0 us)
Async XLA Ops:
  0.6 17.5 %copy-start.3 = (bf16[2,480,256]{2,1,0:T(8,128)(2,1)S(1)}, bf16[2,480,256]{2,1,0:T(8,128)(2,1)}, u32[]{:S(2)}) copy-start(bf16[2,480,256]{2,1,0:T(8,128)(2,1)} %constant.10.clone.bx_ref) | copy-start | bytes 1474564
  2.2 15.9 %copy-start.8 = (s32[160]{0:T(256)S(1)}, s32[160]{0:T(256)}, u32[]{:S(2)}) copy-start(s32[160]{0:T(256)} %param.11) | copy-start | bytes 1924
  2.2 16.0 %copy-start.5 = (f32[120,480]{1,0:T(8,128)S(1)}, f32[120,480]{1,0:T(8,128)}, u32[]{:S(2)}) copy-start(f32[120,480]{1,0:T(8,128)} %pot_ref.1) | copy-start | bytes 691204
  2.2 16.0 %copy-start.6 = (bf16[2,1,40,128]{3,2,1,0:T(8,128)(2,1)S(1)}, bf16[2,1,40,128]{3,2,1,0:T(8,128)(2,1)}, u32[]{:S(2)}) copy-start(bf16[2,1,40,128]{3,2,1,0:T(8,128)(2,1)} %param.9) | copy-start | bytes 61444
  2.2 32.6 %all-to-all-start = ((bf16[12,80,128]{2,1,0:T(8,128)(2,1)}), bf16[12,80,128]{2,1,0:T(8,128)(2,1)S(1)}, u32[]{:S(2)}, u32[]{:S(2)}) async-start(bf16[12,80,128]{2,1,0:T(8,128)(2,1)} %broadcast_in_dim.3), calls=%async_computation | async-start | bytes 491520 | tf_op jit(solution)/shard_map/all_to_all | solution.py:258
  18.0 0.9 copy-start.4
  18.9 13.3 %copy-start.1 = (bf16[2,512,256]{2,1,0:T(8,128)(2,1)S(1)}, bf16[2,512,256]{2,1,0:T(8,128)(2,1)}, u32[]{:S(2)}) copy-start(bf16[2,512,256]{2,1,0:T(8,128)(2,1)} %constant.12.clone.wx_ref) | copy-start | bytes 1572868
  18.9 13.3 %copy-start.2 = (bf16[2,256,480]{2,1,0:T(8,128)(2,1)S(1)}, bf16[2,256,480]{2,1,0:T(8,128)(2,1)}, u32[]{:S(2)}) copy-start(bf16[2,256,480]{2,1,0:T(8,128)(2,1)} %constant.13.clone.bz_ref) | copy-start | bytes 1474564
  20.2 12.0 %copy-start = (bf16[2,256,512]{2,1,0:T(8,128)(2,1)S(1)}, bf16[2,256,512]{2,1,0:T(8,128)(2,1)}, u32[]{:S(2)}) copy-start(bf16[2,256,512]{2,1,0:T(8,128)(2,1)} %constant.11.clone.wz_ref) | copy-start | bytes 1572868
  34.7 17.0 %all-to-all-start.1 = ((bf16[8,160,128]{2,1,0:T(8,128)(2,1)}), bf16[8,160,128]{2,1,0:T(8,128)(2,1)S(1)}, u32[]{:S(2)}, u32[]{:S(2)}) async-start(bf16[8,160,128]{2,1,0:T(8,128)(2,1)} %get-tuple-element.8), calls=%async_computation.1 | async-start | bytes 655360 | tf_op jit(solution)/shard_map/all_to_all | solution.py:266
  87.1 8.5 %copy-start.7 = (s32[24,128]{1,0:T(8,128)S(1)}, s32[24,128]{1,0:T(8,128)}, u32[]{:S(2)}) copy-start(s32[24,128]{1,0:T(8,128)} %constant.14.clone.lane_ref) | copy-start | bytes 36868

commit v7 on v6

--- a/solution.py
+++ b/solution.py
@@ -13,6 +13,16 @@
 M = 256
 F32 = jnp.float32
 BF16 = jnp.bfloat16
+
+FIRST_Z, FIRST_Y, FIRST_YX, LAST_Z = 10, 2, (6, 2), 4
+
+
+def turned(first, count):
+    return [(first + k) % count for k in range(count)]
+
+
+Z_ORDER, Y_ORDER, TAIL_ORDER = turned(FIRST_Z, 12), turned(FIRST_Y, 8), turned(LAST_Z, 12)
+YX_ORDER = [4 * y + x for y in turned(FIRST_YX[0], 8) for x in turned(FIRST_YX[1], 4)]
 
 
 def hi_lo(table):
@@ -50,9 +60,22 @@
     return lax.dot_general(a, b, (((1,), (1,)), ((), ())), preferred_element_type=F32)
 
 
+def start_kernel(ent_hbm, orb_hbm, pot_hbm, zmsg_hbm, ent_ref, orb_ref, pot_ref, sems):
+    first = pl.multiple_of(lax.axis_index("x") * 40, 8)
+    pairs = [(orb_hbm, orb_ref), (ent_hbm.at[pl.ds(first, 40), :], ent_ref), (pot_hbm, pot_ref)]
+    pairs += [(orb_ref, zmsg_hbm.at[z]) for z in range(12)]
+    copies = [pltpu.make_async_copy(src, dst, sems.at[i]) for i, (src, dst) in enumerate(pairs)]
+    for copy in copies[:3]:
+        copy.start()
+    copies[0].wait()
+    for copy in copies[3:]:
+        copy.start()
+    for copy in copies[1:]:
+        copy.wait()
+
+
 def first_kernel(ent_ref, orb_ref, pot_ref, bx_ref, packed_ref):
-    first = pl.multiple_of(lax.axis_index("x") * 40, 8)
-    ent_t = ent_ref[pl.ds(first, 40), :].T
+    ent_t = ent_ref[...].T
     orb = orb_ref[...].astype(F32)
     lane = lax.broadcasted_iota(jnp.int32, (128, 128), 1)
     sub = lax.broadcasted_iota(jnp.int32, (128, 128), 0)
@@ -127,7 +150,7 @@
     inside = (square < 64 * 64) & (slot >= 0)
     kinetic = square.astype(F32) * (1.0 / 4096.0)
     own = all_ref[d, 0:80, :].astype(F32)
-    ent = ent_ref[pl.ds(first, 40), :]
+    ent = ent_ref[...]
     index = jnp.maximum(ent, 0)
     masked, applied_rows = [], []
     for c in range(2):
@@ -144,9 +167,10 @@
 
 def rows_kernel(psi_ref, p_ref, psi_s):
     for c in range(2):
-        for z in range(12):
+        for k, z in enumerate(Z_ORDER):
             at = (2 * z + c) * 80
-            psi_s[at : at + 80, :] = psi_ref[c, z].astype(F32)
+            for part in range(2):
+                psi_s[at + 40 * part : at + 40 * part + 40, :] = psi_ref[c, k, part].astype(F32)
     pad = jnp.zeros((8, 128), F32)
     for part in range(2):
         for s in range(40):
@@ -155,8 +179,8 @@
 
 
 def product_kernel(p_ref, own_ref, block_ref, own_s):
-    for y in range(8):
-        own_s[160 * y : 160 * y + 160, :] = own_ref[y].astype(F32)
+    for k, y in enumerate(Y_ORDER):
+        own_s[160 * y : 160 * y + 160, :] = own_ref[k].astype(F32)
 
     def entries(first):
         rows = [own_s[pl.ds(first + s, 8, stride=160), :] for s in range(40)]
@@ -176,7 +200,10 @@
 
 
 def join_kernel(blocks_ref, joined_ref):
-    sums = [(blocks_ref[y, 0] + blocks_ref[y, 1]) + (blocks_ref[y, 2] + blocks_ref[y, 3]) for y in range(8)]
+    def part(y, x):
+        return blocks_ref[YX_ORDER.index(4 * y + x)]
+
+    sums = [(part(y, 0) + part(y, 1)) + (part(y, 2) + part(y, 3)) for y in range(8)]
     ham = [jnp.concatenate([sums[y][:, 24 * m : 24 * m + 24] for y in range(8)], axis=1) for m in range(2)]
     pad = [jnp.zeros((8, 16), F32)]
     corr = [
@@ -197,12 +224,12 @@
 
 def last_kernel(all_ref, lane_ref, s_hbm, h_hbm, t_s, out_s, sems):
     for c in range(2):
-        for z in range(12):
+        for k, z in enumerate(TAIL_ORDER):
             rows = pl.ds(z * 2 + c, 8, stride=24)
-            tail = all_ref[c, z, 16:24, :]
-            t_s[0, rows, :] = all_ref[c, z, 0:8, :]
+            tail = all_ref[c, k, 16:24, :]
+            t_s[0, rows, :] = all_ref[c, k, 0:8, :]
             t_s[1, rows, :] = tail
-            t_s[2, rows, :] = all_ref[c, z, 8:16, :]
+            t_s[2, rows, :] = all_ref[c, k, 8:16, :]
             t_s[3, rows, :] = jnp.concatenate([tail[:, 64:], tail[:, :64]], axis=1)
     sends = []
     for m in range(2):
@@ -210,13 +237,13 @@
         out_s[m, 128:192, :] = t_s[2 * m + 1].T[:64]
         sends.append(pltpu.make_async_copy(out_s.at[m], h_hbm.at[m], sems.at[m]))
         sends[-1].start()
-    for z in range(12):
+    for k, z in enumerate(TAIL_ORDER):
         low = jnp.broadcast_to(lane_ref[2 * z : 2 * z + 1, :], (8, 128))
         high = jnp.broadcast_to(lane_ref[2 * z + 1 : 2 * z + 2, :], (8, 128))
         for c in range(2):
             rows = pl.ds(z * 2 + c, 8, stride=24)
             for m in range(2):
-                corr = all_ref[c, z, 24 + 8 * m : 32 + 8 * m, :]
+                corr = all_ref[c, k, 24 + 8 * m : 32 + 8 * m, :]
                 t_s[4 + 2 * m, rows, :] = jnp.take_along_axis(corr, low, axis=1)
                 t_s[5 + 2 * m, rows, :] = jnp.take_along_axis(corr, high, axis=1)
 
@@ -252,25 +279,37 @@
     return jax.ShapeDtypeStruct(dims, dtype)
 
 
+def exchange(array, axis, order):
+    return lax.all_to_all(array, axis, 0, 0, tiled=True, axis_index_groups=[order])
+
+
 def body(orbitals, potential, slot_sticks, stick_entries):
     wz, wx, bx, bz = tables(potential.shape[1], 64)
-    own = orbitals.reshape(2, 40, 128)
-    psi = lax.all_to_all(jnp.broadcast_to(own.reshape(80, 128), (12, 80, 128)), "z", 0, 0, tiled=True)
-    packed = call(first_kernel, shape((560, 128), BF16), stick_entries, own, potential, bx)
+    args = [stick_entries, orbitals.reshape(2, 40, 128), potential]
+    zmsg, ent, own, pot = call(
+        start_kernel,
+        [shape((12, 2, 40, 128), BF16), shape((40, 128), jnp.int32), shape((2, 40, 128), BF16), shape((120, 480), F32)],
+        *[pltpu.with_memory_space_constraint(a, pltpu.HBM) for a in args],
+        scratch=[pltpu.SemaphoreType.DMA((15,))],
+        in_specs=[pl.BlockSpec(memory_space=pltpu.HBM)] * 3,
+        out_specs=[pl.BlockSpec(memory_space=pltpu.HBM)] + [pl.BlockSpec(memory_space=pltpu.VMEM)] * 3,
+    )
+    psi = exchange(zmsg, "z", Z_ORDER)
+    packed = call(first_kernel, shape((560, 128), BF16), ent, own, pot, bx)
     everyone = lax.all_gather(packed, "x")
     msg, out = call(
         main_kernel,
         [shape((8, 160, 128), BF16), shape((2, 40, 128), BF16)],
-        everyone, own, stick_entries, slot_sticks.reshape(1, 160), slot_sticks.reshape(160, 1), wz, wx, bz,
-    )
-    arrived = lax.all_to_all(msg, "y", 0, 0, tiled=True)
+        everyone, own, ent, slot_sticks.reshape(1, 160), slot_sticks.reshape(160, 1), wz, wx, bz,
+    )
+    arrived = exchange(msg, "y", Y_ORDER)
     rows = call(
         rows_kernel, shape((2, 32, 5120), BF16), lax.all_gather(psi, "c"), scratch=[pltpu.VMEM((1920, 128), F32)]
     )
     block = call(product_kernel, shape((32, 8, 128), F32), rows, arrived, scratch=[pltpu.VMEM((1280, 128), F32)])
-    blocks = lax.all_to_all(block, ("y", "x"), 0, 0, tiled=True)
-    joined = call(join_kernel, shape((12, 40, 128), F32), blocks.reshape(8, 4, 8, 128))
-    joined = lax.all_to_all(joined, "z", 0, 0, tiled=True)
+    blocks = exchange(block, ("y", "x"), YX_ORDER)
+    joined = call(join_kernel, shape((12, 40, 128), F32), blocks)
+    joined = exchange(joined, "z", TAIL_ORDER)
     correlation, reduced = call(
         last_kernel,
         [shape((2, 192, 192), F32), shape((2, 192, 192), F32)],

time: 97.4 us -> 91.1 us (0.935)
  blocking collectives: 59.4 us -> 53.6 us
  waiting for transfers between devices: 5.37 us -> 3.55 us
  Pallas kernels: 6.41 us -> 8.02 us
  local copies, waits for them, and re-layouts: 2.38 us -> 0.81 us
  starting transfers between devices: 22.6 us -> 23.9 us
    all_to_all x2, blocking collectives: 34.5 us -> 27.6 us  [exchange(): lax.all_to_all(array, axis, 0, 0, tiled=True, axis_index_groups=[order])]
    all_to_all x2, waiting for transfers between devices: 5.37 us -> 3.55 us  [exchange(): lax.all_to_all(array, axis, 0, 0, tiled=True, axis_index_groups=[order])]
    pallas_call x6 -> x7, Pallas kernels: 6.41 us -> 8.02 us  [call(): pl.pallas_call(kernel, out_shape=outs, scratch_shapes=list(scratch), comp...]
    broadcast_in_dim x1 -> x0, local copies, waits for them, and re-layouts: 1.51 us -> none  [body(): jnp.broadcast_to(own.reshape(80, 128), (12, 80, 128))]
    all_to_all x2, starting transfers between devices: 22.6 us -> 23.9 us  [exchange(): lax.all_to_all(array, axis, 0, 0, tiled=True, axis_index_groups=[order])]
  transfers between devices with their start and end apart: 2 -> 2, of which waited for: 1 -> 1; matrix products, arithmetic and copies ran while one was open for 0% -> 0% of each run, Pallas kernels for 4% -> 5%
where the time goes in v7:
time: 91.1 us; the launch traced here: 90.6 us
  blocking collectives  53.6 us (59%)
  starting transfers between devices  23.9 us (26%)
  Pallas kernels  8.02 us (9%)
  waiting for transfers between devices  3.55 us (4%)
    all_to_all x2, blocking collectives, exchange(): lax.all_to_all(array, axis, 0, 0, tiled=True, axis_index_groups=[order])  27.6 us
    all_to_all x2, starting transfers between devices, exchange(): lax.all_to_all(array, axis, 0, 0, tiled=True, axis_index_groups=[order])  23.9 us
    all_gather x1, blocking collectives, body(): everyone = lax.all_gather(packed, 'x')  11.9 us
    all_gather x1, blocking collectives, body(): lax.all_gather(joined, 'c')  9.34 us
    pallas_call x7, Pallas kernels, call(): pl.pallas_call(kernel, out_shape=outs, scratch_shapes=list(scratch), comp...  8.02 us
    all_gather x1, blocking collectives, body(): lax.all_gather(psi, 'c')  4.7 us
    all_to_all x2, waiting for transfers between devices, exchange(): lax.all_to_all(array, axis, 0, 0, tiled=True, axis_index_groups=[order])  3.55 us
  transfers between devices with their start and end apart: 2, of which 1 were waited for; matrix products, arithmetic and copies ran while one was open for 0% of the time, Pallas kernels for 5%

profile of v7, /device:TPU:1, one launch (start us, length us, event | category | flops | bytes accessed | tf_op | source)
XLA Modules:
  0.0 90.6 jit_solution(13980780321477821690)
XLA Ops:
  0.6 0.0 copy-start.3
  0.6 1.6 %shard_map.112 = (bf16[12,2,40,128]{3,2,1,0:T(8,128)(2,1)}, s32[40,128]{1,0:T(8,128)S(1)}, bf16[2,40,128]{2,1,0:T(8,128)(2,1)S(1)}, f32[120,480]{1,0:T(8,128)S(1)}) custom-call(s32[160,128]{1,0:T(8,128)} %ent_hbm.1, bf16[2,40,128]{2,1,0:T(8,128)(2,1)} %bitcast.14, f32[120,480]{1,0:T(8,128)} %pot_hbm.1), custom_call_target="tpu_custom_call" | custom-call | tf_op jit(solution)/shard_map/pallas_call | solution.py:269
  2.2 16.6 %all-to-all-start = ((bf16[12,2,40,128]{3,2,1,0:T(8,128)(2,1)}), bf16[12,2,40,128]{3,2,1,0:T(8,128)(2,1)S(1)}, u32[]{:S(2)}, u32[]{:S(2)}) async-start(bf16[12,2,40,128]{3,2,1,0:T(8,128)(2,1)} %get-tuple-element.15), calls=%async_computation | async-start | bytes 491520 | tf_op jit(solution)/shard_map/all_to_all | solution.py:283
  18.9 0.0 copy-start.5
  18.9 0.7 copy-done.5
  19.5 0.1 copy.15.slot_col_ref
  19.6 0.0 copy-done.3
  19.7 0.0 copy-start.1
  19.7 0.0 copy-start.2
  19.7 1.3 %shard_map.113 = bf16[560,128]{1,0:T(8,128)(2,1)S(1)} custom-call(s32[40,128]{1,0:T(8,128)S(1)} %get-tuple-element.11.ent_ref, bf16[2,40,128]{2,1,0:T(8,128)(2,1)S(1)} %get-tuple-element.12.orb_ref, f32[120,480]{1,0:T(8,128)S(1)} %get-tuple-element.13.pot_ref, bf16[2,480,256]{2,1,0:T(8,128)(2,1)S(1)} %copy-done.3), custom_call_target="tpu_custom_call" | custom-call | tf_op jit(solution)/shard_map/pallas_call | solution.py:269
  21.0 0.0 copy-start
  21.0 11.9 %all-gather = bf16[2240,128]{1,0:T(8,128)(2,1)S(1)} all-gather(bf16[560,128]{1,0:T(8,128)(2,1)S(1)} %shard_map.113), channel_id=2, replica_groups=mesh['y'=8,'z'=12,'c'=2,'x'=4] {'x'}, dimensions={0}, use_global_device_ids=true | all-gather | bytes 716800 | tf_op jit(solution)/shard_map/all_gather | solution.py:299
  33.0 0.0 copy-done.1
  33.0 0.0 copy-done.2
  33.0 0.0 copy-done
  33.0 2.5 %shard_map.114 = (bf16[8,160,128]{2,1,0:T(8,128)(2,1)}, bf16[2,40,128]{2,1,0:T(8,128)(2,1)}) custom-call(bf16[4,560,128]{2,1,0:T(8,128)(2,1)S(1)} %bitcast.9, bf16[2,40,128]{2,1,0:T(8,128)(2,1)S(1)} %get-tuple-element.12.orb_ref, s32[40,128]{1,0:T(8,128)S(1)} %get-tuple-element.11.ent_ref, s32[1,160]{1,0:T(1,128)S(1)} %bitcast.13, ...), custom_call_target="tpu_custom_call" | custom-call | tf_op jit(solution)/shard_map/pallas_call | solution.py:269
  35.5 0.0 all-to-all-done
  35.5 7.3 %all-to-all-start.1 = ((bf16[8,160,128]{2,1,0:T(8,128)(2,1)}), bf16[8,160,128]{2,1,0:T(8,128)(2,1)S(1)}, u32[]{:S(2)}, u32[]{:S(2)}) async-start(bf16[8,160,128]{2,1,0:T(8,128)(2,1)} %get-tuple-element.16), calls=%async_computation.1 | async-start | bytes 655360 | tf_op jit(solution)/shard_map/all_to_all | solution.py:283
  42.8 4.7 %all-gather.1 = bf16[24,2,40,128]{3,2,1,0:T(8,128)(2,1)S(1)} all-gather(bf16[12,2,40,128]{3,2,1,0:T(8,128)(2,1)S(1)} %all-to-all-done), channel_id=3, replica_groups=mesh['y'=8,'z'=12,'c'=2,'x'=4] {'c'}, dimensions={0}, use_global_device_ids=true | all-gather | bytes 737280 | tf_op jit(solution)/shard_map/all_gather | solution.py:307
  47.5 0.4 shard_map.115.p_ref
  47.9 3.5 %all-to-all-done.1.own_ref = bf16[8,160,128]{2,1,0:T(8,128)(2,1)S(1)} async-done(((bf16[8,160,128]{2,1,0:T(8,128)(2,1)}), bf16[8,160,128]{2,1,0:T(8,128)(2,1)S(1)}, u32[]{:S(2)}, u32[]{:S(2)}) %all-to-all-start.1) | async-done | bytes 327712 | tf_op jit(solution)/shard_map/all_to_all | solution.py:283
  51.5 0.8 shard_map.116
  52.2 12.5 %all_to_all.20.blocks_ref = f32[32,8,128]{2,1,0:T(8,128)S(1)} all-to-all(f32[32,8,128]{2,1,0:T(8,128)S(1)} %shard_map.116), channel_id=1, replica_groups={{578,579,576,577,674,675,672,673,2,3,0,1,98,99,96,97,194,195,192,193,29..., dimensions={0} | all-to-all | bytes 262144 | tf_op jit(solution)/shard_map/all_to_all | solution.py:283
  64.7 0.1 shard_map.117
  64.8 15.2 %all_to_all.21 = f32[12,40,128]{2,1,0:T(8,128)S(1)} all-to-all(f32[12,40,128]{2,1,0:T(8,128)S(1)} %shard_map.117), channel_id=1, replica_groups={{32,40,48,56,64,72,80,88,0,8,16,24},{33,41,49,57,65,73,81,89,1,9,17,25}..., dimensions={0} | all-to-all | bytes 491520 | tf_op jit(solution)/shard_map/all_to_all | solution.py:283
  80.0 0.0 copy-start.4
  80.0 9.3 %all-gather.2 = f32[24,40,128]{2,1,0:T(8,128)S(1)} all-gather(f32[12,40,128]{2,1,0:T(8,128)S(1)} %all_to_all.21), channel_id=4, replica_groups=mesh['y'=8,'z'=12,'c'=2,'x'=4] {'c'}, dimensions={0}, use_global_device_ids=true | all-gather | bytes 737280 | tf_op jit(solution)/shard_map/all_gather | solution.py:316
  89.3 0.0 copy-done.4
  89.3 1.3 %shard_map.118 = (f32[2,192,192]{2,1,0:T(8,128)}, f32[2,192,192]{2,1,0:T(8,128)}) custom-call(f32[2,12,40,128]{3,2,1,0:T(8,128)S(1)} %bitcast.10, s32[24,128]{1,0:T(8,128)S(1)} %copy-done.4), custom_call_target="tpu_custom_call" | custom-call | tf_op jit(solution)/shard_map/pallas_call | solution.py:269
Async XLA Ops:
  0.6 19.0 %copy-start.3 = (bf16[2,480,256]{2,1,0:T(8,128)(2,1)S(1)}, bf16[2,480,256]{2,1,0:T(8,128)(2,1)}, u32[]{:S(2)}) copy-start(bf16[2,480,256]{2,1,0:T(8,128)(2,1)} %constant.10.clone.bx_ref) | copy-start | bytes 1474564
  2.2 33.2 %all-to-all-start = ((bf16[12,2,40,128]{3,2,1,0:T(8,128)(2,1)}), bf16[12,2,40,128]{3,2,1,0:T(8,128)(2,1)S(1)}, u32[]{:S(2)}, u32[]{:S(2)}) async-start(bf16[12,2,40,128]{3,2,1,0:T(8,128)(2,1)} %get-tuple-element.15), calls=%async_computation | async-start | bytes 491520 | tf_op jit(solution)/shard_map/all_to_all | solution.py:283
  18.9 0.7 copy-start.5
  19.7 13.3 %copy-start.1 = (bf16[2,512,256]{2,1,0:T(8,128)(2,1)S(1)}, bf16[2,512,256]{2,1,0:T(8,128)(2,1)}, u32[]{:S(2)}) copy-start(bf16[2,512,256]{2,1,0:T(8,128)(2,1)} %constant.12.clone.wx_ref) | copy-start | bytes 1572868
  19.7 13.3 %copy-start.2 = (bf16[2,256,480]{2,1,0:T(8,128)(2,1)S(1)}, bf16[2,256,480]{2,1,0:T(8,128)(2,1)}, u32[]{:S(2)}) copy-start(bf16[2,256,480]{2,1,0:T(8,128)(2,1)} %constant.13.clone.bz_ref) | copy-start | bytes 1474564
  21.0 12.0 %copy-start = (bf16[2,256,512]{2,1,0:T(8,128)(2,1)S(1)}, bf16[2,256,512]{2,1,0:T(8,128)(2,1)}, u32[]{:S(2)}) copy-start(bf16[2,256,512]{2,1,0:T(8,128)(2,1)} %constant.11.clone.wz_ref) | copy-start | bytes 1572868
  35.5 16.0 %all-to-all-start.1 = ((bf16[8,160,128]{2,1,0:T(8,128)(2,1)}), bf16[8,160,128]{2,1,0:T(8,128)(2,1)S(1)}, u32[]{:S(2)}, u32[]{:S(2)}) async-start(bf16[8,160,128]{2,1,0:T(8,128)(2,1)} %get-tuple-element.16), calls=%async_computation.1 | async-start | bytes 655360 | tf_op jit(solution)/shard_map/all_to_all | solution.py:283
  80.0 9.3 %copy-start.4 = (s32[24,128]{1,0:T(8,128)S(1)}, s32[24,128]{1,0:T(8,128)}, u32[]{:S(2)}) copy-start(s32[24,128]{1,0:T(8,128)} %constant.14.clone.lane_ref) | copy-start | bytes 36868

commit v8 on v7

--- a/solution.py
+++ b/solution.py
@@ -14,7 +14,7 @@
 F32 = jnp.float32
 BF16 = jnp.bfloat16
 
-FIRST_Z, FIRST_Y, FIRST_YX, LAST_Z = 10, 2, (6, 2), 4
+FIRST_Z, FIRST_Y, FIRST_YX, LAST_Z = 11, 3, (7, 2), 5
 
 
 def turned(first, count):
@@ -60,15 +60,18 @@
     return lax.dot_general(a, b, (((1,), (1,)), ((), ())), preferred_element_type=F32)
 
 
-def start_kernel(ent_hbm, orb_hbm, pot_hbm, zmsg_hbm, ent_ref, orb_ref, pot_ref, sems):
+def start_kernel(
+    ent_hbm, orb_hbm, pot_hbm, slot_hbm, zmsg_hbm, ent_ref, orb_ref, pot_ref, slot_ref, sems
+):
     first = pl.multiple_of(lax.axis_index("x") * 40, 8)
     pairs = [(orb_hbm, orb_ref), (ent_hbm.at[pl.ds(first, 40), :], ent_ref), (pot_hbm, pot_ref)]
+    pairs.append((slot_hbm, slot_ref))
     pairs += [(orb_ref, zmsg_hbm.at[z]) for z in range(12)]
     copies = [pltpu.make_async_copy(src, dst, sems.at[i]) for i, (src, dst) in enumerate(pairs)]
-    for copy in copies[:3]:
+    for copy in copies[:4]:
         copy.start()
     copies[0].wait()
-    for copy in copies[3:]:
+    for copy in copies[4:]:
         copy.start()
     for copy in copies[1:]:
         copy.wait()
@@ -106,7 +109,7 @@
     first = pl.multiple_of(d * 40, 8)
 
     def rows_of_all(start, count):
-        return jnp.concatenate([all_ref[d, start : start + count, :].astype(F32) for d in range(4)], axis=0)
+        return jnp.concatenate([all_ref[k, start : start + count, :].astype(F32) for k in range(4)], axis=0)
 
     def gathered_v(start):
         halves = [rows_of_all(start, 120), rows_of_all(start + 120, 120)]
@@ -285,14 +288,20 @@
 
 def body(orbitals, potential, slot_sticks, stick_entries):
     wz, wx, bx, bz = tables(potential.shape[1], 64)
-    args = [stick_entries, orbitals.reshape(2, 40, 128), potential]
-    zmsg, ent, own, pot = call(
+    args = [stick_entries, orbitals.reshape(2, 40, 128), potential, slot_sticks.reshape(1, 160)]
+    zmsg, ent, own, pot, slots = call(
         start_kernel,
-        [shape((12, 2, 40, 128), BF16), shape((40, 128), jnp.int32), shape((2, 40, 128), BF16), shape((120, 480), F32)],
+        [
+            shape((12, 2, 40, 128), BF16),
+            shape((40, 128), jnp.int32),
+            shape((2, 40, 128), BF16),
+            shape((120, 480), F32),
+            shape((1, 160), jnp.int32),
+        ],
         *[pltpu.with_memory_space_constraint(a, pltpu.HBM) for a in args],
-        scratch=[pltpu.SemaphoreType.DMA((15,))],
-        in_specs=[pl.BlockSpec(memory_space=pltpu.HBM)] * 3,
-        out_specs=[pl.BlockSpec(memory_space=pltpu.HBM)] + [pl.BlockSpec(memory_space=pltpu.VMEM)] * 3,
+        scratch=[pltpu.SemaphoreType.DMA((16,))],
+        in_specs=[pl.BlockSpec(memory_space=pltpu.HBM)] * 4,
+        out_specs=[pl.BlockSpec(memory_space=pltpu.HBM)] + [pl.BlockSpec(memory_space=pltpu.VMEM)] * 4,
     )
     psi = exchange(zmsg, "z", Z_ORDER)
     packed = call(first_kernel, shape((560, 128), BF16), ent, own, pot, bx)
@@ -300,7 +309,7 @@
     msg, out = call(
         main_kernel,
         [shape((8, 160, 128), BF16), shape((2, 40, 128), BF16)],
-        everyone, own, ent, slot_sticks.reshape(1, 160), slot_sticks.reshape(160, 1), wz, wx, bz,
+        everyone, own, ent, slots, slots.reshape(160, 1), wz, wx, bz,
     )
     arrived = exchange(msg, "y", Y_ORDER)
     rows = call(

time: 91.1 us -> 89.5 us (0.982)
    all_gather x1, blocking collectives: 9.34 us -> 6.51 us  [body(): lax.all_gather(joined, 'c')]
    all_to_all x2, blocking collectives: 27.6 us -> 30.1 us  [exchange(): lax.all_to_all(array, axis, 0, 0, tiled=True, axis_index_groups=[order])]
where the time goes in v8:
time: 89.5 us; the launch traced here: 89 us
  blocking collectives  53.2 us (59%)
  starting transfers between devices  24.1 us (27%)
  Pallas kernels  8.01 us (9%)
  waiting for transfers between devices  2.91 us (3%)
    all_to_all x2, blocking collectives, exchange(): lax.all_to_all(array, axis, 0, 0, tiled=True, axis_index_groups=[order])  30.1 us
    all_to_all x2, starting transfers between devices, exchange(): lax.all_to_all(array, axis, 0, 0, tiled=True, axis_index_groups=[order])  24.1 us
    all_gather x1, blocking collectives, body(): everyone = lax.all_gather(packed, 'x')  12 us
    pallas_call x7, Pallas kernels, call(): pl.pallas_call(kernel, out_shape=outs, scratch_shapes=list(scratch), comp...  8.01 us
    all_gather x1, blocking collectives, body(): lax.all_gather(joined, 'c')  6.51 us
    all_gather x1, blocking collectives, body(): lax.all_gather(psi, 'c')  4.67 us
    all_to_all x2, waiting for transfers between devices, exchange(): lax.all_to_all(array, axis, 0, 0, tiled=True, axis_index_groups=[order])  2.91 us
  transfers between devices with their start and end apart: 2, of which 1 were waited for; matrix products, arithmetic and copies ran while one was open for 0% of the time, Pallas kernels for 5%

profile of v8, /device:TPU:1, one launch (start us, length us, event | category | flops | bytes accessed | tf_op | source)
XLA Modules:
  0.0 89.0 jit_solution(1778561263251205718)
XLA Ops:
  0.6 0.0 copy-start.3
  0.6 1.6 %shard_map.112 = (bf16[12,2,40,128]{3,2,1,0:T(8,128)(2,1)}, s32[40,128]{1,0:T(8,128)S(1)}, bf16[2,40,128]{2,1,0:T(8,128)(2,1)S(1)}, f32[120,480]{1,0:T(8,128)S(1)}, s32[1,160]{1,0:T(1,128)S(1)}) custom-call(s32[160,128]{1,0:T(8,128)} %ent_hbm.1, bf16[2,40,128]{2,1,0:T(8,128)(2,1)} %bitcast.13, f32[120,480]{1,0:T(8,128)} %pot_hbm.1, s32[1,160]{1,0:T(1,128)} %bitcast.14), custom_call_target="tpu_custom_call" | custom-call | tf_op jit(solution)/shard_map/pallas_call | solution.py:272
  2.3 16.6 %all-to-all-start = ((bf16[12,2,40,128]{3,2,1,0:T(8,128)(2,1)}), bf16[12,2,40,128]{3,2,1,0:T(8,128)(2,1)S(1)}, u32[]{:S(2)}, u32[]{:S(2)}) async-start(bf16[12,2,40,128]{3,2,1,0:T(8,128)(2,1)} %get-tuple-element.17), calls=%async_computation | async-start | bytes 491520 | tf_op jit(solution)/shard_map/all_to_all | solution.py:286
  18.9 0.1 copy.15.slot_col_ref
  19.0 0.0 copy-done.3
  19.0 0.0 copy-start.1
  19.0 0.0 copy-start.2
  19.0 1.3 %shard_map.113 = bf16[560,128]{1,0:T(8,128)(2,1)S(1)} custom-call(s32[40,128]{1,0:T(8,128)S(1)} %get-tuple-element.12.ent_ref, bf16[2,40,128]{2,1,0:T(8,128)(2,1)S(1)} %get-tuple-element.13.orb_ref, f32[120,480]{1,0:T(8,128)S(1)} %get-tuple-element.14.pot_ref, bf16[2,480,256]{2,1,0:T(8,128)(2,1)S(1)} %copy-done.3), custom_call_target="tpu_custom_call" | custom-call | tf_op jit(solution)/shard_map/pallas_call | solution.py:272
  20.4 0.0 copy-start
  20.4 12.0 %all-gather = bf16[2240,128]{1,0:T(8,128)(2,1)S(1)} all-gather(bf16[560,128]{1,0:T(8,128)(2,1)S(1)} %shard_map.113), channel_id=2, replica_groups=mesh['y'=8,'z'=12,'c'=2,'x'=4] {'x'}, dimensions={0}, use_global_device_ids=true | all-gather | bytes 716800 | tf_op jit(solution)/shard_map/all_gather | solution.py:308
  32.3 0.0 copy-done.1
  32.3 0.0 copy-done.2
  32.3 0.0 copy-done
  32.3 2.5 %shard_map.114 = (bf16[8,160,128]{2,1,0:T(8,128)(2,1)}, bf16[2,40,128]{2,1,0:T(8,128)(2,1)}) custom-call(bf16[4,560,128]{2,1,0:T(8,128)(2,1)S(1)} %bitcast.9, bf16[2,40,128]{2,1,0:T(8,128)(2,1)S(1)} %get-tuple-element.13.orb_ref, s32[40,128]{1,0:T(8,128)S(1)} %get-tuple-element.12.ent_ref, s32[1,160]{1,0:T(1,128)S(1)} %get-tuple-element.15.slot_row_ref, ...), custom_call_target="tpu_custom_call" | custom-call | tf_op jit(solution)/shard_map/pallas_call | solution.py:272
  34.8 0.0 all-to-all-done
  34.8 7.4 %all-to-all-start.1 = ((bf16[8,160,128]{2,1,0:T(8,128)(2,1)}), bf16[8,160,128]{2,1,0:T(8,128)(2,1)S(1)}, u32[]{:S(2)}, u32[]{:S(2)}) async-start(bf16[8,160,128]{2,1,0:T(8,128)(2,1)} %get-tuple-element.18), calls=%async_computation.1 | async-start | bytes 655360 | tf_op jit(solution)/shard_map/all_to_all | solution.py:286
  42.3 4.7 %all-gather.1 = bf16[24,2,40,128]{3,2,1,0:T(8,128)(2,1)S(1)} all-gather(bf16[12,2,40,128]{3,2,1,0:T(8,128)(2,1)S(1)} %all-to-all-done), channel_id=3, replica_groups=mesh['y'=8,'z'=12,'c'=2,'x'=4] {'c'}, dimensions={0}, use_global_device_ids=true | all-gather | bytes 737280 | tf_op jit(solution)/shard_map/all_gather | solution.py:316
  46.9 0.4 shard_map.115.p_ref
  47.3 2.9 %all-to-all-done.1.own_ref = bf16[8,160,128]{2,1,0:T(8,128)(2,1)S(1)} async-done(((bf16[8,160,128]{2,1,0:T(8,128)(2,1)}), bf16[8,160,128]{2,1,0:T(8,128)(2,1)S(1)}, u32[]{:S(2)}, u32[]{:S(2)}) %all-to-all-start.1) | async-done | bytes 327712 | tf_op jit(solution)/shard_map/all_to_all | solution.py:286
  50.2 0.7 shard_map.116
  51.0 14.3 %all_to_all.20.blocks_ref = f32[32,8,128]{2,1,0:T(8,128)S(1)} all-to-all(f32[32,8,128]{2,1,0:T(8,128)S(1)} %shard_map.116), channel_id=1, replica_groups={{674,675,672,673,2,3,0,1,98,99,96,97,194,195,192,193,290,291,288,289,38..., dimensions={0} | all-to-all | bytes 262144 | tf_op jit(solution)/shard_map/all_to_all | solution.py:286
  65.3 0.1 shard_map.117
  65.4 15.8 %all_to_all.21 = f32[12,40,128]{2,1,0:T(8,128)S(1)} all-to-all(f32[12,40,128]{2,1,0:T(8,128)S(1)} %shard_map.117), channel_id=1, replica_groups={{40,48,56,64,72,80,88,0,8,16,24,32},{41,49,57,65,73,81,89,1,9,17,25,33}..., dimensions={0} | all-to-all | bytes 491520 | tf_op jit(solution)/shard_map/all_to_all | solution.py:286
  81.2 0.0 copy-start.4
  81.2 6.5 %all-gather.2 = f32[24,40,128]{2,1,0:T(8,128)S(1)} all-gather(f32[12,40,128]{2,1,0:T(8,128)S(1)} %all_to_all.21), channel_id=4, replica_groups=mesh['y'=8,'z'=12,'c'=2,'x'=4] {'c'}, dimensions={0}, use_global_device_ids=true | all-gather | bytes 737280 | tf_op jit(solution)/shard_map/all_gather | solution.py:325
  87.7 0.0 copy-done.4
  87.7 1.3 %shard_map.118 = (f32[2,192,192]{2,1,0:T(8,128)}, f32[2,192,192]{2,1,0:T(8,128)}) custom-call(f32[2,12,40,128]{3,2,1,0:T(8,128)S(1)} %bitcast.10, s32[24,128]{1,0:T(8,128)S(1)} %copy-done.4), custom_call_target="tpu_custom_call" | custom-call | tf_op jit(solution)/shard_map/pallas_call | solution.py:272
Async XLA Ops:
  0.6 18.3 %copy-start.3 = (bf16[2,480,256]{2,1,0:T(8,128)(2,1)S(1)}, bf16[2,480,256]{2,1,0:T(8,128)(2,1)}, u32[]{:S(2)}) copy-start(bf16[2,480,256]{2,1,0:T(8,128)(2,1)} %constant.10.clone.bx_ref) | copy-start | bytes 1474564
  2.3 32.6 %all-to-all-start = ((bf16[12,2,40,128]{3,2,1,0:T(8,128)(2,1)}), bf16[12,2,40,128]{3,2,1,0:T(8,128)(2,1)S(1)}, u32[]{:S(2)}, u32[]{:S(2)}) async-start(bf16[12,2,40,128]{3,2,1,0:T(8,128)(2,1)} %get-tuple-element.17), calls=%async_computation | async-start | bytes 491520 | tf_op jit(solution)/shard_map/all_to_all | solution.py:286
  19.0 13.3 %copy-start.1 = (bf16[2,512,256]{2,1,0:T(8,128)(2,1)S(1)}, bf16[2,512,256]{2,1,0:T(8,128)(2,1)}, u32[]{:S(2)}) copy-start(bf16[2,512,256]{2,1,0:T(8,128)(2,1)} %constant.12.clone.wx_ref) | copy-start | bytes 1572868
  19.0 13.3 %copy-start.2 = (bf16[2,256,480]{2,1,0:T(8,128)(2,1)S(1)}, bf16[2,256,480]{2,1,0:T(8,128)(2,1)}, u32[]{:S(2)}) copy-start(bf16[2,256,480]{2,1,0:T(8,128)(2,1)} %constant.13.clone.bz_ref) | copy-start | bytes 1474564
  20.4 12.0 %copy-start = (bf16[2,256,512]{2,1,0:T(8,128)(2,1)S(1)}, bf16[2,256,512]{2,1,0:T(8,128)(2,1)}, u32[]{:S(2)}) copy-start(bf16[2,256,512]{2,1,0:T(8,128)(2,1)} %constant.11.clone.wz_ref) | copy-start | bytes 1572868
  34.8 15.4 %all-to-all-start.1 = ((bf16[8,160,128]{2,1,0:T(8,128)(2,1)}), bf16[8,160,128]{2,1,0:T(8,128)(2,1)S(1)}, u32[]{:S(2)}, u32[]{:S(2)}) async-start(bf16[8,160,128]{2,1,0:T(8,128)(2,1)} %get-tuple-element.18), calls=%async_computation.1 | async-start | bytes 655360 | tf_op jit(solution)/shard_map/all_to_all | solution.py:286
  81.2 6.5 %copy-start.4 = (s32[24,128]{1,0:T(8,128)S(1)}, s32[24,128]{1,0:T(8,128)}, u32[]{:S(2)}) copy-start(s32[24,128]{1,0:T(8,128)} %constant.14.clone.lane_ref) | copy-start | bytes 36868

commit v9 on v8

--- a/solution.py
+++ b/solution.py
@@ -14,14 +14,18 @@
 F32 = jnp.float32
 BF16 = jnp.bfloat16
 
-FIRST_Z, FIRST_Y, FIRST_YX, LAST_Z = 11, 3, (7, 2), 5
+FIRST_Z, FIRST_Y, FIRST_YX, LAST_Z = 11, 3, (3, 2), 5
 
 
 def turned(first, count):
     return [(first + k) % count for k in range(count)]
 
 
-Z_ORDER, Y_ORDER, TAIL_ORDER = turned(FIRST_Z, 12), turned(FIRST_Y, 8), turned(LAST_Z, 12)
+def outward(first, count):
+    return [(first + (k + 1) // 2 * (1 if k % 2 else -1)) % count for k in range(count)]
+
+
+Z_ORDER, Y_ORDER, TAIL_ORDER = turned(FIRST_Z, 12), outward(FIRST_Y, 8), outward(LAST_Z, 12)
 YX_ORDER = [4 * y + x for y in turned(FIRST_YX[0], 8) for x in turned(FIRST_YX[1], 4)]
 
 

time: 89.5 us -> 87.5 us (0.978)
  waiting for transfers between devices: 2.91 us -> 1.55 us
    all_to_all x2, waiting for transfers between devices: 2.91 us -> 1.55 us  [exchange(): lax.all_to_all(array, axis, 0, 0, tiled=True, axis_index_groups=[order])]
where the time goes in v9:
time: 87.5 us; the launch traced here: 87 us
  blocking collectives  52.6 us (60%)
  starting transfers between devices  24.1 us (28%)
  Pallas kernels  8.01 us (9%)
  waiting for transfers between devices  1.55 us (2%)
    all_to_all x2, blocking collectives, exchange(): lax.all_to_all(array, axis, 0, 0, tiled=True, axis_index_groups=[order])  30 us
    all_to_all x2, starting transfers between devices, exchange(): lax.all_to_all(array, axis, 0, 0, tiled=True, axis_index_groups=[order])  24.1 us
    all_gather x1, blocking collectives, body(): everyone = lax.all_gather(packed, 'x')  12 us
    pallas_call x7, Pallas kernels, call(): pl.pallas_call(kernel, out_shape=outs, scratch_shapes=list(scratch), comp...  8.01 us
    all_gather x1, blocking collectives, body(): lax.all_gather(joined, 'c')  5.9 us
    all_gather x1, blocking collectives, body(): lax.all_gather(psi, 'c')  4.67 us
  transfers between devices with their start and end apart: 2, of which 1 were waited for; matrix products, arithmetic and copies ran while one was open for 0% of the time, Pallas kernels for 5%

profile of v9, /device:TPU:1, one launch (start us, length us, event | category | flops | bytes accessed | tf_op | source)
XLA Modules:
  0.0 87.0 jit_solution(17322602694826750922)
XLA Ops:
  0.6 0.0 copy-start.3
  0.6 1.6 %shard_map.112 = (bf16[12,2,40,128]{3,2,1,0:T(8,128)(2,1)}, s32[40,128]{1,0:T(8,128)S(1)}, bf16[2,40,128]{2,1,0:T(8,128)(2,1)S(1)}, f32[120,480]{1,0:T(8,128)S(1)}, s32[1,160]{1,0:T(1,128)S(1)}) custom-call(s32[160,128]{1,0:T(8,128)} %ent_hbm.1, bf16[2,40,128]{2,1,0:T(8,128)(2,1)} %bitcast.13, f32[120,480]{1,0:T(8,128)} %pot_hbm.1, s32[1,160]{1,0:T(1,128)} %bitcast.14), custom_call_target="tpu_custom_call" | custom-call | tf_op jit(solution)/shard_map/pallas_call | solution.py:276
  2.3 16.6 %all-to-all-start = ((bf16[12,2,40,128]{3,2,1,0:T(8,128)(2,1)}), bf16[12,2,40,128]{3,2,1,0:T(8,128)(2,1)S(1)}, u32[]{:S(2)}, u32[]{:S(2)}) async-start(bf16[12,2,40,128]{3,2,1,0:T(8,128)(2,1)} %get-tuple-element.17), calls=%async_computation | async-start | bytes 491520 | tf_op jit(solution)/shard_map/all_to_all | solution.py:290
  18.9 0.1 copy.15.slot_col_ref
  19.0 0.0 copy-done.3
  19.0 0.0 copy-start.1
  19.0 0.0 copy-start.2
  19.0 1.3 %shard_map.113 = bf16[560,128]{1,0:T(8,128)(2,1)S(1)} custom-call(s32[40,128]{1,0:T(8,128)S(1)} %get-tuple-element.12.ent_ref, bf16[2,40,128]{2,1,0:T(8,128)(2,1)S(1)} %get-tuple-element.13.orb_ref, f32[120,480]{1,0:T(8,128)S(1)} %get-tuple-element.14.pot_ref, bf16[2,480,256]{2,1,0:T(8,128)(2,1)S(1)} %copy-done.3), custom_call_target="tpu_custom_call" | custom-call | tf_op jit(solution)/shard_map/pallas_call | solution.py:276
  20.4 0.0 copy-start
  20.4 12.0 %all-gather = bf16[2240,128]{1,0:T(8,128)(2,1)S(1)} all-gather(bf16[560,128]{1,0:T(8,128)(2,1)S(1)} %shard_map.113), channel_id=2, replica_groups=mesh['y'=8,'z'=12,'c'=2,'x'=4] {'x'}, dimensions={0}, use_global_device_ids=true | all-gather | bytes 716800 | tf_op jit(solution)/shard_map/all_gather | solution.py:312
  32.3 0.0 copy-done.1
  32.3 0.0 copy-done.2
  32.3 0.0 copy-done
  32.3 2.5 %shard_map.114 = (bf16[8,160,128]{2,1,0:T(8,128)(2,1)}, bf16[2,40,128]{2,1,0:T(8,128)(2,1)}) custom-call(bf16[4,560,128]{2,1,0:T(8,128)(2,1)S(1)} %bitcast.9, bf16[2,40,128]{2,1,0:T(8,128)(2,1)S(1)} %get-tuple-element.13.orb_ref, s32[40,128]{1,0:T(8,128)S(1)} %get-tuple-element.12.ent_ref, s32[1,160]{1,0:T(1,128)S(1)} %get-tuple-element.15.slot_row_ref, ...), custom_call_target="tpu_custom_call" | custom-call | tf_op jit(solution)/shard_map/pallas_call | solution.py:276
  34.8 0.0 all-to-all-done
  34.8 7.4 %all-to-all-start.1 = ((bf16[8,160,128]{2,1,0:T(8,128)(2,1)}), bf16[8,160,128]{2,1,0:T(8,128)(2,1)S(1)}, u32[]{:S(2)}, u32[]{:S(2)}) async-start(bf16[8,160,128]{2,1,0:T(8,128)(2,1)} %get-tuple-element.18), calls=%async_computation.1 | async-start | bytes 655360 | tf_op jit(solution)/shard_map/all_to_all | solution.py:290
  42.3 4.7 %all-gather.1 = bf16[24,2,40,128]{3,2,1,0:T(8,128)(2,1)S(1)} all-gather(bf16[12,2,40,128]{3,2,1,0:T(8,128)(2,1)S(1)} %all-to-all-done), channel_id=3, replica_groups=mesh['y'=8,'z'=12,'c'=2,'x'=4] {'c'}, dimensions={0}, use_global_device_ids=true | all-gather | bytes 737280 | tf_op jit(solution)/shard_map/all_gather | solution.py:320
  46.9 0.4 shard_map.115.p_ref
  47.3 1.6 %all-to-all-done.1.own_ref = bf16[8,160,128]{2,1,0:T(8,128)(2,1)S(1)} async-done(((bf16[8,160,128]{2,1,0:T(8,128)(2,1)}), bf16[8,160,128]{2,1,0:T(8,128)(2,1)S(1)}, u32[]{:S(2)}, u32[]{:S(2)}) %all-to-all-start.1) | async-done | bytes 327712 | tf_op jit(solution)/shard_map/all_to_all | solution.py:290
  48.9 0.7 shard_map.116
  49.6 14.1 %all_to_all.20.blocks_ref = f32[32,8,128]{2,1,0:T(8,128)S(1)} all-to-all(f32[32,8,128]{2,1,0:T(8,128)S(1)} %shard_map.116), channel_id=1, replica_groups={{290,291,288,289,386,387,384,385,482,483,480,481,578,579,576,577,674,67..., dimensions={0} | all-to-all | bytes 262144 | tf_op jit(solution)/shard_map/all_to_all | solution.py:290
  63.8 0.1 shard_map.117
  63.9 15.9 %all_to_all.21 = f32[12,40,128]{2,1,0:T(8,128)S(1)} all-to-all(f32[12,40,128]{2,1,0:T(8,128)S(1)} %shard_map.117), channel_id=1, replica_groups={{40,48,32,56,24,64,16,72,8,80,0,88},{41,49,33,57,25,65,17,73,9,81,1,89}..., dimensions={0} | all-to-all | bytes 491520 | tf_op jit(solution)/shard_map/all_to_all | solution.py:290
  79.8 0.0 copy-start.4
  79.8 5.9 %all-gather.2 = f32[24,40,128]{2,1,0:T(8,128)S(1)} all-gather(f32[12,40,128]{2,1,0:T(8,128)S(1)} %all_to_all.21), channel_id=4, replica_groups=mesh['y'=8,'z'=12,'c'=2,'x'=4] {'c'}, dimensions={0}, use_global_device_ids=true | all-gather | bytes 737280 | tf_op jit(solution)/shard_map/all_gather | solution.py:329
  85.7 0.0 copy-done.4
  85.7 1.3 %shard_map.118 = (f32[2,192,192]{2,1,0:T(8,128)}, f32[2,192,192]{2,1,0:T(8,128)}) custom-call(f32[2,12,40,128]{3,2,1,0:T(8,128)S(1)} %bitcast.10, s32[24,128]{1,0:T(8,128)S(1)} %copy-done.4), custom_call_target="tpu_custom_call" | custom-call | tf_op jit(solution)/shard_map/pallas_call | solution.py:276
Async XLA Ops:
  0.6 18.3 %copy-start.3 = (bf16[2,480,256]{2,1,0:T(8,128)(2,1)S(1)}, bf16[2,480,256]{2,1,0:T(8,128)(2,1)}, u32[]{:S(2)}) copy-start(bf16[2,480,256]{2,1,0:T(8,128)(2,1)} %constant.10.clone.bx_ref) | copy-start | bytes 1474564
  2.3 32.6 %all-to-all-start = ((bf16[12,2,40,128]{3,2,1,0:T(8,128)(2,1)}), bf16[12,2,40,128]{3,2,1,0:T(8,128)(2,1)S(1)}, u32[]{:S(2)}, u32[]{:S(2)}) async-start(bf16[12,2,40,128]{3,2,1,0:T(8,128)(2,1)} %get-tuple-element.17), calls=%async_computation | async-start | bytes 491520 | tf_op jit(solution)/shard_map/all_to_all | solution.py:290
  19.0 13.3 %copy-start.1 = (bf16[2,512,256]{2,1,0:T(8,128)(2,1)S(1)}, bf16[2,512,256]{2,1,0:T(8,128)(2,1)}, u32[]{:S(2)}) copy-start(bf16[2,512,256]{2,1,0:T(8,128)(2,1)} %constant.12.clone.wx_ref) | copy-start | bytes 1572868
  19.0 13.3 %copy-start.2 = (bf16[2,256,480]{2,1,0:T(8,128)(2,1)S(1)}, bf16[2,256,480]{2,1,0:T(8,128)(2,1)}, u32[]{:S(2)}) copy-start(bf16[2,256,480]{2,1,0:T(8,128)(2,1)} %constant.13.clone.bz_ref) | copy-start | bytes 1474564
  20.4 12.0 %copy-start = (bf16[2,256,512]{2,1,0:T(8,128)(2,1)S(1)}, bf16[2,256,512]{2,1,0:T(8,128)(2,1)}, u32[]{:S(2)}) copy-start(bf16[2,256,512]{2,1,0:T(8,128)(2,1)} %constant.11.clone.wz_ref) | copy-start | bytes 1572868
  34.8 14.1 %all-to-all-start.1 = ((bf16[8,160,128]{2,1,0:T(8,128)(2,1)}), bf16[8,160,128]{2,1,0:T(8,128)(2,1)S(1)}, u32[]{:S(2)}, u32[]{:S(2)}) async-start(bf16[8,160,128]{2,1,0:T(8,128)(2,1)} %get-tuple-element.18), calls=%async_computation.1 | async-start | bytes 655360 | tf_op jit(solution)/shard_map/all_to_all | solution.py:290
  79.8 5.9 %copy-start.4 = (s32[24,128]{1,0:T(8,128)S(1)}, s32[24,128]{1,0:T(8,128)}, u32[]{:S(2)}) copy-start(s32[24,128]{1,0:T(8,128)} %constant.14.clone.lane_ref) | copy-start | bytes 36868

commit v10 on v9

--- a/solution.py
+++ b/solution.py
@@ -108,9 +108,25 @@
     packed_ref[320:560, :] = lo
 
 
-def main_kernel(all_ref, orb_ref, ent_ref, slot_row_ref, slot_col_ref, wz_ref, wx_ref, bz_ref, msg_ref, out_ref):
+def main_kernel(all_ref, orb_ref, ent_ref, slot_row_ref, slot_col_ref, wz_ref, wx_ref, bz_ref, msg_hbm, out_ref, msg_s, *sems):
     d = lax.axis_index("x")
     first = pl.multiple_of(d * 40, 8)
+
+    ent = ent_ref[...]
+    for c in range(2):
+        msg_s[40 * c : 40 * c + 40, :] = jnp.where(ent >= 0, orb_ref[c].astype(F32), 0.0)
+    msg_t = msg_s[...].astype(BF16)
+    half_s = sems[0]
+    half_s[0] = msg_t
+    sends = []
+
+    def send(part):
+        for y in range(8):
+            target = msg_hbm.at[y, pl.ds(80 * part, 80), :]
+            sends.append(pltpu.make_async_copy(half_s.at[part], target, sems[1].at[8 * part + y]))
+            sends[-1].start()
+
+    send(0)
 
     def rows_of_all(start, count):
         return jnp.concatenate([all_ref[k, start : start + count, :].astype(F32) for k in range(4)], axis=0)
@@ -157,19 +173,18 @@
     inside = (square < 64 * 64) & (slot >= 0)
     kinetic = square.astype(F32) * (1.0 / 4096.0)
     own = all_ref[d, 0:80, :].astype(F32)
-    ent = ent_ref[...]
     index = jnp.maximum(ent, 0)
-    masked, applied_rows = [], []
+    applied_rows = []
     for c in range(2):
         value = kinetic * own[40 * c : 40 * c + 40] + applied[40 * c : 40 * c + 40]
         h = jnp.where(inside, value, 0.0).astype(BF16).astype(F32)
         moved = [jnp.take_along_axis(h[8 * g : 8 * g + 8], index[8 * g : 8 * g + 8], axis=1) for g in range(5)]
         applied_rows.append(jnp.where(ent >= 0, jnp.concatenate(moved, axis=0), 0.0))
-        masked.append(jnp.where(ent >= 0, orb_ref[c].astype(F32), 0.0))
         out_ref[c] = applied_rows[c].astype(BF16)
-    message = jnp.concatenate(masked + applied_rows, axis=0).astype(BF16)
-    for y in range(8):
-        msg_ref[y] = message
+    half_s[1] = jnp.concatenate(applied_rows, axis=0).astype(BF16)
+    send(1)
+    for copy in sends:
+        copy.wait()
 
 
 def rows_kernel(psi_ref, p_ref, psi_s):
@@ -314,6 +329,8 @@
         main_kernel,
         [shape((8, 160, 128), BF16), shape((2, 40, 128), BF16)],
         everyone, own, ent, slots, slots.reshape(160, 1), wz, wx, bz,
+        scratch=[pltpu.VMEM((80, 128), F32), pltpu.VMEM((2, 80, 128), BF16), pltpu.SemaphoreType.DMA((16,))],
+        out_specs=[pl.BlockSpec(memory_space=pltpu.HBM), pl.BlockSpec(memory_space=pltpu.VMEM)],
     )
     arrived = exchange(msg, "y", Y_ORDER)
     rows = call(

time: 87.5 us -> 88 us (level)
    all_to_all x2, blocking collectives: 30 us -> 28.8 us  [exchange(): lax.all_to_all(array, axis, 0, 0, tiled=True, axis_index_groups=[order])]
    all_gather x1, blocking collectives: 5.9 us -> 6.94 us  [body(): lax.all_gather(joined, 'c')]
  transfers between devices with their start and end apart: 2 -> 2, of which waited for: 1 -> 1; matrix products, arithmetic and copies ran while one was open for 0% -> 0% of each run, Pallas kernels for 5% -> 6%
where the time goes in v10:
time: 88 us; the launch traced here: 87.5 us
  blocking collectives  52.3 us (59%)
  starting transfers between devices  24.1 us (27%)
  Pallas kernels  8.68 us (10%)
  waiting for transfers between devices  1.55 us (2%)
    all_to_all x2, blocking collectives, exchange(): lax.all_to_all(array, axis, 0, 0, tiled=True, axis_index_groups=[order])  28.8 us
    all_to_all x2, starting transfers between devices, exchange(): lax.all_to_all(array, axis, 0, 0, tiled=True, axis_index_groups=[order])  24.1 us
    all_gather x1, blocking collectives, body(): everyone = lax.all_gather(packed, 'x')  12 us
    pallas_call x7, Pallas kernels, call(): pl.pallas_call(kernel, out_shape=outs, scratch_shapes=list(scratch), comp...  8.68 us
    all_gather x1, blocking collectives, body(): lax.all_gather(joined, 'c')  6.94 us
    all_gather x1, blocking collectives, body(): lax.all_gather(psi, 'c')  4.67 us
  transfers between devices with their start and end apart: 2, of which 1 were waited for; matrix products, arithmetic and copies ran while one was open for 0% of the time, Pallas kernels for 6%

profile of v10, /device:TPU:1, one launch (start us, length us, event | category | flops | bytes accessed | tf_op | source)
XLA Modules:
  0.0 87.5 jit_solution(10543896846179447245)
XLA Ops:
  0.6 0.0 copy-start.3
  0.6 1.6 %shard_map.112 = (bf16[12,2,40,128]{3,2,1,0:T(8,128)(2,1)}, s32[40,128]{1,0:T(8,128)S(1)}, bf16[2,40,128]{2,1,0:T(8,128)(2,1)S(1)}, f32[120,480]{1,0:T(8,128)S(1)}, s32[1,160]{1,0:T(1,128)S(1)}) custom-call(s32[160,128]{1,0:T(8,128)} %ent_hbm.1, bf16[2,40,128]{2,1,0:T(8,128)(2,1)} %bitcast.13, f32[120,480]{1,0:T(8,128)} %pot_hbm.1, s32[1,160]{1,0:T(1,128)} %bitcast.14), custom_call_target="tpu_custom_call" | custom-call | tf_op jit(solution)/shard_map/pallas_call | solution.py:291
  2.3 16.6 %all-to-all-start = ((bf16[12,2,40,128]{3,2,1,0:T(8,128)(2,1)}), bf16[12,2,40,128]{3,2,1,0:T(8,128)(2,1)S(1)}, u32[]{:S(2)}, u32[]{:S(2)}) async-start(bf16[12,2,40,128]{3,2,1,0:T(8,128)(2,1)} %get-tuple-element.17), calls=%async_computation | async-start | bytes 491520 | tf_op jit(solution)/shard_map/all_to_all | solution.py:305
  18.9 0.1 copy.15.slot_col_ref
  19.0 0.0 copy-done.3
  19.0 0.0 copy-start.1
  19.0 0.0 copy-start.2
  19.0 1.3 %shard_map.113 = bf16[560,128]{1,0:T(8,128)(2,1)S(1)} custom-call(s32[40,128]{1,0:T(8,128)S(1)} %get-tuple-element.12.ent_ref, bf16[2,40,128]{2,1,0:T(8,128)(2,1)S(1)} %get-tuple-element.13.orb_ref, f32[120,480]{1,0:T(8,128)S(1)} %get-tuple-element.14.pot_ref, bf16[2,480,256]{2,1,0:T(8,128)(2,1)S(1)} %copy-done.3), custom_call_target="tpu_custom_call" | custom-call | tf_op jit(solution)/shard_map/pallas_call | solution.py:291
  20.4 0.0 copy-start
  20.4 12.0 %all-gather = bf16[2240,128]{1,0:T(8,128)(2,1)S(1)} all-gather(bf16[560,128]{1,0:T(8,128)(2,1)S(1)} %shard_map.113), channel_id=2, replica_groups=mesh['y'=8,'z'=12,'c'=2,'x'=4] {'x'}, dimensions={0}, use_global_device_ids=true | all-gather | bytes 716800 | tf_op jit(solution)/shard_map/all_gather | solution.py:327
  32.3 0.0 copy-done.1
  32.3 0.0 copy-done.2
  32.3 0.0 copy-done
  32.3 3.1 %shard_map.114 = (bf16[8,160,128]{2,1,0:T(8,128)(2,1)}, bf16[2,40,128]{2,1,0:T(8,128)(2,1)}) custom-call(bf16[4,560,128]{2,1,0:T(8,128)(2,1)S(1)} %bitcast.9, bf16[2,40,128]{2,1,0:T(8,128)(2,1)S(1)} %get-tuple-element.13.orb_ref, s32[40,128]{1,0:T(8,128)S(1)} %get-tuple-element.12.ent_ref, s32[1,160]{1,0:T(1,128)S(1)} %get-tuple-element.15.slot_row_ref, ...), custom_call_target="tpu_custom_call" | custom-call | tf_op jit(solution)/shard_map/pallas_call | solution.py:291
  35.5 0.0 all-to-all-done
  35.5 7.5 %all-to-all-start.1 = ((bf16[8,160,128]{2,1,0:T(8,128)(2,1)}), bf16[8,160,128]{2,1,0:T(8,128)(2,1)S(1)}, u32[]{:S(2)}, u32[]{:S(2)}) async-start(bf16[8,160,128]{2,1,0:T(8,128)(2,1)} %get-tuple-element.18), calls=%async_computation.1 | async-start | bytes 655360 | tf_op jit(solution)/shard_map/all_to_all | solution.py:305
  43.0 4.7 %all-gather.1 = bf16[24,2,40,128]{3,2,1,0:T(8,128)(2,1)S(1)} all-gather(bf16[12,2,40,128]{3,2,1,0:T(8,128)(2,1)S(1)} %all-to-all-done), channel_id=3, replica_groups=mesh['y'=8,'z'=12,'c'=2,'x'=4] {'c'}, dimensions={0}, use_global_device_ids=true | all-gather | bytes 737280 | tf_op jit(solution)/shard_map/all_gather | solution.py:337
  47.6 0.4 shard_map.115.p_ref
  48.0 1.5 %all-to-all-done.1.own_ref = bf16[8,160,128]{2,1,0:T(8,128)(2,1)S(1)} async-done(((bf16[8,160,128]{2,1,0:T(8,128)(2,1)}), bf16[8,160,128]{2,1,0:T(8,128)(2,1)S(1)}, u32[]{:S(2)}, u32[]{:S(2)}) %all-to-all-start.1) | async-done | bytes 327712 | tf_op jit(solution)/shard_map/all_to_all | solution.py:305
  49.6 0.7 shard_map.116
  50.3 14.1 %all_to_all.20.blocks_ref = f32[32,8,128]{2,1,0:T(8,128)S(1)} all-to-all(f32[32,8,128]{2,1,0:T(8,128)S(1)} %shard_map.116), channel_id=1, replica_groups={{290,291,288,289,386,387,384,385,482,483,480,481,578,579,576,577,674,67..., dimensions={0} | all-to-all | bytes 262144 | tf_op jit(solution)/shard_map/all_to_all | solution.py:305
  64.4 0.1 shard_map.117
  64.6 14.6 %all_to_all.21 = f32[12,40,128]{2,1,0:T(8,128)S(1)} all-to-all(f32[12,40,128]{2,1,0:T(8,128)S(1)} %shard_map.117), channel_id=1, replica_groups={{40,48,32,56,24,64,16,72,8,80,0,88},{41,49,33,57,25,65,17,73,9,81,1,89}..., dimensions={0} | all-to-all | bytes 491520 | tf_op jit(solution)/shard_map/all_to_all | solution.py:305
  79.2 0.0 copy-start.4
  79.2 6.9 %all-gather.2 = f32[24,40,128]{2,1,0:T(8,128)S(1)} all-gather(f32[12,40,128]{2,1,0:T(8,128)S(1)} %all_to_all.21), channel_id=4, replica_groups=mesh['y'=8,'z'=12,'c'=2,'x'=4] {'c'}, dimensions={0}, use_global_device_ids=true | all-gather | bytes 737280 | tf_op jit(solution)/shard_map/all_gather | solution.py:346
  86.2 0.0 copy-done.4
  86.2 1.3 %shard_map.118 = (f32[2,192,192]{2,1,0:T(8,128)}, f32[2,192,192]{2,1,0:T(8,128)}) custom-call(f32[2,12,40,128]{3,2,1,0:T(8,128)S(1)} %bitcast.10, s32[24,128]{1,0:T(8,128)S(1)} %copy-done.4), custom_call_target="tpu_custom_call" | custom-call | tf_op jit(solution)/shard_map/pallas_call | solution.py:291
Async XLA Ops:
  0.6 18.3 %copy-start.3 = (bf16[2,480,256]{2,1,0:T(8,128)(2,1)S(1)}, bf16[2,480,256]{2,1,0:T(8,128)(2,1)}, u32[]{:S(2)}) copy-start(bf16[2,480,256]{2,1,0:T(8,128)(2,1)} %constant.10.clone.bx_ref) | copy-start | bytes 1474564
  2.3 33.2 %all-to-all-start = ((bf16[12,2,40,128]{3,2,1,0:T(8,128)(2,1)}), bf16[12,2,40,128]{3,2,1,0:T(8,128)(2,1)S(1)}, u32[]{:S(2)}, u32[]{:S(2)}) async-start(bf16[12,2,40,128]{3,2,1,0:T(8,128)(2,1)} %get-tuple-element.17), calls=%async_computation | async-start | bytes 491520 | tf_op jit(solution)/shard_map/all_to_all | solution.py:305
  19.0 13.3 %copy-start.1 = (bf16[2,512,256]{2,1,0:T(8,128)(2,1)S(1)}, bf16[2,512,256]{2,1,0:T(8,128)(2,1)}, u32[]{:S(2)}) copy-start(bf16[2,512,256]{2,1,0:T(8,128)(2,1)} %constant.12.clone.wx_ref) | copy-start | bytes 1572868
  19.0 13.3 %copy-start.2 = (bf16[2,256,480]{2,1,0:T(8,128)(2,1)S(1)}, bf16[2,256,480]{2,1,0:T(8,128)(2,1)}, u32[]{:S(2)}) copy-start(bf16[2,256,480]{2,1,0:T(8,128)(2,1)} %constant.13.clone.bz_ref) | copy-start | bytes 1474564
  20.4 12.0 %copy-start = (bf16[2,256,512]{2,1,0:T(8,128)(2,1)S(1)}, bf16[2,256,512]{2,1,0:T(8,128)(2,1)}, u32[]{:S(2)}) copy-start(bf16[2,256,512]{2,1,0:T(8,128)(2,1)} %constant.11.clone.wz_ref) | copy-start | bytes 1572868
  35.5 14.1 %all-to-all-start.1 = ((bf16[8,160,128]{2,1,0:T(8,128)(2,1)}), bf16[8,160,128]{2,1,0:T(8,128)(2,1)S(1)}, u32[]{:S(2)}, u32[]{:S(2)}) async-start(bf16[8,160,128]{2,1,0:T(8,128)(2,1)} %get-tuple-element.18), calls=%async_computation.1 | async-start | bytes 655360 | tf_op jit(solution)/shard_map/all_to_all | solution.py:305
  79.2 6.9 %copy-start.4 = (s32[24,128]{1,0:T(8,128)S(1)}, s32[24,128]{1,0:T(8,128)}, u32[]{:S(2)}) copy-start(s32[24,128]{1,0:T(8,128)} %constant.14.clone.lane_ref) | copy-start | bytes 36868

commit v11 on v9

--- a/solution.py
+++ b/solution.py
@@ -26,7 +26,7 @@
 
 
 Z_ORDER, Y_ORDER, TAIL_ORDER = turned(FIRST_Z, 12), outward(FIRST_Y, 8), outward(LAST_Z, 12)
-YX_ORDER = [4 * y + x for y in turned(FIRST_YX[0], 8) for x in turned(FIRST_YX[1], 4)]
+YX_ORDER = [4 * y + x for y in outward(FIRST_YX[0], 8) for x in outward(FIRST_YX[1], 4)]
 
 
 def hi_lo(table):

time: 87.5 us -> 87.4 us (level)
  no operation moved by 1% of the time
where the time goes in v11:
time: 87.4 us; the launch traced here: 86.9 us
  blocking collectives  52.5 us (60%)
  starting transfers between devices  24.1 us (28%)
  Pallas kernels  8.01 us (9%)
  waiting for transfers between devices  1.55 us (2%)
    all_to_all x2, blocking collectives, exchange(): lax.all_to_all(array, axis, 0, 0, tiled=True, axis_index_groups=[order])  29.9 us
    all_to_all x2, starting transfers between devices, exchange(): lax.all_to_all(array, axis, 0, 0, tiled=True, axis_index_groups=[order])  24.1 us
    all_gather x1, blocking collectives, body(): everyone = lax.all_gather(packed, 'x')  12 us
    pallas_call x7, Pallas kernels, call(): pl.pallas_call(kernel, out_shape=outs, scratch_shapes=list(scratch), comp...  8.01 us
    all_gather x1, blocking collectives, body(): lax.all_gather(joined, 'c')  5.9 us
    all_gather x1, blocking collectives, body(): lax.all_gather(psi, 'c')  4.67 us
  transfers between devices with their start and end apart: 2, of which 1 were waited for; matrix products, arithmetic and copies ran while one was open for 0% of the time, Pallas kernels for 5%

profile of v11, /device:TPU:1, one launch (start us, length us, event | category | flops | bytes accessed | tf_op | source)
XLA Modules:
  0.0 86.9 jit_solution(13446760463878524963)
XLA Ops:
  0.6 0.0 copy-start.3
  0.6 1.6 %shard_map.112 = (bf16[12,2,40,128]{3,2,1,0:T(8,128)(2,1)}, s32[40,128]{1,0:T(8,128)S(1)}, bf16[2,40,128]{2,1,0:T(8,128)(2,1)S(1)}, f32[120,480]{1,0:T(8,128)S(1)}, s32[1,160]{1,0:T(1,128)S(1)}) custom-call(s32[160,128]{1,0:T(8,128)} %ent_hbm.1, bf16[2,40,128]{2,1,0:T(8,128)(2,1)} %bitcast.13, f32[120,480]{1,0:T(8,128)} %pot_hbm.1, s32[1,160]{1,0:T(1,128)} %bitcast.14), custom_call_target="tpu_custom_call" | custom-call | tf_op jit(solution)/shard_map/pallas_call | solution.py:276
  2.3 16.6 %all-to-all-start = ((bf16[12,2,40,128]{3,2,1,0:T(8,128)(2,1)}), bf16[12,2,40,128]{3,2,1,0:T(8,128)(2,1)S(1)}, u32[]{:S(2)}, u32[]{:S(2)}) async-start(bf16[12,2,40,128]{3,2,1,0:T(8,128)(2,1)} %get-tuple-element.17), calls=%async_computation | async-start | bytes 491520 | tf_op jit(solution)/shard_map/all_to_all | solution.py:290
  18.9 0.1 copy.15.slot_col_ref
  19.0 0.0 copy-done.3
  19.0 0.0 copy-start.1
  19.0 0.0 copy-start.2
  19.0 1.3 %shard_map.113 = bf16[560,128]{1,0:T(8,128)(2,1)S(1)} custom-call(s32[40,128]{1,0:T(8,128)S(1)} %get-tuple-element.12.ent_ref, bf16[2,40,128]{2,1,0:T(8,128)(2,1)S(1)} %get-tuple-element.13.orb_ref, f32[120,480]{1,0:T(8,128)S(1)} %get-tuple-element.14.pot_ref, bf16[2,480,256]{2,1,0:T(8,128)(2,1)S(1)} %copy-done.3), custom_call_target="tpu_custom_call" | custom-call | tf_op jit(solution)/shard_map/pallas_call | solution.py:276
  20.4 0.0 copy-start
  20.4 12.0 %all-gather = bf16[2240,128]{1,0:T(8,128)(2,1)S(1)} all-gather(bf16[560,128]{1,0:T(8,128)(2,1)S(1)} %shard_map.113), channel_id=2, replica_groups=mesh['y'=8,'z'=12,'c'=2,'x'=4] {'x'}, dimensions={0}, use_global_device_ids=true | all-gather | bytes 716800 | tf_op jit(solution)/shard_map/all_gather | solution.py:312
  32.3 0.0 copy-done.1
  32.3 0.0 copy-done.2
  32.3 0.0 copy-done
  32.3 2.5 %shard_map.114 = (bf16[8,160,128]{2,1,0:T(8,128)(2,1)}, bf16[2,40,128]{2,1,0:T(8,128)(2,1)}) custom-call(bf16[4,560,128]{2,1,0:T(8,128)(2,1)S(1)} %bitcast.9, bf16[2,40,128]{2,1,0:T(8,128)(2,1)S(1)} %get-tuple-element.13.orb_ref, s32[40,128]{1,0:T(8,128)S(1)} %get-tuple-element.12.ent_ref, s32[1,160]{1,0:T(1,128)S(1)} %get-tuple-element.15.slot_row_ref, ...), custom_call_target="tpu_custom_call" | custom-call | tf_op jit(solution)/shard_map/pallas_call | solution.py:276
  34.8 0.0 all-to-all-done
  34.8 7.4 %all-to-all-start.1 = ((bf16[8,160,128]{2,1,0:T(8,128)(2,1)}), bf16[8,160,128]{2,1,0:T(8,128)(2,1)S(1)}, u32[]{:S(2)}, u32[]{:S(2)}) async-start(bf16[8,160,128]{2,1,0:T(8,128)(2,1)} %get-tuple-element.18), calls=%async_computation.1 | async-start | bytes 655360 | tf_op jit(solution)/shard_map/all_to_all | solution.py:290
  42.3 4.7 %all-gather.1 = bf16[24,2,40,128]{3,2,1,0:T(8,128)(2,1)S(1)} all-gather(bf16[12,2,40,128]{3,2,1,0:T(8,128)(2,1)S(1)} %all-to-all-done), channel_id=3, replica_groups=mesh['y'=8,'z'=12,'c'=2,'x'=4] {'c'}, dimensions={0}, use_global_device_ids=true | all-gather | bytes 737280 | tf_op jit(solution)/shard_map/all_gather | solution.py:320
  46.9 0.4 shard_map.115.p_ref
  47.3 1.6 %all-to-all-done.1.own_ref = bf16[8,160,128]{2,1,0:T(8,128)(2,1)S(1)} async-done(((bf16[8,160,128]{2,1,0:T(8,128)(2,1)}), bf16[8,160,128]{2,1,0:T(8,128)(2,1)S(1)}, u32[]{:S(2)}, u32[]{:S(2)}) %all-to-all-start.1) | async-done | bytes 327712 | tf_op jit(solution)/shard_map/all_to_all | solution.py:290
  48.9 0.7 shard_map.116
  49.6 14.0 %all_to_all.20.blocks_ref = f32[32,8,128]{2,1,0:T(8,128)S(1)} all-to-all(f32[32,8,128]{2,1,0:T(8,128)S(1)} %shard_map.116), channel_id=1, replica_groups={{290,291,289,288,386,387,385,384,194,195,193,192,482,483,481,480,98,99,..., dimensions={0} | all-to-all | bytes 262144 | tf_op jit(solution)/shard_map/all_to_all | solution.py:290
  63.6 0.1 shard_map.117
  63.8 15.9 %all_to_all.21 = f32[12,40,128]{2,1,0:T(8,128)S(1)} all-to-all(f32[12,40,128]{2,1,0:T(8,128)S(1)} %shard_map.117), channel_id=1, replica_groups={{40,48,32,56,24,64,16,72,8,80,0,88},{41,49,33,57,25,65,17,73,9,81,1,89}..., dimensions={0} | all-to-all | bytes 491520 | tf_op jit(solution)/shard_map/all_to_all | solution.py:290
  79.7 0.0 copy-start.4
  79.7 5.9 %all-gather.2 = f32[24,40,128]{2,1,0:T(8,128)S(1)} all-gather(f32[12,40,128]{2,1,0:T(8,128)S(1)} %all_to_all.21), channel_id=4, replica_groups=mesh['y'=8,'z'=12,'c'=2,'x'=4] {'c'}, dimensions={0}, use_global_device_ids=true | all-gather | bytes 737280 | tf_op jit(solution)/shard_map/all_gather | solution.py:329
  85.6 0.0 copy-done.4
  85.6 1.3 %shard_map.118 = (f32[2,192,192]{2,1,0:T(8,128)}, f32[2,192,192]{2,1,0:T(8,128)}) custom-call(f32[2,12,40,128]{3,2,1,0:T(8,128)S(1)} %bitcast.10, s32[24,128]{1,0:T(8,128)S(1)} %copy-done.4), custom_call_target="tpu_custom_call" | custom-call | tf_op jit(solution)/shard_map/pallas_call | solution.py:276
Async XLA Ops:
  0.6 18.3 %copy-start.3 = (bf16[2,480,256]{2,1,0:T(8,128)(2,1)S(1)}, bf16[2,480,256]{2,1,0:T(8,128)(2,1)}, u32[]{:S(2)}) copy-start(bf16[2,480,256]{2,1,0:T(8,128)(2,1)} %constant.10.clone.bx_ref) | copy-start | bytes 1474564
  2.3 32.6 %all-to-all-start = ((bf16[12,2,40,128]{3,2,1,0:T(8,128)(2,1)}), bf16[12,2,40,128]{3,2,1,0:T(8,128)(2,1)S(1)}, u32[]{:S(2)}, u32[]{:S(2)}) async-start(bf16[12,2,40,128]{3,2,1,0:T(8,128)(2,1)} %get-tuple-element.17), calls=%async_computation | async-start | bytes 491520 | tf_op jit(solution)/shard_map/all_to_all | solution.py:290
  19.0 13.3 %copy-start.1 = (bf16[2,512,256]{2,1,0:T(8,128)(2,1)S(1)}, bf16[2,512,256]{2,1,0:T(8,128)(2,1)}, u32[]{:S(2)}) copy-start(bf16[2,512,256]{2,1,0:T(8,128)(2,1)} %constant.12.clone.wx_ref) | copy-start | bytes 1572868
  19.0 13.3 %copy-start.2 = (bf16[2,256,480]{2,1,0:T(8,128)(2,1)S(1)}, bf16[2,256,480]{2,1,0:T(8,128)(2,1)}, u32[]{:S(2)}) copy-start(bf16[2,256,480]{2,1,0:T(8,128)(2,1)} %constant.13.clone.bz_ref) | copy-start | bytes 1474564
  20.4 12.0 %copy-start = (bf16[2,256,512]{2,1,0:T(8,128)(2,1)S(1)}, bf16[2,256,512]{2,1,0:T(8,128)(2,1)}, u32[]{:S(2)}) copy-start(bf16[2,256,512]{2,1,0:T(8,128)(2,1)} %constant.11.clone.wz_ref) | copy-start | bytes 1572868
  34.8 14.1 %all-to-all-start.1 = ((bf16[8,160,128]{2,1,0:T(8,128)(2,1)}), bf16[8,160,128]{2,1,0:T(8,128)(2,1)S(1)}, u32[]{:S(2)}, u32[]{:S(2)}) async-start(bf16[8,160,128]{2,1,0:T(8,128)(2,1)} %get-tuple-element.18), calls=%async_computation.1 | async-start | bytes 655360 | tf_op jit(solution)/shard_map/all_to_all | solution.py:290
  79.7 5.9 %copy-start.4 = (s32[24,128]{1,0:T(8,128)S(1)}, s32[24,128]{1,0:T(8,128)}, u32[]{:S(2)}) copy-start(s32[24,128]{1,0:T(8,128)} %constant.14.clone.lane_ref) | copy-start | bytes 36868
